TPU v7x, 128 devices: a whole 4x4x4 slice. The times are simulated.
128 devices in a mesh: section: 2 (over z_lo), span: 32 (over x, y, core), seq: 2 (over z_hi).
Axes of the slice: x: 4, y: 4, z: 4 (z_hi: 2, z_lo: 2; z = z_hi * 2 + z_lo), core: 2. Of those that a mesh axis runs over, the one named last changes fastest.
Arguments:
- latents: bfloat16 [32256, 5120], P(('span', 'seq')), may hold values from -6 to 6
- queries: bfloat16 [2, 32256, 5120], P('section', ('span', 'seq')), may hold values from -12 to 12, as said below
- key_states: bfloat16 [2, 32256, 5120], P('section', ('span', 'seq')), may hold values from -12 to 12
- value_states: bfloat16 [2, 32256, 5120], P('section', ('span', 'seq')), may hold values from -6 to 6
- gate_scales: float32 [2, 5120], P('section'), may hold values from 4 to 12
- window: int32 [31], replicated, may hold values from 1 to 10, 170 in all
- intersection: int32 [31], replicated, may hold values from 1 to 10, 170 in all
- blend_index: int32 [31, 10], replicated, may hold values from 0 to 7
Outputs:
- denoised: bfloat16 [32256, 5120], P('span', ('section', 'seq'))
Inputs may be any that keep to these rules, and one draw needn't show every extreme that they name: `queries`: queries of the span lie in the stated range. `window`: 10 is reached in every draw. `intersection`: 10 is reached in every draw.
All inputs are finite; a program needn't handle non-finite values.
Results may differ from a plain program's by a relative error of at most 0.0095.
Values may be sent and summed in bfloat16 or wider, within the bound.
No kernel may reach another device: no remote copies, remote signals or barrier semaphores. Data moves between devices by JAX's collectives and lax.ppermute only.
A program may use at most 192 MiB of HBM per device.

v0:
```python
import functools
import math

import jax
import jax.numpy as jnp
from jax import lax
from jax.experimental import pallas as pl
from jax.experimental.pallas import tpu as pltpu
from jax.sharding import PartitionSpec as P


HEAD_DIM = 128
TOK_FRAME = 48
BF = 10
WEIGHTS = 8
TAIL = BF * TOK_FRAME
QUARTER_HEADS = 10
CHUNKS = (2, 2, 2, 2, 1, 1)
GROUPS = ((0, 1), (2, 3), (4, 5))
VMEM_LIMIT = 66000 * 1024
PAIR_AXES = ("section", "seq")


def spot(section, seq):
    return section * 2 + seq


def to_partner(block, flip_section, flip_seq):
    pairs = [
        (spot(s, q), spot(s ^ flip_section, q ^ flip_seq)) for s in range(2) for q in range(2)
    ]
    return lax.ppermute(block, PAIR_AXES, pairs)


def to_next_span(block):
    length = lax.axis_size("span")
    return lax.ppermute(block, "span", [(i, i + 1) for i in range(length - 1)])


def pack_kernel(width, start, cols_ref, q_ref, k_ref, v_ref, *rest):
    outs, (stage, in_sems, out_sems) = rest[:3], rest[3:]
    copies = []
    for dest in range(3):
        col = pl.multiple_of(cols_ref[dest] + start, HEAD_DIM)
        for which, ref in enumerate((q_ref, k_ref, v_ref)):
            taken = pltpu.make_async_copy(
                ref.at[0, :, pl.ds(col, width)], stage.at[dest, which], in_sems.at[dest, which]
            )
            taken.start()
            copies.append((dest, which, taken))
    sent = []
    for dest, which, taken in copies:
        taken.wait()
        put = pltpu.make_async_copy(
            stage.at[dest, which], outs[dest].at[which], out_sems.at[dest, which]
        )
        put.start()
        sent.append(put)
    for put in sent:
        put.wait()


def pack(cols, queries, key_states, value_states, start, width):
    rows = queries.shape[1]
    shape = jax.ShapeDtypeStruct((3, rows, width), jnp.bfloat16)
    return pl.pallas_call(
        functools.partial(pack_kernel, width, start),
        grid_spec=pltpu.PrefetchScalarGridSpec(
            num_scalar_prefetch=1,
            grid=(),
            in_specs=[pl.BlockSpec(memory_space=pl.ANY)] * 3,
            out_specs=[pl.BlockSpec(memory_space=pl.ANY)] * 3,
            scratch_shapes=[
                pltpu.VMEM((3, 3, rows, width), jnp.bfloat16),
                pltpu.SemaphoreType.DMA((3, 3)),
                pltpu.SemaphoreType.DMA((3, 3)),
            ],
        ),
        out_shape=[shape] * 3,
        cost_estimate=pl.CostEstimate(
            flops=9 * rows * width * 8, bytes_accessed=36 * rows * width, transcendentals=0
        ),
        compiler_params=pltpu.CompilerParams(vmem_limit_bytes=VMEM_LIMIT),
        name="pack",
    )(cols, queries, key_states, value_states)


def near_kernel(
    width, start, info_ref, k_ref, v_ref, seq_ref, sec_ref, dia_ref, out_ref, stage, sems, out_sems
):
    rows = k_ref.shape[1]
    cut = pl.ds(rows - TAIL, TAIL)
    cols = pl.ds(pl.multiple_of(info_ref[1] * HEAD_DIM + start, HEAD_DIM), width)
    late = info_ref[3] == 1

    @pl.when(late)
    def _():
        pltpu.make_async_copy(k_ref.at[0, cut, cols], stage.at[0], sems.at[0]).start()
        pltpu.make_async_copy(v_ref.at[0, cut, cols], stage.at[1], sems.at[1]).start()
        pltpu.make_async_copy(sec_ref.at[1, cut], stage.at[2], sems.at[2]).start()
        pltpu.make_async_copy(sec_ref.at[2, cut], stage.at[3], sems.at[3]).start()

    @pl.when(jnp.logical_not(late))
    def _():
        pltpu.make_async_copy(seq_ref.at[1, cut], stage.at[0], sems.at[0]).start()
        pltpu.make_async_copy(seq_ref.at[2, cut], stage.at[1], sems.at[1]).start()
        pltpu.make_async_copy(dia_ref.at[1, cut], stage.at[2], sems.at[2]).start()
        pltpu.make_async_copy(dia_ref.at[2, cut], stage.at[3], sems.at[3]).start()

    for slot in range(4):
        pltpu.make_async_copy(seq_ref.at[1, cut], stage.at[slot], sems.at[slot]).wait()
        pltpu.make_async_copy(stage.at[slot], out_ref.at[slot], out_sems.at[slot]).start()
    for slot in range(4):
        pltpu.make_async_copy(stage.at[slot], out_ref.at[slot], out_sems.at[slot]).wait()


def near_rows(info, key_states, value_states, seq_in, sec_in, dia_in, start, width):
    return pl.pallas_call(
        functools.partial(near_kernel, width, start),
        grid_spec=pltpu.PrefetchScalarGridSpec(
            num_scalar_prefetch=1,
            grid=(),
            in_specs=[pl.BlockSpec(memory_space=pl.ANY)] * 5,
            out_specs=pl.BlockSpec(memory_space=pl.ANY),
            scratch_shapes=[
                pltpu.VMEM((4, TAIL, width), jnp.bfloat16),
                pltpu.SemaphoreType.DMA((4,)),
                pltpu.SemaphoreType.DMA((4,)),
            ],
        ),
        out_shape=jax.ShapeDtypeStruct((4, TAIL, width), jnp.bfloat16),
        cost_estimate=pl.CostEstimate(
            flops=4 * TAIL * width * 8, bytes_accessed=16 * TAIL * width, transcendentals=0
        ),
        compiler_params=pltpu.CompilerParams(vmem_limit_bytes=VMEM_LIMIT),
        name="near",
    )(info, key_states, value_states, seq_in, sec_in, dia_in)


def attend_kernel(
    info_ref, q_ref, k_ref, v_ref, seq_ref, sec_ref, dia_ref, near_ref, *rest
):
    out_ref, qs, ks, vs = rest[-4:]
    rows = q_ref.shape[1]

    @pl.when(pl.program_id(0) == 0)
    def _():
        lane = lax.broadcasted_iota(jnp.int32, (rows, HEAD_DIM), 1)
        for slot in range(6):
            vs[slot, :, HEAD_DIM:] = (lane == 0).astype(jnp.bfloat16)

    qs[0] = q_ref[0]
    ks[0] = k_ref[0]
    vs[0, :, :HEAD_DIM] = v_ref[0]
    for slot, ref in ((1, seq_ref), (2, sec_ref), (3, dia_ref)):
        qs[slot] = ref[0]
        ks[slot] = ref[1]
        vs[slot, :, :HEAD_DIM] = ref[2]
    vs[4, :TAIL, :HEAD_DIM] = near_ref[1]
    vs[5, :TAIL, :HEAD_DIM] = near_ref[3]
    factor = math.log2(math.e) / math.sqrt(HEAD_DIM)
    place = lax.broadcasted_iota(jnp.int32, (1, TAIL), 1)
    bias = jnp.where(place >= info_ref[0], 0.0, -jnp.inf)

    def one(layer, carry):
        keys = (ks[2 * layer], ks[2 * layer + 1], near_ref[2 * layer])
        values = (vs[2 * layer], vs[2 * layer + 1], vs[4 + layer, :TAIL])
        scores = []
        for half in range(2):
            query = qs[2 * layer + half]
            parts = [
                lax.dot_general(
                    query, key, (((1,), (1,)), ((), ())), preferred_element_type=jnp.float32
                )
                for key in keys
            ]
            scores.append(parts[:2] + [parts[2] + bias])
        lifted = []
        for parts in scores:
            top = factor * functools.reduce(
                jnp.maximum, [jnp.max(part, axis=-1, keepdims=True) for part in parts]
            )
            lifted.append([jnp.exp2(part * factor - top).astype(jnp.bfloat16) for part in parts])
        for half, parts in enumerate(lifted):
            mixed = sum(
                jnp.dot(part, value, preferred_element_type=jnp.float32)
                for part, value in zip(parts, values)
            )
            out_ref[2 * layer + half] = (
                mixed[:, :HEAD_DIM] / mixed[:, HEAD_DIM : HEAD_DIM + 1]
            ).astype(jnp.bfloat16)
        return carry

    lax.fori_loop(0, 2, one, 0)


def attend(
    info, queries, key_states, value_states, seq_in, sec_in, dia_in, near, first, heads, place,
    group_heads, filled,
):
    rows = queries.shape[1]
    keys = 2 * rows + TAIL
    local = pl.BlockSpec((1, rows, HEAD_DIM), lambda h, info: (0, 0, info[1] + first + h))
    partner = pl.BlockSpec((3, rows, HEAD_DIM), lambda h, info: (0, 0, h))
    operands = [info, queries, key_states, value_states, seq_in, sec_in, dia_in, near]
    in_specs = [local, local, local, partner, partner, partner]
    in_specs.append(pl.BlockSpec((4, TAIL, HEAD_DIM), lambda h, info: (0, 0, h)))
    aliases = {}
    if filled is not None:
        aliases = {len(operands): 0}
        operands.append(filled)
        in_specs.append(pl.BlockSpec(memory_space=pl.ANY))
    return pl.pallas_call(
        attend_kernel,
        grid_spec=pltpu.PrefetchScalarGridSpec(
            num_scalar_prefetch=1,
            grid=(heads,),
            in_specs=in_specs,
            out_specs=pl.BlockSpec((4, rows, HEAD_DIM), lambda h, info: (0, 0, place + h)),
            scratch_shapes=[pltpu.VMEM((4, rows, HEAD_DIM), jnp.bfloat16)] * 2
            + [pltpu.VMEM((6, rows, 2 * HEAD_DIM), jnp.bfloat16)],
        ),
        out_shape=jax.ShapeDtypeStruct((4, rows, group_heads * HEAD_DIM), jnp.bfloat16),
        input_output_aliases=aliases,
        cost_estimate=pl.CostEstimate(
            flops=heads * 4 * rows * keys * HEAD_DIM * 4,
            bytes_accessed=heads * HEAD_DIM * rows * 40,
            transcendentals=heads * 4 * rows * keys,
        ),
        compiler_params=pltpu.CompilerParams(vmem_limit_bytes=VMEM_LIMIT),
        name="attend",
    )(*operands)


def gated(info_ref, own_ref, other_ref, near_ref, far_ref, own_gate, other_gate, near):
    latent = jnp.where(near, near_ref[...], far_ref[...]).astype(jnp.float32)
    own = own_gate[...] * own_ref[0].astype(jnp.float32)
    other = other_gate[...] * other_ref[0].astype(jnp.float32)
    leads = info_ref[2] == 0
    after = (latent + jnp.where(leads, own, other)).astype(jnp.bfloat16)
    return after.astype(jnp.float32) + jnp.where(leads, other, own)


def late_kernel(info_ref, picks_ref, *rest):
    (own_ref, other_ref, near_ref, far_ref, own_gate, other_gate), rest = rest[:6], rest[6:]
    out_ref, tail_ref = rest[-2:]
    made = gated(
        info_ref, own_ref, other_ref, near_ref, far_ref, own_gate, other_gate, info_ref[3] == 1
    )
    out_ref[0] = made.astype(jnp.bfloat16)
    tail_ref[...] = made[made.shape[0] - TAIL :].astype(jnp.bfloat16)


def early_kernel(info_ref, picks_ref, *rest):
    (own_ref, other_ref, near_ref, far_ref, own_gate, other_gate, tail_ref), rest = (
        rest[:7], rest[7:]
    )
    out_ref = rest[-1]
    made = gated(
        info_ref, own_ref, other_ref, near_ref, far_ref, own_gate, other_gate, info_ref[3] == 0
    )
    out_ref[0] = made.astype(jnp.bfloat16)
    shared = info_ref[4]
    for frame in range(BF):
        source = jnp.clip(BF - shared + frame, 0, BF - 1)
        weight = (picks_ref[frame].astype(jnp.float32) + 0.5) / WEIGHTS
        begin = pl.multiple_of(source * TOK_FRAME, TOK_FRAME)
        before = tail_ref[pl.ds(begin, TOK_FRAME), :].astype(jnp.float32)
        lead = made[frame * TOK_FRAME : (frame + 1) * TOK_FRAME]
        lead = lead.astype(jnp.bfloat16).astype(jnp.float32)

        @pl.when(frame < shared)
        def _():
            mixed = weight * lead + (1.0 - weight) * before
            out_ref[0, pl.ds(frame * TOK_FRAME, TOK_FRAME), :] = mixed.astype(jnp.bfloat16)


def finish(late, info, picks, att, latents, far, gate, other_gate, first, heads, second, tail):
    rows = att.shape[1]
    width = 2 * HEAD_DIM
    half = 1 if late else 0
    from_own = lambda seq: jnp.where(seq == half, 0, 1)
    here = lambda h, info, picks: (0, info[1] // 2 + first // 2 + h)
    part = lambda h, info, picks: (0, h)
    operands = [info, picks, att, att, latents, far, gate, other_gate]
    in_specs = [
        pl.BlockSpec((1, rows, width), lambda h, info, picks: (from_own(info[3]), 0, h)),
        pl.BlockSpec((1, rows, width), lambda h, info, picks: (2 + from_own(info[3]), 0, h)),
        pl.BlockSpec((rows, width), here),
        pl.BlockSpec((rows, width), part),
        pl.BlockSpec((1, width), here),
        pl.BlockSpec((1, width), lambda h, info, picks: (0, first // 2 + h)),
    ]
    out_specs = [pl.BlockSpec((1, rows, width), lambda h, info, picks: (half, 0, first // 2 + h))]
    out_shape = [jax.ShapeDtypeStruct((2, rows, QUARTER_HEADS * HEAD_DIM), jnp.bfloat16)]
    if late:
        out_specs.append(pl.BlockSpec((TAIL, width), part))
        out_shape.append(jax.ShapeDtypeStruct((TAIL, heads * HEAD_DIM), jnp.bfloat16))
    else:
        operands.append(tail)
        in_specs.append(pl.BlockSpec((TAIL, width), part))
    aliases = {}
    if second is not None:
        aliases = {len(operands): 0}
        operands.append(second)
        in_specs.append(pl.BlockSpec(memory_space=pl.ANY))
    return pl.pallas_call(
        late_kernel if late else early_kernel,
        grid_spec=pltpu.PrefetchScalarGridSpec(
            num_scalar_prefetch=2,
            grid=(heads // 2,),
            in_specs=in_specs,
            out_specs=out_specs,
        ),
        out_shape=out_shape,
        input_output_aliases=aliases,
        cost_estimate=pl.CostEstimate(
            flops=rows * heads * HEAD_DIM * 200,
            bytes_accessed=rows * heads * HEAD_DIM * 12,
            transcendentals=0,
        ),
        compiler_params=pltpu.CompilerParams(vmem_limit_bytes=VMEM_LIMIT),
        name="late" if late else "early",
    )(*operands)


def local(
    latents, queries, key_states, value_states, gate_scales, window, intersection, blend_index
):
    rows = latents.shape[0]
    quarter = QUARTER_HEADS * HEAD_DIM
    span_pos = lax.axis_index("span")
    section = lax.axis_index("section")
    seq = lax.axis_index("seq")
    earlier = jnp.maximum(span_pos - 1, 0)
    follows = span_pos > 0
    closed = jnp.where(follows, TAIL - TOK_FRAME * window[earlier], TAIL)
    shared = jnp.where(follows, intersection[earlier], 0)
    info = jnp.stack(
        [closed, spot(section, seq) * QUARTER_HEADS, section, seq, shared]
    ).astype(jnp.int32)
    picks = blend_index[earlier]
    cols = quarter * jnp.stack(
        [spot(section, 1 - seq), spot(1 - section, seq), spot(1 - section, 1 - seq)]
    ).astype(jnp.int32)

    chunks = len(CHUNKS)
    starts = [sum(CHUNKS[:i]) for i in range(chunks)]
    other_gate = to_partner(
        lax.dynamic_slice_in_dim(gate_scales, cols[1], quarter, 1), 1, 0
    )
    arrived = []
    for first, heads in zip(starts, CHUNKS):
        for_seq, for_sec, for_dia = pack(
            cols, queries, key_states, value_states, first * HEAD_DIM, heads * HEAD_DIM
        )
        from_dia = to_partner(for_dia, 1, 1)
        from_seq = to_partner(for_seq, 0, 1)
        from_sec = to_partner(for_sec, 1, 0)
        arrived.append((from_seq, from_sec, from_dia))
    group_first = [starts[group[0]] for group in GROUPS]
    group_heads = [sum(CHUNKS[k] for k in group) for group in GROUPS]
    far_latents = []
    for first, heads in zip(group_first, group_heads):
        sent = lax.dynamic_slice_in_dim(
            latents, cols[2] + first * HEAD_DIM, heads * HEAD_DIM, 1
        )
        far_latents.append(to_partner(sent, 1, 1))

    attended = []
    for g, group in enumerate(GROUPS):
        filled = None
        for k in group:
            first, heads = starts[k], CHUNKS[k]
            near = near_rows(
                info, key_states, value_states, *arrived[k], first * HEAD_DIM,
                heads * HEAD_DIM,
            )
            near = to_next_span(near)
            filled = attend(
                info, queries, key_states, value_states, *arrived[k], near, first, heads,
                first - group_first[g], group_heads[g], filled,
            )
        attended.append(filled)

    tails = []

    def finished(second, g, late):
        return finish(
            late, info, picks, attended[g], latents, far_latents[g], gate_scales, other_gate,
            group_first[g], group_heads[g], second, None if late else tails[g],
        )

    second = None
    for g in range(len(GROUPS)):
        second, tail = finished(second, g, True)
        tails.append(to_next_span(tail))
    for g in range(len(GROUPS)):
        (second,) = finished(second, g, False)
    return second.reshape(2 * rows, quarter)


def solution(mesh):
    in_specs = (
        P(("span", "seq"), None),
        P("section", ("span", "seq"), None),
        P("section", ("span", "seq"), None),
        P("section", ("span", "seq"), None),
        P("section", None),
        P(),
        P(),
        P(),
    )
    out_specs = P("span", ("section", "seq"))

    return jax.shard_map(local, mesh=mesh, in_specs=in_specs, out_specs=out_specs, check_vma=False)
```

profile of v0, /device:TPU:2, one launch (start us, length us, event | category | flops | bytes accessed | tf_op | source)
XLA Modules:
  0.0 298.7 jit_solution(7103202909969430197)
XLA Ops:
  0.7 2.9 pack.7
  3.5 4.0 %collective-permute-start.4 = (bf16[3,504,128]{2,1,0:T(8,128)(2,1)}, bf16[3,504,128]{2,1,0:T(8,128)(2,1)}, u32[]{:S(2)}, u32[]{:S(2)}) collective-permute-start(bf16[3,504,128]{2,1,0:T(8,128)(2,1)} %get-tuple-element.32), channel_id=1, source_target_pairs={{0,1},{1,0},{64,65},{65,64},{2,3},{3,2},{66,67},{67,66},{4,5},{5,4... | collective-permute-start | bytes 1161224 | tf_op jit(solution)/shard_map/ppermute | solution.py:32
  8.5 3.3 %pack.11 = (bf16[3,504,256]{2,1,0:T(8,128)(2,1)}, bf16[3,504,256]{2,1,0:T(8,128)(2,1)}, bf16[3,504,256]{2,1,0:T(8,128)(2,1)}) custom-call(s32[3]{0:T(128)} %add_multiply_fusion.cols_ref, bf16[1,504,5120]{2,1,0:T(8,128)(2,1)} %q_ref.23, bf16[1,504,5120]{2,1,0:T(8,128)(2,1)} %k_ref.35, bf16[1,504,5120]{2,1,0:T(8,128)(2,1)} %v_ref.35), custom_call_target="tpu_custom_call" | custom-call | flops 9289728 | bytes 4644864 | tf_op jit(solution)/shard_map/pack/pallas_call | solution.py:66
  13.1 2.9 collective-permute-start.6
  16.0 2.8 pack.6
  18.9 2.3 collective-permute-start
  21.2 5.8 %collective-permute-done.5.sec_ref = bf16[3,504,128]{2,1,0:T(8,128)(2,1)} collective-permute-done((bf16[3,504,128]{2,1,0:T(8,128)(2,1)}, bf16[3,504,128]{2,1,0:T(8,128)(2,1)}, u32[]{:S(2)}, u32[]{:S(2)}) %collective-permute-start.5) | collective-permute-done | bytes 387104 | tf_op jit(solution)/shard_map/ppermute | solution.py:32
  26.9 3.3 %pack.10 = (bf16[3,504,256]{2,1,0:T(8,128)(2,1)}, bf16[3,504,256]{2,1,0:T(8,128)(2,1)}, bf16[3,504,256]{2,1,0:T(8,128)(2,1)}) custom-call(s32[3]{0:T(128)} %add_multiply_fusion.cols_ref, bf16[1,504,5120]{2,1,0:T(8,128)(2,1)} %q_ref.23, bf16[1,504,5120]{2,1,0:T(8,128)(2,1)} %k_ref.35, bf16[1,504,5120]{2,1,0:T(8,128)(2,1)} %v_ref.35), custom_call_target="tpu_custom_call" | custom-call | flops 9289728 | bytes 4644864 | tf_op jit(solution)/shard_map/pack/pallas_call | solution.py:66
  30.3 10.8 %collective-permute-done.6.dia_ref = bf16[3,504,128]{2,1,0:T(8,128)(2,1)} collective-permute-done((bf16[3,504,128]{2,1,0:T(8,128)(2,1)}, bf16[3,504,128]{2,1,0:T(8,128)(2,1)}, u32[]{:S(2)}, u32[]{:S(2)}) %collective-permute-start.6) | collective-permute-done | bytes 387104 | tf_op jit(solution)/shard_map/ppermute | solution.py:32
  41.1 3.1 %collective-permute-start.19 = (bf16[3,504,256]{2,1,0:T(8,128)(2,1)}, bf16[3,504,256]{2,1,0:T(8,128)(2,1)}, u32[]{:S(2)}, u32[]{:S(2)}) collective-permute-start(bf16[3,504,256]{2,1,0:T(8,128)(2,1)} %get-tuple-element.41), channel_id=1, source_target_pairs={{0,1},{1,0},{64,65},{65,64},{2,3},{3,2},{66,67},{67,66},{4,5},{5,4... | collective-permute-start | bytes 2322440 | tf_op jit(solution)/shard_map/ppermute | solution.py:32
  44.1 23.4 %collective-permute-done.seq_ref = bf16[3,504,128]{2,1,0:T(8,128)(2,1)} collective-permute-done((bf16[3,504,128]{2,1,0:T(8,128)(2,1)}, bf16[3,504,128]{2,1,0:T(8,128)(2,1)}, u32[]{:S(2)}, u32[]{:S(2)}) %collective-permute-start) | collective-permute-done | bytes 387104 | tf_op jit(solution)/shard_map/ppermute | solution.py:32
  69.0 3.3 %pack.9 = (bf16[3,504,256]{2,1,0:T(8,128)(2,1)}, bf16[3,504,256]{2,1,0:T(8,128)(2,1)}, bf16[3,504,256]{2,1,0:T(8,128)(2,1)}) custom-call(s32[3]{0:T(128)} %add_multiply_fusion.cols_ref, bf16[1,504,5120]{2,1,0:T(8,128)(2,1)} %q_ref.23, bf16[1,504,5120]{2,1,0:T(8,128)(2,1)} %k_ref.35, bf16[1,504,5120]{2,1,0:T(8,128)(2,1)} %v_ref.35), custom_call_target="tpu_custom_call" | custom-call | flops 9289728 | bytes 4644864 | tf_op jit(solution)/shard_map/pack/pallas_call | solution.py:66
  72.3 3.7 %collective-permute-start.14 = (bf16[3,504,256]{2,1,0:T(8,128)(2,1)}, bf16[3,504,256]{2,1,0:T(8,128)(2,1)}, u32[]{:S(2)}, u32[]{:S(2)}) collective-permute-start(bf16[3,504,256]{2,1,0:T(8,128)(2,1)} %get-tuple-element.38), channel_id=1, source_target_pairs={{0,1},{1,0},{64,65},{65,64},{2,3},{3,2},{66,67},{67,66},{4,5},{5,4... | collective-permute-start | bytes 2322440 | tf_op jit(solution)/shard_map/ppermute | solution.py:32
  76.7 7.4 %collective-permute-done.19.seq_ref = bf16[3,504,256]{2,1,0:T(8,128)(2,1)} collective-permute-done((bf16[3,504,256]{2,1,0:T(8,128)(2,1)}, bf16[3,504,256]{2,1,0:T(8,128)(2,1)}, u32[]{:S(2)}, u32[]{:S(2)}) %collective-permute-start.19) | collective-permute-done | bytes 774176 | tf_op jit(solution)/shard_map/ppermute | solution.py:32
  84.1 3.7 %collective-permute-start.21 = (bf16[3,504,256]{2,1,0:T(8,128)(2,1)}, bf16[3,504,256]{2,1,0:T(8,128)(2,1)}, u32[]{:S(2)}, u32[]{:S(2)}) collective-permute-start(bf16[3,504,256]{2,1,0:T(8,128)(2,1)} %get-tuple-element.43), channel_id=1, source_target_pairs={{0,65},{1,64},{64,1},{65,0},{2,67},{3,66},{66,3},{67,2},{4,69},{5,... | collective-permute-start | bytes 2322440 | tf_op jit(solution)/shard_map/ppermute | solution.py:32
  87.8 3.3 %pack.8 = (bf16[3,504,256]{2,1,0:T(8,128)(2,1)}, bf16[3,504,256]{2,1,0:T(8,128)(2,1)}, bf16[3,504,256]{2,1,0:T(8,128)(2,1)}) custom-call(s32[3]{0:T(128)} %add_multiply_fusion.cols_ref, bf16[1,504,5120]{2,1,0:T(8,128)(2,1)} %q_ref.23, bf16[1,504,5120]{2,1,0:T(8,128)(2,1)} %k_ref.35, bf16[1,504,5120]{2,1,0:T(8,128)(2,1)} %v_ref.35), custom_call_target="tpu_custom_call" | custom-call | flops 9289728 | bytes 4644864 | tf_op jit(solution)/shard_map/pack/pallas_call | solution.py:66
  91.1 10.6 %collective-permute-done.20.sec_ref = bf16[3,504,256]{2,1,0:T(8,128)(2,1)} collective-permute-done((bf16[3,504,256]{2,1,0:T(8,128)(2,1)}, bf16[3,504,256]{2,1,0:T(8,128)(2,1)}, u32[]{:S(2)}, u32[]{:S(2)}) %collective-permute-start.20) | collective-permute-done | bytes 774176 | tf_op jit(solution)/shard_map/ppermute | solution.py:32
  102.8 14.5 %collective-permute-done.14.seq_ref = bf16[3,504,256]{2,1,0:T(8,128)(2,1)} collective-permute-done((bf16[3,504,256]{2,1,0:T(8,128)(2,1)}, bf16[3,504,256]{2,1,0:T(8,128)(2,1)}, u32[]{:S(2)}, u32[]{:S(2)}) %collective-permute-start.14) | collective-permute-done | bytes 774176 | tf_op jit(solution)/shard_map/ppermute | solution.py:32
  118.9 16.0 %collective-permute-done.15.sec_ref = bf16[3,504,256]{2,1,0:T(8,128)(2,1)} collective-permute-done((bf16[3,504,256]{2,1,0:T(8,128)(2,1)}, bf16[3,504,256]{2,1,0:T(8,128)(2,1)}, u32[]{:S(2)}, u32[]{:S(2)}) %collective-permute-start.15) | collective-permute-done | bytes 774176 | tf_op jit(solution)/shard_map/ppermute | solution.py:32
  139.3 2.7 near.11
  142.0 1.9 collective-permute-start.26
  144.0 2.7 near.9
  146.7 3.6 %collective-permute-start.17 = (bf16[4,480,256]{2,1,0:T(8,128)(2,1)}, bf16[4,480,256]{2,1,0:T(8,128)(2,1)}, u32[]{:S(2)}, u32[]{:S(2)}) collective-permute-start(bf16[4,480,256]{2,1,0:T(8,128)(2,1)} %near.9), channel_id=1, source_target_pairs={{0,2},{2,4},{4,6},{6,8},{8,10},{10,12},{12,14},{14,16},{16,18},{18... | collective-permute-start | bytes 2949128 | tf_op jit(solution)/shard_map/ppermute | solution.py:37
  156.8 2.7 near.10
  159.6 8.5 %collective-permute-done.11.sec_ref = bf16[3,504,256]{2,1,0:T(8,128)(2,1)} collective-permute-done((bf16[3,504,256]{2,1,0:T(8,128)(2,1)}, bf16[3,504,256]{2,1,0:T(8,128)(2,1)}, u32[]{:S(2)}, u32[]{:S(2)}) %collective-permute-start.11) | collective-permute-done | bytes 774176 | tf_op jit(solution)/shard_map/ppermute | solution.py:32
  168.1 1.9 collective-permute-start.22
  170.1 2.7 constant_dynamic-slice_fusion
  178.6 2.8 near.8
  181.4 3.6 %collective-permute-start.13 = (bf16[4,480,256]{2,1,0:T(8,128)(2,1)}, bf16[4,480,256]{2,1,0:T(8,128)(2,1)}, u32[]{:S(2)}, u32[]{:S(2)}) collective-permute-start(bf16[4,480,256]{2,1,0:T(8,128)(2,1)} %near.8), channel_id=1, source_target_pairs={{0,2},{2,4},{4,6},{6,8},{8,10},{10,12},{12,14},{14,16},{16,18},{18... | collective-permute-start | bytes 2949128 | tf_op jit(solution)/shard_map/ppermute | solution.py:37
  186.8 2.5 near.7
  190.5 2.4 near.6
  192.9 2.6 collective-permute-start.27
  195.6 12.6 %attend.10.rest_0_ = bf16[4,504,512]{2,1,0:T(8,128)(2,1)} custom-call(s32[5]{0:T(128)} %stack.35.info_ref, bf16[1,504,5120]{2,1,0:T(8,128)(2,1)} %q_ref.23, bf16[1,504,5120]{2,1,0:T(8,128)(2,1)} %k_ref.35, bf16[1,504,5120]{2,1,0:T(8,128)(2,1)} %v_ref.35, bf16[3,504,256]{2,1,0:T(8,128)(2,1)} %collective-permute-done.23.seq_ref, ...), custom_call_target="tpu_custom_call" | custom-call | flops 3071803392 | bytes 5160960 | tf_op jit(solution)/shard_map/attend/pallas_call | solution.py:213
  209.1 12.5 %attend.8.rest_0_ = bf16[4,504,512]{2,1,0:T(8,128)(2,1)} custom-call(s32[5]{0:T(128)} %stack.35.info_ref, bf16[1,504,5120]{2,1,0:T(8,128)(2,1)} %q_ref.23, bf16[1,504,5120]{2,1,0:T(8,128)(2,1)} %k_ref.35, bf16[1,504,5120]{2,1,0:T(8,128)(2,1)} %v_ref.35, bf16[3,504,256]{2,1,0:T(8,128)(2,1)} %collective-permute-done.14.seq_ref, ...), custom_call_target="tpu_custom_call" | custom-call | flops 3071803392 | bytes 5160960 | tf_op jit(solution)/shard_map/attend/pallas_call | solution.py:213
  221.6 1.9 collective-permute-start.7
  223.6 3.6 %collective-permute-start.3 = (bf16[4,480,128]{2,1,0:T(8,128)(2,1)}, bf16[4,480,128]{2,1,0:T(8,128)(2,1)}, u32[]{:S(2)}, u32[]{:S(2)}) collective-permute-start(bf16[4,480,128]{2,1,0:T(8,128)(2,1)} %near.6), channel_id=1, source_target_pairs={{0,2},{2,4},{4,6},{6,8},{8,10},{10,12},{12,14},{14,16},{16,18},{18... | collective-permute-start | bytes 1474568 | tf_op jit(solution)/shard_map/ppermute | solution.py:37
  227.1 12.6 %attend.11.rest_0_.rest_1_ = bf16[4,504,512]{2,1,0:T(8,128)(2,1)} custom-call(s32[5]{0:T(128)} %stack.35.info_ref, bf16[1,504,5120]{2,1,0:T(8,128)(2,1)} %q_ref.23, bf16[1,504,5120]{2,1,0:T(8,128)(2,1)} %k_ref.35, bf16[1,504,5120]{2,1,0:T(8,128)(2,1)} %v_ref.35, ...), custom_call_target="tpu_custom_call", output_to_operand_aliasing={{}: (8, {})} | custom-call | flops 3071803392 | bytes 5160960 | tf_op jit(solution)/shard_map/attend/pallas_call | solution.py:213
  239.7 2.6 collective-permute-start.8
  242.3 3.4 %late.3 = (bf16[2,504,1280]{2,1,0:T(8,128)(2,1)}, bf16[480,512]{1,0:T(8,128)(2,1)}) custom-call(s32[5]{0:T(128)} %stack.35.info_ref, s32[10]{0:T(128)} %dynamic-slice_reduce_fusion.picks_ref, bf16[4,504,512]{2,1,0:T(8,128)(2,1)} %attend.11.rest_0_.rest_1_, bf16[4,504,512]{2,1,0:T(8,128)(2,1)} %attend.11.rest_0_.rest_1_, bf16[504,5120]{1,0:T(8,128)(2,1)} %rest_2_.11, ...), custom_call_target="tpu_custom_call" | custom-call | flops 51609600 | bytes 3096576 | tf_op jit(solution)/shard_map/late/pallas_call | solution.py:307
  245.7 12.6 %attend.9.rest_0_.rest_1_ = bf16[4,504,512]{2,1,0:T(8,128)(2,1)} custom-call(s32[5]{0:T(128)} %stack.35.info_ref, bf16[1,504,5120]{2,1,0:T(8,128)(2,1)} %q_ref.23, bf16[1,504,5120]{2,1,0:T(8,128)(2,1)} %k_ref.35, bf16[1,504,5120]{2,1,0:T(8,128)(2,1)} %v_ref.35, bf16[3,504,256]{2,1,0:T(8,128)(2,1)} %collective-permute-done.10.seq_ref, ...), custom_call_target="tpu_custom_call", output_to_operand_aliasing={{}: (8, {})} | custom-call | flops 3071803392 | bytes 5160960 | tf_op jit(solution)/shard_map/attend/pallas_call | solution.py:213
  258.3 3.4 %late.4 = (bf16[2,504,1280]{2,1,0:T(8,128)(2,1)}, bf16[480,512]{1,0:T(8,128)(2,1)}) custom-call(s32[5]{0:T(128)} %stack.35.info_ref, s32[10]{0:T(128)} %dynamic-slice_reduce_fusion.picks_ref, bf16[4,504,512]{2,1,0:T(8,128)(2,1)} %attend.9.rest_0_.rest_1_, bf16[4,504,512]{2,1,0:T(8,128)(2,1)} %attend.9.rest_0_.rest_1_, ...), custom_call_target="tpu_custom_call", output_to_operand_aliasing={{0}: (8, {})} | custom-call | flops 51609600 | bytes 3096576 | tf_op jit(solution)/shard_map/late/pallas_call | solution.py:307
  263.6 3.5 %collective-permute-start.30 = (bf16[480,512]{1,0:T(8,128)(2,1)}, bf16[480,512]{1,0:T(8,128)(2,1)}, u32[]{:S(2)}, u32[]{:S(2)}) collective-permute-start(bf16[480,512]{1,0:T(8,128)(2,1)} %get-tuple-element.51), channel_id=1, source_target_pairs={{0,2},{2,4},{4,6},{6,8},{8,10},{10,12},{12,14},{14,16},{16,18},{18... | collective-permute-start | bytes 1474568 | tf_op jit(solution)/shard_map/ppermute | solution.py:37
  267.1 7.8 %attend.6.rest_0_ = bf16[4,504,256]{2,1,0:T(8,128)(2,1)} custom-call(s32[5]{0:T(128)} %stack.35.info_ref, bf16[1,504,5120]{2,1,0:T(8,128)(2,1)} %q_ref.23, bf16[1,504,5120]{2,1,0:T(8,128)(2,1)} %k_ref.35, bf16[1,504,5120]{2,1,0:T(8,128)(2,1)} %v_ref.35, bf16[3,504,128]{2,1,0:T(8,128)(2,1)} %collective-permute-done.4.seq_ref, ...), custom_call_target="tpu_custom_call" | custom-call | flops 1535901696 | bytes 2580480 | tf_op jit(solution)/shard_map/attend/pallas_call | solution.py:213
  274.9 7.8 %attend.7.rest_0_.rest_1_ = bf16[4,504,256]{2,1,0:T(8,128)(2,1)} custom-call(s32[5]{0:T(128)} %stack.35.info_ref, bf16[1,504,5120]{2,1,0:T(8,128)(2,1)} %q_ref.23, bf16[1,504,5120]{2,1,0:T(8,128)(2,1)} %k_ref.35, bf16[1,504,5120]{2,1,0:T(8,128)(2,1)} %v_ref.35, bf16[3,504,128]{2,1,0:T(8,128)(2,1)} %collective-permute-done.seq_ref, ...), custom_call_target="tpu_custom_call", output_to_operand_aliasing={{}: (8, {})} | custom-call | flops 1535901696 | bytes 2580480 | tf_op jit(solution)/shard_map/attend/pallas_call | solution.py:213
  282.7 3.0 %late.5 = (bf16[2,504,1280]{2,1,0:T(8,128)(2,1)}, bf16[480,256]{1,0:T(8,128)(2,1)}) custom-call(s32[5]{0:T(128)} %stack.35.info_ref, s32[10]{0:T(128)} %dynamic-slice_reduce_fusion.picks_ref, bf16[4,504,256]{2,1,0:T(8,128)(2,1)} %attend.7.rest_0_.rest_1_, bf16[4,504,256]{2,1,0:T(8,128)(2,1)} %attend.7.rest_0_.rest_1_, ...), custom_call_target="tpu_custom_call", output_to_operand_aliasing={{0}: (8, {})} | custom-call | flops 25804800 | bytes 1548288 | tf_op jit(solution)/shard_map/late/pallas_call | solution.py:307
  287.6 3.6 %early.3.rest_7_ = bf16[2,504,1280]{2,1,0:T(8,128)(2,1)} custom-call(s32[5]{0:T(128)} %stack.35.info_ref, s32[10]{0:T(128)} %dynamic-slice_reduce_fusion.picks_ref, bf16[4,504,512]{2,1,0:T(8,128)(2,1)} %attend.11.rest_0_.rest_1_, bf16[4,504,512]{2,1,0:T(8,128)(2,1)} %attend.11.rest_0_.rest_1_, ...), custom_call_target="tpu_custom_call", output_to_operand_aliasing={{}: (9, {})} | custom-call | flops 51609600 | bytes 3096576 | tf_op jit(solution)/shard_map/early/pallas_call | solution.py:307
  291.2 3.6 %early.4.rest_7_ = bf16[2,504,1280]{2,1,0:T(8,128)(2,1)} custom-call(s32[5]{0:T(128)} %stack.35.info_ref, s32[10]{0:T(128)} %dynamic-slice_reduce_fusion.picks_ref, bf16[4,504,512]{2,1,0:T(8,128)(2,1)} %attend.9.rest_0_.rest_1_, bf16[4,504,512]{2,1,0:T(8,128)(2,1)} %attend.9.rest_0_.rest_1_, ...), custom_call_target="tpu_custom_call", output_to_operand_aliasing={{}: (9, {})} | custom-call | flops 51609600 | bytes 3096576 | tf_op jit(solution)/shard_map/early/pallas_call | solution.py:307
  295.6 3.1 %early.5 = bf16[2,504,1280]{2,1,0:T(8,128)(2,1)} custom-call(s32[5]{0:T(128)} %stack.35.info_ref, s32[10]{0:T(128)} %dynamic-slice_reduce_fusion.picks_ref, bf16[4,504,256]{2,1,0:T(8,128)(2,1)} %attend.7.rest_0_.rest_1_, bf16[4,504,256]{2,1,0:T(8,128)(2,1)} %attend.7.rest_0_.rest_1_, bf16[504,5120]{1,0:T(8,128)(2,1)} %rest_2_.11, ...), custom_call_target="tpu_custom_call", output_to_operand_aliasing={{}: (9, {})} | custom-call | flops 25804800 | bytes 1548288 | tf_op jit(solution)/shard_map/early/pallas_call | solution.py:307
  (47 shorter events, 25.5 us)
Async XLA Ops:
  3.5 15.3 %collective-permute-start.4 = (bf16[3,504,128]{2,1,0:T(8,128)(2,1)}, bf16[3,504,128]{2,1,0:T(8,128)(2,1)}, u32[]{:S(2)}, u32[]{:S(2)}) collective-permute-start(bf16[3,504,128]{2,1,0:T(8,128)(2,1)} %get-tuple-element.32), channel_id=1, source_target_pairs={{0,1},{1,0},{64,65},{65,64},{2,3},{3,2},{66,67},{67,66},{4,5},{5,4... | collective-permute-start | bytes 1161224 | tf_op jit(solution)/shard_map/ppermute | solution.py:32
  7.5 19.5 %collective-permute-start.5 = (bf16[3,504,128]{2,1,0:T(8,128)(2,1)}, bf16[3,504,128]{2,1,0:T(8,128)(2,1)}, u32[]{:S(2)}, u32[]{:S(2)}) collective-permute-start(bf16[3,504,128]{2,1,0:T(8,128)(2,1)} %get-tuple-element.33), channel_id=1, source_target_pairs={{0,64},{1,65},{64,0},{65,1},{2,66},{3,67},{66,2},{67,3},{4,68},{5,... | collective-permute-start | bytes 1161224 | tf_op jit(solution)/shard_map/ppermute | solution.py:32
  11.8 60.5 %collective-permute-start.23 = (bf16[3,504,256]{2,1,0:T(8,128)(2,1)}, bf16[3,504,256]{2,1,0:T(8,128)(2,1)}, u32[]{:S(2)}, u32[]{:S(2)}) collective-permute-start(bf16[3,504,256]{2,1,0:T(8,128)(2,1)} %get-tuple-element.44), channel_id=1, source_target_pairs={{0,1},{1,0},{64,65},{65,64},{2,3},{3,2},{66,67},{67,66},{4,5},{5,4... | collective-permute-start | bytes 2322440 | tf_op jit(solution)/shard_map/ppermute | solution.py:32
  13.1 62.9 %collective-permute-start.24 = (bf16[3,504,256]{2,1,0:T(8,128)(2,1)}, bf16[3,504,256]{2,1,0:T(8,128)(2,1)}, u32[]{:S(2)}, u32[]{:S(2)}) collective-permute-start(bf16[3,504,256]{2,1,0:T(8,128)(2,1)} %get-tuple-element.45), channel_id=1, source_target_pairs={{0,64},{1,65},{64,0},{65,1},{2,66},{3,67},{66,2},{67,3},{4,68},{5,... | collective-permute-start | bytes 2322440 | tf_op jit(solution)/shard_map/ppermute | solution.py:32
  13.1 28.0 %collective-permute-start.6 = (bf16[3,504,128]{2,1,0:T(8,128)(2,1)}, bf16[3,504,128]{2,1,0:T(8,128)(2,1)}, u32[]{:S(2)}, u32[]{:S(2)}) collective-permute-start(bf16[3,504,128]{2,1,0:T(8,128)(2,1)} %get-tuple-element.34), channel_id=1, source_target_pairs={{0,65},{1,64},{64,1},{65,0},{2,67},{3,66},{66,3},{67,2},{4,69},{5,... | collective-permute-start | bytes 1161224 | tf_op jit(solution)/shard_map/ppermute | solution.py:32
  18.9 48.7 %collective-permute-start = (bf16[3,504,128]{2,1,0:T(8,128)(2,1)}, bf16[3,504,128]{2,1,0:T(8,128)(2,1)}, u32[]{:S(2)}, u32[]{:S(2)}) collective-permute-start(bf16[3,504,128]{2,1,0:T(8,128)(2,1)} %get-tuple-element.29), channel_id=1, source_target_pairs={{0,1},{1,0},{64,65},{65,64},{2,3},{3,2},{66,67},{67,66},{4,5},{5,4... | collective-permute-start | bytes 1161224 | tf_op jit(solution)/shard_map/ppermute | solution.py:32
  26.9 49.1 %collective-permute-start.25 = (bf16[3,504,256]{2,1,0:T(8,128)(2,1)}, bf16[3,504,256]{2,1,0:T(8,128)(2,1)}, u32[]{:S(2)}, u32[]{:S(2)}) collective-permute-start(bf16[3,504,256]{2,1,0:T(8,128)(2,1)} %get-tuple-element.46), channel_id=1, source_target_pairs={{0,65},{1,64},{64,1},{65,0},{2,67},{3,66},{66,3},{67,2},{4,69},{5,... | collective-permute-start | bytes 2322440 | tf_op jit(solution)/shard_map/ppermute | solution.py:32
  41.1 43.0 %collective-permute-start.19 = (bf16[3,504,256]{2,1,0:T(8,128)(2,1)}, bf16[3,504,256]{2,1,0:T(8,128)(2,1)}, u32[]{:S(2)}, u32[]{:S(2)}) collective-permute-start(bf16[3,504,256]{2,1,0:T(8,128)(2,1)} %get-tuple-element.41), channel_id=1, source_target_pairs={{0,1},{1,0},{64,65},{65,64},{2,3},{3,2},{66,67},{67,66},{4,5},{5,4... | collective-permute-start | bytes 2322440 | tf_op jit(solution)/shard_map/ppermute | solution.py:32
  67.5 34.1 %collective-permute-start.20 = (bf16[3,504,256]{2,1,0:T(8,128)(2,1)}, bf16[3,504,256]{2,1,0:T(8,128)(2,1)}, u32[]{:S(2)}, u32[]{:S(2)}) collective-permute-start(bf16[3,504,256]{2,1,0:T(8,128)(2,1)} %get-tuple-element.42), channel_id=1, source_target_pairs={{0,64},{1,65},{64,0},{65,1},{2,66},{3,67},{66,2},{67,3},{4,68},{5,... | collective-permute-start | bytes 2322440 | tf_op jit(solution)/shard_map/ppermute | solution.py:32
  72.3 45.0 %collective-permute-start.14 = (bf16[3,504,256]{2,1,0:T(8,128)(2,1)}, bf16[3,504,256]{2,1,0:T(8,128)(2,1)}, u32[]{:S(2)}, u32[]{:S(2)}) collective-permute-start(bf16[3,504,256]{2,1,0:T(8,128)(2,1)} %get-tuple-element.38), channel_id=1, source_target_pairs={{0,1},{1,0},{64,65},{65,64},{2,3},{3,2},{66,67},{67,66},{4,5},{5,4... | collective-permute-start | bytes 2322440 | tf_op jit(solution)/shard_map/ppermute | solution.py:32
  76.0 58.9 %collective-permute-start.15 = (bf16[3,504,256]{2,1,0:T(8,128)(2,1)}, bf16[3,504,256]{2,1,0:T(8,128)(2,1)}, u32[]{:S(2)}, u32[]{:S(2)}) collective-permute-start(bf16[3,504,256]{2,1,0:T(8,128)(2,1)} %get-tuple-element.39), channel_id=1, source_target_pairs={{0,64},{1,65},{64,0},{65,1},{2,66},{3,67},{66,2},{67,3},{4,68},{5,... | collective-permute-start | bytes 2322440 | tf_op jit(solution)/shard_map/ppermute | solution.py:32
  76.0 66.0 %collective-permute-start.16 = (bf16[3,504,256]{2,1,0:T(8,128)(2,1)}, bf16[3,504,256]{2,1,0:T(8,128)(2,1)}, u32[]{:S(2)}, u32[]{:S(2)}) collective-permute-start(bf16[3,504,256]{2,1,0:T(8,128)(2,1)} %get-tuple-element.40), channel_id=1, source_target_pairs={{0,65},{1,64},{64,1},{65,0},{2,67},{3,66},{66,3},{67,2},{4,69},{5,... | collective-permute-start | bytes 2322440 | tf_op jit(solution)/shard_map/ppermute | solution.py:32
  84.1 62.6 %collective-permute-start.21 = (bf16[3,504,256]{2,1,0:T(8,128)(2,1)}, bf16[3,504,256]{2,1,0:T(8,128)(2,1)}, u32[]{:S(2)}, u32[]{:S(2)}) collective-permute-start(bf16[3,504,256]{2,1,0:T(8,128)(2,1)} %get-tuple-element.43), channel_id=1, source_target_pairs={{0,65},{1,64},{64,1},{65,0},{2,67},{3,66},{66,3},{67,2},{4,69},{5,... | collective-permute-start | bytes 2322440 | tf_op jit(solution)/shard_map/ppermute | solution.py:32
  101.7 48.9 %collective-permute-start.10 = (bf16[3,504,256]{2,1,0:T(8,128)(2,1)}, bf16[3,504,256]{2,1,0:T(8,128)(2,1)}, u32[]{:S(2)}, u32[]{:S(2)}) collective-permute-start(bf16[3,504,256]{2,1,0:T(8,128)(2,1)} %get-tuple-element.35), channel_id=1, source_target_pairs={{0,1},{1,0},{64,65},{65,64},{2,3},{3,2},{66,67},{67,66},{4,5},{5,4... | collective-permute-start | bytes 2322440 | tf_op jit(solution)/shard_map/ppermute | solution.py:32
  117.3 50.8 %collective-permute-start.11 = (bf16[3,504,256]{2,1,0:T(8,128)(2,1)}, bf16[3,504,256]{2,1,0:T(8,128)(2,1)}, u32[]{:S(2)}, u32[]{:S(2)}) collective-permute-start(bf16[3,504,256]{2,1,0:T(8,128)(2,1)} %get-tuple-element.36), channel_id=1, source_target_pairs={{0,64},{1,65},{64,0},{65,1},{2,66},{3,67},{66,2},{67,3},{4,68},{5,... | collective-permute-start | bytes 2322440 | tf_op jit(solution)/shard_map/ppermute | solution.py:32
  134.9 33.2 %collective-permute-start.12 = (bf16[3,504,256]{2,1,0:T(8,128)(2,1)}, bf16[3,504,256]{2,1,0:T(8,128)(2,1)}, u32[]{:S(2)}, u32[]{:S(2)}) collective-permute-start(bf16[3,504,256]{2,1,0:T(8,128)(2,1)} %get-tuple-element.37), channel_id=1, source_target_pairs={{0,65},{1,64},{64,1},{65,0},{2,67},{3,66},{66,3},{67,2},{4,69},{5,... | collective-permute-start | bytes 2322440 | tf_op jit(solution)/shard_map/ppermute | solution.py:32
  142.0 50.9 %collective-permute-start.26 = (bf16[4,480,256]{2,1,0:T(8,128)(2,1)}, bf16[4,480,256]{2,1,0:T(8,128)(2,1)}, u32[]{:S(2)}, u32[]{:S(2)}) collective-permute-start(bf16[4,480,256]{2,1,0:T(8,128)(2,1)} %near.11), channel_id=1, source_target_pairs={{0,2},{2,4},{4,6},{6,8},{8,10},{10,12},{12,14},{14,16},{16,18},{18... | collective-permute-start | bytes 2949128 | tf_op jit(solution)/shard_map/ppermute | solution.py:37
  146.7 61.4 %collective-permute-start.17 = (bf16[4,480,256]{2,1,0:T(8,128)(2,1)}, bf16[4,480,256]{2,1,0:T(8,128)(2,1)}, u32[]{:S(2)}, u32[]{:S(2)}) collective-permute-start(bf16[4,480,256]{2,1,0:T(8,128)(2,1)} %near.9), channel_id=1, source_target_pairs={{0,2},{2,4},{4,6},{6,8},{8,10},{10,12},{12,14},{14,16},{16,18},{18... | collective-permute-start | bytes 2949128 | tf_op jit(solution)/shard_map/ppermute | solution.py:37
  150.5 30.8 %collective-permute-start.1 = (bf16[3,504,128]{2,1,0:T(8,128)(2,1)}, bf16[3,504,128]{2,1,0:T(8,128)(2,1)}, u32[]{:S(2)}, u32[]{:S(2)}) collective-permute-start(bf16[3,504,128]{2,1,0:T(8,128)(2,1)} %get-tuple-element.30), channel_id=1, source_target_pairs={{0,64},{1,65},{64,0},{65,1},{2,66},{3,67},{66,2},{67,3},{4,68},{5,... | collective-permute-start | bytes 1161224 | tf_op jit(solution)/shard_map/ppermute | solution.py:32
  168.1 21.1 %collective-permute-start.2 = (bf16[3,504,128]{2,1,0:T(8,128)(2,1)}, bf16[3,504,128]{2,1,0:T(8,128)(2,1)}, u32[]{:S(2)}, u32[]{:S(2)}) collective-permute-start(bf16[3,504,128]{2,1,0:T(8,128)(2,1)} %get-tuple-element.31), channel_id=1, source_target_pairs={{0,65},{1,64},{64,1},{65,0},{2,67},{3,66},{66,3},{67,2},{4,69},{5,... | collective-permute-start | bytes 1161224 | tf_op jit(solution)/shard_map/ppermute | solution.py:32
  168.1 55.4 %collective-permute-start.22 = (bf16[4,480,256]{2,1,0:T(8,128)(2,1)}, bf16[4,480,256]{2,1,0:T(8,128)(2,1)}, u32[]{:S(2)}, u32[]{:S(2)}) collective-permute-start(bf16[4,480,256]{2,1,0:T(8,128)(2,1)} %near.10), channel_id=1, source_target_pairs={{0,2},{2,4},{4,6},{6,8},{8,10},{10,12},{12,14},{14,16},{16,18},{18... | collective-permute-start | bytes 2949128 | tf_op jit(solution)/shard_map/ppermute | solution.py:37
  181.4 64.4 %collective-permute-start.13 = (bf16[4,480,256]{2,1,0:T(8,128)(2,1)}, bf16[4,480,256]{2,1,0:T(8,128)(2,1)}, u32[]{:S(2)}, u32[]{:S(2)}) collective-permute-start(bf16[4,480,256]{2,1,0:T(8,128)(2,1)} %near.8), channel_id=1, source_target_pairs={{0,2},{2,4},{4,6},{6,8},{8,10},{10,12},{12,14},{14,16},{16,18},{18... | collective-permute-start | bytes 2949128 | tf_op jit(solution)/shard_map/ppermute | solution.py:37
  189.2 32.4 %collective-permute-start.9 = (f32[1,1280]{1,0:T(1,128)}, f32[1,1280]{1,0:T(1,128)}, u32[]{:S(2)}, u32[]{:S(2)}) collective-permute-start(f32[1,1280]{1,0:T(1,128)} %constant_dynamic-slice_fusion.2), channel_id=1, source_target_pairs={{0,64},{1,65},{64,0},{65,1},{2,66},{3,67},{66,2},{67,3},{4,68},{5,... | collective-permute-start | bytes 15368 | tf_op jit(solution)/shard_map/ppermute | solution.py:32
  192.9 46.8 %collective-permute-start.27 = (bf16[504,512]{1,0:T(8,128)(2,1)}, bf16[504,512]{1,0:T(8,128)(2,1)}, u32[]{:S(2)}, u32[]{:S(2)}) collective-permute-start(bf16[504,512]{1,0:T(8,128)(2,1)} %get-tuple-element.53), channel_id=1, source_target_pairs={{0,65},{1,64},{64,1},{65,0},{2,67},{3,66},{66,3},{67,2},{4,69},{5,... | collective-permute-start | bytes 1548296 | tf_op jit(solution)/shard_map/ppermute | solution.py:32
  208.1 50.1 %collective-permute-start.18 = (bf16[504,512]{1,0:T(8,128)(2,1)}, bf16[504,512]{1,0:T(8,128)(2,1)}, u32[]{:S(2)}, u32[]{:S(2)}) collective-permute-start(bf16[504,512]{1,0:T(8,128)(2,1)} %get-tuple-element.54), channel_id=1, source_target_pairs={{0,65},{1,64},{64,1},{65,0},{2,67},{3,66},{66,3},{67,2},{4,69},{5,... | collective-permute-start | bytes 1548296 | tf_op jit(solution)/shard_map/ppermute | solution.py:32
  221.6 45.5 %collective-permute-start.7 = (bf16[4,480,128]{2,1,0:T(8,128)(2,1)}, bf16[4,480,128]{2,1,0:T(8,128)(2,1)}, u32[]{:S(2)}, u32[]{:S(2)}) collective-permute-start(bf16[4,480,128]{2,1,0:T(8,128)(2,1)} %near.7), channel_id=1, source_target_pairs={{0,2},{2,4},{4,6},{6,8},{8,10},{10,12},{12,14},{14,16},{16,18},{18... | collective-permute-start | bytes 1474568 | tf_op jit(solution)/shard_map/ppermute | solution.py:37
  223.6 51.3 %collective-permute-start.3 = (bf16[4,480,128]{2,1,0:T(8,128)(2,1)}, bf16[4,480,128]{2,1,0:T(8,128)(2,1)}, u32[]{:S(2)}, u32[]{:S(2)}) collective-permute-start(bf16[4,480,128]{2,1,0:T(8,128)(2,1)} %near.6), channel_id=1, source_target_pairs={{0,2},{2,4},{4,6},{6,8},{8,10},{10,12},{12,14},{14,16},{16,18},{18... | collective-permute-start | bytes 1474568 | tf_op jit(solution)/shard_map/ppermute | solution.py:37
  239.7 43.0 %collective-permute-start.8 = (bf16[504,256]{1,0:T(8,128)(2,1)}, bf16[504,256]{1,0:T(8,128)(2,1)}, u32[]{:S(2)}, u32[]{:S(2)}) collective-permute-start(bf16[504,256]{1,0:T(8,128)(2,1)} %constant_dynamic-slice_fusion.3), channel_id=1, source_target_pairs={{0,65},{1,64},{64,1},{65,0},{2,67},{3,66},{66,3},{67,2},{4,69},{5,... | collective-permute-start | bytes 774152 | tf_op jit(solution)/shard_map/ppermute | solution.py:32
  261.7 29.5 %collective-permute-start.29 = (bf16[480,512]{1,0:T(8,128)(2,1)}, bf16[480,512]{1,0:T(8,128)(2,1)}, u32[]{:S(2)}, u32[]{:S(2)}) collective-permute-start(bf16[480,512]{1,0:T(8,128)(2,1)} %get-tuple-element.50), channel_id=1, source_target_pairs={{0,2},{2,4},{4,6},{6,8},{8,10},{10,12},{12,14},{14,16},{16,18},{18... | collective-permute-start | bytes 1474568 | tf_op jit(solution)/shard_map/ppermute | solution.py:37
  263.6 24.0 %collective-permute-start.30 = (bf16[480,512]{1,0:T(8,128)(2,1)}, bf16[480,512]{1,0:T(8,128)(2,1)}, u32[]{:S(2)}, u32[]{:S(2)}) collective-permute-start(bf16[480,512]{1,0:T(8,128)(2,1)} %get-tuple-element.51), channel_id=1, source_target_pairs={{0,2},{2,4},{4,6},{6,8},{8,10},{10,12},{12,14},{14,16},{16,18},{18... | collective-permute-start | bytes 1474568 | tf_op jit(solution)/shard_map/ppermute | solution.py:37
  285.7 9.9 %collective-permute-start.28 = (bf16[480,256]{1,0:T(8,128)(2,1)}, bf16[480,256]{1,0:T(8,128)(2,1)}, u32[]{:S(2)}, u32[]{:S(2)}) collective-permute-start(bf16[480,256]{1,0:T(8,128)(2,1)} %get-tuple-element.49), channel_id=1, source_target_pairs={{0,2},{2,4},{4,6},{6,8},{8,10},{10,12},{12,14},{14,16},{16,18},{18... | collective-permute-start | bytes 737288 | tf_op jit(solution)/shard_map/ppermute | solution.py:37
where the time goes:
time: 302 us; the launch traced here: 299 us
  Pallas kernels  121 us (40%)
  waiting for transfers between devices  98.1 us (32%)
  starting transfers between devices  59.6 us (20%)
  local copies, waits for them, and re-layouts  11.8 us (4%)
  between operations  7.91 us (3%)
    ppermute x22, waiting for transfers between devices, to_partner(): return lax.ppermute(block, PAIR_AXES, pairs)  97.3 us
    pallas_call x6, Pallas kernels, attend(): pl.pallas_call(attend_kernel, grid_spec=pltpu.PrefetchScalarGridSpec(num_...  65.7 us
    ppermute x22, starting transfers between devices, to_partner(): return lax.ppermute(block, PAIR_AXES, pairs)  35.7 us
    ppermute x9, starting transfers between devices, to_next_span(): return lax.ppermute(block, 'span', [(i, i + 1) for i in range(length - 1)])  23.9 us
    pallas_call x6, Pallas kernels, finish(): pl.pallas_call(late_kernel if late else early_kernel, grid_spec=pltpu.Pre...  20.1 us
    pallas_call x6, Pallas kernels, pack(): pl.pallas_call(functools.partial(pack_kernel, width, start), grid_spec=pl...  18.9 us
    pallas_call x6, Pallas kernels, near_rows(): pl.pallas_call(functools.partial(near_kernel, width, start), grid_spec=pl...  15.9 us
  transfers between devices with their start and end apart: 31, of which 10 were waited for; matrix products, arithmetic and copies ran while one was open for 4% of the time, Pallas kernels for 38%

commit v1 on v0

v1 whole, which is shorter than its diff:
```python
import functools
import math

import jax
import jax.numpy as jnp
from jax import lax
from jax.experimental import pallas as pl
from jax.experimental.pallas import tpu as pltpu
from jax.sharding import PartitionSpec as P


HEAD_DIM = 128
TOK_FRAME = 48
BF = 10
WEIGHTS = 8
TAIL = BF * TOK_FRAME
QUARTER_HEADS = 10
CHUNKS = (3, 3, 2, 2)
GROUPS = ((0, 1), (2,), (3,))
SENDS = (("z", 0), ("z", 1), ("kv", 2), ("kv", 3), ("q", 2), ("q", 3))
VMEM_LIMIT = 66000 * 1024
PAIR_AXES = ("section", "seq")


def spot(section, seq):
    return section * 2 + seq


def to_partner(block, flip_section, flip_seq):
    pairs = [
        (spot(s, q), spot(s ^ flip_section, q ^ flip_seq)) for s in range(2) for q in range(2)
    ]
    return lax.ppermute(block, PAIR_AXES, pairs)


def to_next_span(block):
    length = lax.axis_size("span")
    return lax.ppermute(block, "span", [(i, i + 1) for i in range(length - 1)])


def pack_kernel(width, start, dests, count, *rest):
    sources, outs, (stage, in_sems, out_sems) = rest[:count], rest[count:-3], rest[-3:]
    section, seq = lax.axis_index("section"), lax.axis_index("seq")
    copies = []
    for at, (flip_section, flip_seq) in enumerate(dests):
        other_section = 1 - section if flip_section else section
        other_seq = 1 - seq if flip_seq else seq
        col = spot(other_section, other_seq) * QUARTER_HEADS * HEAD_DIM + start
        col = pl.multiple_of(col, HEAD_DIM)
        for which, ref in enumerate(sources):
            taken = pltpu.make_async_copy(
                ref.at[0, :, pl.ds(col, width)], stage.at[at, which], in_sems.at[at, which]
            )
            taken.start()
            copies.append((at, which, taken))
    sent = []
    for at, which, taken in copies:
        taken.wait()
        put = pltpu.make_async_copy(
            stage.at[at, which], outs[at].at[which], out_sems.at[at, which]
        )
        put.start()
        sent.append(put)
    for put in sent:
        put.wait()


def pack(sources, start, width, dests):
    rows, count = sources[0].shape[1], len(sources)
    shape = jax.ShapeDtypeStruct((count, rows, width), jnp.bfloat16)
    return pl.pallas_call(
        functools.partial(pack_kernel, width, start, dests, count),
        in_specs=[pl.BlockSpec(memory_space=pl.ANY)] * count,
        out_specs=[pl.BlockSpec(memory_space=pl.ANY)] * len(dests),
        scratch_shapes=[
            pltpu.VMEM((len(dests), count, rows, width), jnp.bfloat16),
            pltpu.SemaphoreType.DMA((len(dests), count)),
            pltpu.SemaphoreType.DMA((len(dests), count)),
        ],
        out_shape=[shape] * len(dests),
        cost_estimate=pl.CostEstimate(
            flops=count * len(dests) * rows * width * 8,
            bytes_accessed=4 * count * len(dests) * rows * width,
            transcendentals=0,
        ),
        compiler_params=pltpu.CompilerParams(vmem_limit_bytes=VMEM_LIMIT),
        name="pack",
    )(*sources)


def near_kernel(
    width, start, info_ref, k_ref, v_ref, seq_ref, sec_ref, dia_ref, out_ref, stage, sems, out_sems
):
    rows = k_ref.shape[1]
    cut = pl.ds(rows - TAIL, TAIL)
    cols = pl.ds(pl.multiple_of(info_ref[1] * HEAD_DIM + start, HEAD_DIM), width)
    late = info_ref[3] == 1

    @pl.when(late)
    def _():
        pltpu.make_async_copy(k_ref.at[0, cut, cols], stage.at[0], sems.at[0]).start()
        pltpu.make_async_copy(v_ref.at[0, cut, cols], stage.at[1], sems.at[1]).start()
        pltpu.make_async_copy(sec_ref.at[0, cut], stage.at[2], sems.at[2]).start()
        pltpu.make_async_copy(sec_ref.at[1, cut], stage.at[3], sems.at[3]).start()

    @pl.when(jnp.logical_not(late))
    def _():
        pltpu.make_async_copy(seq_ref.at[0, cut], stage.at[0], sems.at[0]).start()
        pltpu.make_async_copy(seq_ref.at[1, cut], stage.at[1], sems.at[1]).start()
        pltpu.make_async_copy(dia_ref.at[0, cut], stage.at[2], sems.at[2]).start()
        pltpu.make_async_copy(dia_ref.at[1, cut], stage.at[3], sems.at[3]).start()

    for slot in range(4):
        pltpu.make_async_copy(seq_ref.at[0, cut], stage.at[slot], sems.at[slot]).wait()
        pltpu.make_async_copy(stage.at[slot], out_ref.at[slot], out_sems.at[slot]).start()
    for slot in range(4):
        pltpu.make_async_copy(stage.at[slot], out_ref.at[slot], out_sems.at[slot]).wait()


def near_rows(info, key_states, value_states, seq_in, sec_in, dia_in, start, width):
    return pl.pallas_call(
        functools.partial(near_kernel, width, start),
        grid_spec=pltpu.PrefetchScalarGridSpec(
            num_scalar_prefetch=1,
            grid=(),
            in_specs=[pl.BlockSpec(memory_space=pl.ANY)] * 5,
            out_specs=pl.BlockSpec(memory_space=pl.ANY),
            scratch_shapes=[
                pltpu.VMEM((4, TAIL, width), jnp.bfloat16),
                pltpu.SemaphoreType.DMA((4,)),
                pltpu.SemaphoreType.DMA((4,)),
            ],
        ),
        out_shape=jax.ShapeDtypeStruct((4, TAIL, width), jnp.bfloat16),
        cost_estimate=pl.CostEstimate(
            flops=4 * TAIL * width * 8, bytes_accessed=16 * TAIL * width, transcendentals=0
        ),
        compiler_params=pltpu.CompilerParams(vmem_limit_bytes=VMEM_LIMIT),
        name="near",
    )(info, key_states, value_states, seq_in, sec_in, dia_in)


def attend_kernel(
    info_ref, q_ref, k_ref, v_ref, seq_q, sec_q, dia_q, seq_kv, sec_kv, dia_kv, near_ref,
    own_gate, other_gate, *rest
):
    out_ref, qs, ks, vs = rest[-4:]
    rows = q_ref.shape[1]

    @pl.when(pl.program_id(0) == 0)
    def _():
        lane = lax.broadcasted_iota(jnp.int32, (rows, HEAD_DIM), 1)
        for slot in range(6):
            vs[slot, :, HEAD_DIM:] = (lane == 0).astype(jnp.bfloat16)

    qs[0] = q_ref[0]
    ks[0] = k_ref[0]
    vs[0, :, :HEAD_DIM] = v_ref[0]
    for slot, q_in, kv_in in ((1, seq_q, seq_kv), (2, sec_q, sec_kv), (3, dia_q, dia_kv)):
        qs[slot] = q_in[0]
        ks[slot] = kv_in[0]
        vs[slot, :, :HEAD_DIM] = kv_in[1]
    vs[4, :TAIL, :HEAD_DIM] = near_ref[1]
    vs[5, :TAIL, :HEAD_DIM] = near_ref[3]
    factor = math.log2(math.e) / math.sqrt(HEAD_DIM)
    place = lax.broadcasted_iota(jnp.int32, (1, TAIL), 1)
    bias = jnp.where(place >= info_ref[0], 0.0, -jnp.inf)

    gated = [None, None]
    for layer, gate_ref in enumerate((own_gate, other_gate)):
        keys = (ks[2 * layer], ks[2 * layer + 1], near_ref[2 * layer])
        values = (vs[2 * layer], vs[2 * layer + 1], vs[4 + layer, :TAIL])
        scores = []
        for half in range(2):
            query = qs[2 * layer + half]
            parts = [
                lax.dot_general(
                    query, key, (((1,), (1,)), ((), ())), preferred_element_type=jnp.float32
                )
                for key in keys
            ]
            scores.append(parts[:2] + [parts[2] + bias])
        lifted = []
        for parts in scores:
            top = factor * functools.reduce(
                jnp.maximum, [jnp.max(part, axis=-1, keepdims=True) for part in parts]
            )
            lifted.append([jnp.exp2(part * factor - top).astype(jnp.bfloat16) for part in parts])
        for half, parts in enumerate(lifted):
            mixed = sum(
                jnp.dot(part, value, preferred_element_type=jnp.float32)
                for part, value in zip(parts, values)
            )
            attended = (mixed[:, :HEAD_DIM] / mixed[:, HEAD_DIM : HEAD_DIM + 1]).astype(
                jnp.bfloat16
            )
            term = gate_ref[...] * attended.astype(jnp.float32)
            if layer == 0:
                gated[half] = term
            else:
                out_ref[half] = (gated[half] + term).astype(jnp.bfloat16)


def attend(
    info, queries, key_states, value_states, queries_in, pairs_in, near, gate, other_gate, first,
    heads, place, group_heads, filled,
):
    rows = queries.shape[1]
    keys = 2 * rows + TAIL
    local = pl.BlockSpec((1, rows, HEAD_DIM), lambda h, info: (0, 0, info[1] + first + h))
    last = queries_in[0].shape[0] - 1
    operands = [info, queries, key_states, value_states, *queries_in, *pairs_in, near]
    operands += [gate, other_gate]
    in_specs = [local, local, local]
    in_specs += [pl.BlockSpec((1, rows, HEAD_DIM), lambda h, info: (last, 0, h))] * 3
    in_specs += [pl.BlockSpec((2, rows, HEAD_DIM), lambda h, info: (0, 0, h))] * 3
    in_specs.append(pl.BlockSpec((4, TAIL, HEAD_DIM), lambda h, info: (0, 0, h)))
    in_specs.append(pl.BlockSpec((1, HEAD_DIM), lambda h, info: (0, info[1] + first + h)))
    in_specs.append(pl.BlockSpec((1, HEAD_DIM), lambda h, info: (0, first + h)))
    aliases = {}
    if filled is not None:
        aliases = {len(operands): 0}
        operands.append(filled)
        in_specs.append(pl.BlockSpec(memory_space=pl.ANY))
    return pl.pallas_call(
        attend_kernel,
        grid_spec=pltpu.PrefetchScalarGridSpec(
            num_scalar_prefetch=1,
            grid=(heads,),
            in_specs=in_specs,
            out_specs=pl.BlockSpec((2, rows, HEAD_DIM), lambda h, info: (0, 0, place + h)),
            scratch_shapes=[pltpu.VMEM((4, rows, HEAD_DIM), jnp.bfloat16)] * 2
            + [pltpu.VMEM((6, rows, 2 * HEAD_DIM), jnp.bfloat16)],
        ),
        out_shape=jax.ShapeDtypeStruct((2, rows, group_heads * HEAD_DIM), jnp.bfloat16),
        input_output_aliases=aliases,
        cost_estimate=pl.CostEstimate(
            flops=heads * 4 * rows * keys * HEAD_DIM * 4,
            bytes_accessed=heads * HEAD_DIM * rows * 40,
            transcendentals=heads * 4 * rows * keys,
        ),
        compiler_params=pltpu.CompilerParams(vmem_limit_bytes=VMEM_LIMIT),
        name="attend",
    )(*operands)


def tail_rows(gated, latents, far, seq, first, width, base):
    cut = far.shape[0] - TAIL
    added = lax.dynamic_slice(gated, (1 - seq, cut, 0), (1, TAIL, width))[0]
    near = lax.dynamic_slice(latents, (cut, base + first * HEAD_DIM), (TAIL, width))
    latent = jnp.where(seq == 1, near, far[cut:])
    return (latent.astype(jnp.float32) + added.astype(jnp.float32)).astype(jnp.bfloat16)


def finish_kernel(info_ref, picks_ref, gated_ref, near_ref, far_ref, tail_ref, *rest):
    out_ref = rest[-1]
    seq = info_ref[3]
    for half, ref in enumerate((near_ref, far_ref)):
        whole = ref[...].astype(jnp.float32) + gated_ref[half].astype(jnp.float32)
        out_ref[seq if half == 0 else 1 - seq] = whole.astype(jnp.bfloat16)
    shared = info_ref[4]
    for frame in range(BF):
        source = jnp.clip(BF - shared + frame, 0, BF - 1)
        weight = (picks_ref[frame].astype(jnp.float32) + 0.5) / WEIGHTS
        begin = pl.multiple_of(source * TOK_FRAME, TOK_FRAME)
        place = pl.ds(frame * TOK_FRAME, TOK_FRAME)

        @pl.when(frame < shared)
        def _():
            before = tail_ref[pl.ds(begin, TOK_FRAME), :].astype(jnp.float32)
            lead = out_ref[0, place, :].astype(jnp.float32)
            mixed = weight * lead + (1.0 - weight) * before
            out_ref[0, place, :] = mixed.astype(jnp.bfloat16)


def finish(info, picks, gated, latents, far, tail, first, heads, second):
    rows = gated.shape[1]
    width = 2 * HEAD_DIM
    here = lambda h, info, picks: (0, info[1] // 2 + first // 2 + h)
    part = lambda h, info, picks: (0, h)
    operands = [info, picks, gated, latents, far, tail]
    in_specs = [
        pl.BlockSpec((2, rows, width), lambda h, info, picks: (0, 0, h)),
        pl.BlockSpec((rows, width), here),
        pl.BlockSpec((rows, width), part),
        pl.BlockSpec((TAIL, width), part),
    ]
    aliases = {}
    if second is not None:
        aliases = {len(operands): 0}
        operands.append(second)
        in_specs.append(pl.BlockSpec(memory_space=pl.ANY))
    return pl.pallas_call(
        finish_kernel,
        grid_spec=pltpu.PrefetchScalarGridSpec(
            num_scalar_prefetch=2,
            grid=(heads // 2,),
            in_specs=in_specs,
            out_specs=pl.BlockSpec(
                (2, rows, width), lambda h, info, picks: (0, 0, first // 2 + h)
            ),
        ),
        out_shape=jax.ShapeDtypeStruct((2, rows, QUARTER_HEADS * HEAD_DIM), jnp.bfloat16),
        input_output_aliases=aliases,
        cost_estimate=pl.CostEstimate(
            flops=rows * heads * HEAD_DIM * 200,
            bytes_accessed=rows * heads * HEAD_DIM * 18,
            transcendentals=0,
        ),
        compiler_params=pltpu.CompilerParams(vmem_limit_bytes=VMEM_LIMIT),
        name="finish",
    )(*operands)


def local(
    latents, queries, key_states, value_states, gate_scales, window, intersection, blend_index
):
    rows = latents.shape[0]
    quarter = QUARTER_HEADS * HEAD_DIM
    span_pos = lax.axis_index("span")
    section = lax.axis_index("section")
    seq = lax.axis_index("seq")
    earlier = jnp.maximum(span_pos - 1, 0)
    follows = span_pos > 0
    closed = jnp.where(follows, TAIL - TOK_FRAME * window[earlier], TAIL)
    shared = jnp.where(follows, intersection[earlier], 0)
    info = jnp.stack(
        [closed, spot(section, seq) * QUARTER_HEADS, section, seq, shared]
    ).astype(jnp.int32)
    picks = blend_index[earlier]
    base = spot(section, seq) * quarter
    far_base = spot(1 - section, 1 - seq) * quarter

    chunks, groups = len(CHUNKS), len(GROUPS)
    starts = [sum(CHUNKS[:i]) for i in range(chunks)]
    group_first = [starts[group[0]] for group in GROUPS]
    group_heads = [sum(CHUNKS[k] for k in group) for group in GROUPS]
    queries_in, pairs_in = {}, {}
    for kind, k in SENDS:
        first, heads = starts[k], CHUNKS[k]
        sources = {"z": (key_states, value_states, queries), "kv": (key_states, value_states),
                   "q": (queries,)}[kind]
        ways = {"dia": (1, 1), "seq": (0, 1), "sec": (1, 0)}
        arrived = {}
        batches = (("dia",), ("seq", "sec")) if (kind, k) == SENDS[0] else (tuple(ways),)
        for batch in batches:
            packed = pack(
                sources, first * HEAD_DIM, heads * HEAD_DIM, tuple(ways[way] for way in batch)
            )
            for way, block in zip(batch, packed):
                arrived[way] = to_partner(block, *ways[way])
        arrived = (arrived["seq"], arrived["sec"], arrived["dia"])
        if kind in ("z", "q"):
            queries_in[k] = arrived
        if kind in ("z", "kv"):
            pairs_in[k] = arrived
    far_latents = []
    for first, heads in zip(group_first, group_heads):
        sent = lax.dynamic_slice_in_dim(
            latents, far_base + first * HEAD_DIM, heads * HEAD_DIM, 1
        )
        far_latents.append(to_partner(sent, 1, 1))
    other_gate = to_partner(
        lax.dynamic_slice_in_dim(gate_scales, spot(1 - section, seq) * quarter, quarter, 1), 1, 0
    )

    attended = []
    for g, group in enumerate(GROUPS):
        filled = None
        for k in group:
            first, heads = starts[k], CHUNKS[k]
            near = near_rows(
                info, key_states, value_states, *pairs_in[k], first * HEAD_DIM,
                heads * HEAD_DIM,
            )
            near = to_next_span(near)
            filled = attend(
                info, queries, key_states, value_states, queries_in[k], pairs_in[k], near,
                gate_scales, other_gate, first, heads, first - group_first[g], group_heads[g], filled,
            )
        attended.append(filled)

    tails = []
    for g in range(groups):
        far = far_latents[g]
        if g:
            far, _ = lax.optimization_barrier((far, tails[-1]))
        tail = tail_rows(
            attended[g], latents, far, seq, group_first[g], group_heads[g] * HEAD_DIM, base
        )
        tails.append(tail)
    arrived_tails = []
    for g in range(groups):
        arrived_tails.append(to_next_span(tails[g]))
    second = None
    for g in range(groups):
        second = finish(
            info, picks, attended[g], latents, far_latents[g], arrived_tails[g],
            group_first[g], group_heads[g], second,
        )
    return second.reshape(2 * rows, quarter)


def solution(mesh):
    in_specs = (
        P(("span", "seq"), None),
        P("section", ("span", "seq"), None),
        P("section", ("span", "seq"), None),
        P("section", ("span", "seq"), None),
        P("section", None),
        P(),
        P(),
        P(),
    )
    out_specs = P("span", ("section", "seq"))

    return jax.shard_map(local, mesh=mesh, in_specs=in_specs, out_specs=out_specs, check_vma=False)
```

time: 302 us -> 311 us (1.030)
  waiting for transfers between devices: 98.1 us -> 148 us
  Pallas kernels: 121 us -> 95.4 us
  starting transfers between devices: 59.6 us -> 48.4 us
  between operations: 7.91 us -> 1.54 us
  other arithmetic: 0.65 us -> 6.64 us
  local copies, waits for them, and re-layouts: 11.8 us -> 8.61 us
    ppermute x22, waiting for transfers between devices: 97.3 us -> 148 us  [to_partner(): return lax.ppermute(block, PAIR_AXES, pairs)]
    pallas_call x12 -> x10, Pallas kernels: 39 us -> 27.3 us  [the longest x7 16.2 us: pack(): pl.pallas_call(functools.partial(pack_kernel, width, start, dests, count)...]
    pallas_call x6 -> x4, Pallas kernels: 65.7 us -> 57 us  [attend(): pl.pallas_call(attend_kernel, grid_spec=pltpu.PrefetchScalarGridSpec(num_...]
    convert_element_type x0 -> x3, other arithmetic: none -> 6.64 us  [tail_rows(): (latent.astype(jnp.float32) + added.astype(jnp.float32)).astype(jnp.bfloa...]
    ppermute x9 -> x7, starting transfers between devices: 23.9 us -> 18.3 us  [to_next_span(): return lax.ppermute(block, 'span', [(i, i + 1) for i in range(length - 1)])]
    ppermute x22, starting transfers between devices: 35.7 us -> 30.2 us  [to_partner(): return lax.ppermute(block, PAIR_AXES, pairs)]
    pallas_call x6 -> x4, Pallas kernels: 15.9 us -> 11.2 us  [near_rows(): pl.pallas_call(functools.partial(near_kernel, width, start), grid_spec=pl...]
  transfers between devices with their start and end apart: 31 -> 29, of which waited for: 10 -> 7; matrix products, arithmetic and copies ran while one was open for 4% -> 5% of each run, Pallas kernels for 38% -> 29%
where the time goes in v1:
time: 311 us; the launch traced here: 308 us
  waiting for transfers between devices  148 us (48%)
  Pallas kernels  95.4 us (31%)
  starting transfers between devices  48.4 us (16%)
  local copies, waits for them, and re-layouts  8.61 us (3%)
  other arithmetic  6.64 us (2%)
    ppermute x22, waiting for transfers between devices, to_partner(): return lax.ppermute(block, PAIR_AXES, pairs)  148 us
    pallas_call x4, Pallas kernels, attend(): pl.pallas_call(attend_kernel, grid_spec=pltpu.PrefetchScalarGridSpec(num_...  57 us
    ppermute x22, starting transfers between devices, to_partner(): return lax.ppermute(block, PAIR_AXES, pairs)  30.2 us
    ppermute x7, starting transfers between devices, to_next_span(): return lax.ppermute(block, 'span', [(i, i + 1) for i in range(length - 1)])  18.3 us
    pallas_call x7, Pallas kernels, pack(): pl.pallas_call(functools.partial(pack_kernel, width, start, dests, count)...  16.2 us
    pallas_call x4, Pallas kernels, near_rows(): pl.pallas_call(functools.partial(near_kernel, width, start), grid_spec=pl...  11.2 us
    pallas_call x3, Pallas kernels, finish(): pl.pallas_call(finish_kernel, grid_spec=pltpu.PrefetchScalarGridSpec(num_...  11 us
    convert_element_type x3, other arithmetic, tail_rows(): (latent.astype(jnp.float32) + added.astype(jnp.float32)).astype(jnp.bfloa...  6.64 us
  transfers between devices with their start and end apart: 29, of which 7 were waited for; matrix products, arithmetic and copies ran while one was open for 5% of the time, Pallas kernels for 29%

profile of v1, /device:TPU:2, one launch (start us, length us, event | category | flops | bytes accessed | tf_op | source)
XLA Modules:
  0.0 308.3 jit_solution(17713961709989237677)
XLA Ops:
  0.0 2.5 pack.10
  2.5 4.0 %collective-permute-start.15 = (bf16[3,504,384]{2,1,0:T(8,128)(2,1)}, bf16[3,504,384]{2,1,0:T(8,128)(2,1)}, u32[]{:S(2)}, u32[]{:S(2)}) collective-permute-start(bf16[3,504,384]{2,1,0:T(8,128)(2,1)} %get-tuple-element.33), channel_id=1, source_target_pairs={{0,1},{1,0},{64,65},{65,64},{2,3},{3,2},{66,67},{67,66},{4,5},{5,4... | collective-permute-start | bytes 3483656 | tf_op jit(solution)/shard_map/ppermute | solution.py:33
  7.5 1.9 pack.12
  9.4 1.2 collective-permute-start.19
  10.7 2.3 pack.13
  13.0 2.5 collective-permute-start.22
  17.2 57.5 %collective-permute-done.7.other_gate = f32[1,1280]{1,0:T(1,128)} collective-permute-done((f32[1,1280]{1,0:T(1,128)S(1)}, f32[1,1280]{1,0:T(1,128)}, u32[]{:S(2)}, u32[]{:S(2)}) %collective-permute-start.7) | collective-permute-done | bytes 5152 | tf_op jit(solution)/shard_map/ppermute | solution.py:33
  74.7 1.0 collective-permute-start.23
  75.7 2.1 pack.11
  78.6 3.1 pack.9
  81.7 2.5 collective-permute-start.11
  84.1 5.5 %collective-permute-done.23.sec_ref.sec_kv = bf16[2,504,256]{2,1,0:T(8,128)(2,1)} collective-permute-done((bf16[2,504,256]{2,1,0:T(8,128)(2,1)}, bf16[2,504,256]{2,1,0:T(8,128)(2,1)}, u32[]{:S(2)}, u32[]{:S(2)}) %collective-permute-start.23) | collective-permute-done | bytes 516128 | tf_op jit(solution)/shard_map/ppermute | solution.py:33
  91.3 2.5 collective-permute-start.24
  93.9 2.3 pack.8
  96.2 36.5 %collective-permute-done.17.dia_ref.dia_q.dia_kv = bf16[3,504,384]{2,1,0:T(8,128)(2,1)} collective-permute-done((bf16[3,504,384]{2,1,0:T(8,128)(2,1)}, bf16[3,504,384]{2,1,0:T(8,128)(2,1)}, u32[]{:S(2)}, u32[]{:S(2)}) %collective-permute-start.17) | collective-permute-done | bytes 1161248 | tf_op jit(solution)/shard_map/ppermute | solution.py:33
  132.7 1.3 dynamic_slice.40
  134.1 1.2 dynamic_slice.39
  137.2 2.9 near.6
  140.1 37.4 %collective-permute-done.24.dia_ref.dia_kv = bf16[2,504,256]{2,1,0:T(8,128)(2,1)} collective-permute-done((bf16[2,504,256]{2,1,0:T(8,128)(2,1)}, bf16[2,504,256]{2,1,0:T(8,128)(2,1)}, u32[]{:S(2)}, u32[]{:S(2)}) %collective-permute-start.24) | collective-permute-done | bytes 516128 | tf_op jit(solution)/shard_map/ppermute | solution.py:33
  177.5 1.9 collective-permute-start.18
  179.4 2.8 near.7
  182.2 3.6 %collective-permute-start.25 = (bf16[4,480,256]{2,1,0:T(8,128)(2,1)}, bf16[4,480,256]{2,1,0:T(8,128)(2,1)}, u32[]{:S(2)}, u32[]{:S(2)}) collective-permute-start(bf16[4,480,256]{2,1,0:T(8,128)(2,1)} %near.7), channel_id=1, source_target_pairs={{0,2},{2,4},{4,6},{6,8},{8,10},{10,12},{12,14},{14,16},{16,18},{18... | collective-permute-start | bytes 2949128 | tf_op jit(solution)/shard_map/ppermute | solution.py:38
  186.7 2.8 near.5
  189.5 1.9 collective-permute-start.14
  191.5 8.4 %collective-permute-done.4.sec_ref.sec_kv = bf16[2,504,256]{2,1,0:T(8,128)(2,1)} collective-permute-done((bf16[2,504,256]{2,1,0:T(8,128)(2,1)}, bf16[2,504,256]{2,1,0:T(8,128)(2,1)}, u32[]{:S(2)}, u32[]{:S(2)}) %collective-permute-start.4) | collective-permute-done | bytes 516128 | tf_op jit(solution)/shard_map/ppermute | solution.py:33
  200.1 1.0 collective-permute-done.5.dia_ref.dia_kv
  201.9 2.0 pack.7
  203.8 1.9 constant_dynamic-slice_fusion.1
  205.8 2.1 constant_dynamic-slice_fusion
  207.8 2.8 near.4
  210.6 2.6 collective-permute-start.10
  214.8 12.0 %attend.7.gated_ref = bf16[2,504,256]{2,1,0:T(8,128)(2,1)} custom-call(s32[5]{0:T(128)} %stack.23.info_ref, bf16[1,504,5120]{2,1,0:T(8,128)(2,1)} %q_ref.7, bf16[1,504,5120]{2,1,0:T(8,128)(2,1)} %k_ref.15, bf16[1,504,5120]{2,1,0:T(8,128)(2,1)} %v_ref.15, bf16[1,504,256]{2,1,0:T(8,128)(2,1)} %collective-permute-done.19.seq_q, ...), custom_call_target="tpu_custom_call" | custom-call | flops 3071803392 | bytes 5160960 | tf_op jit(solution)/shard_map/attend/pallas_call | solution.py:225
  226.8 2.1 collective-permute-start.6
  228.9 16.5 %attend.5.rest_0_ = bf16[2,504,768]{2,1,0:T(8,128)(2,1)} custom-call(s32[5]{0:T(128)} %stack.23.info_ref, bf16[1,504,5120]{2,1,0:T(8,128)(2,1)} %q_ref.7, bf16[1,504,5120]{2,1,0:T(8,128)(2,1)} %k_ref.15, bf16[1,504,5120]{2,1,0:T(8,128)(2,1)} %v_ref.15, bf16[3,504,384]{2,1,0:T(8,128)(2,1)} %collective-permute-done.15.seq_ref.seq_q.seq_kv, ...), custom_call_target="tpu_custom_call" | custom-call | flops 4607705088 | bytes 7741440 | tf_op jit(solution)/shard_map/attend/pallas_call | solution.py:225
  245.4 2.6 collective-permute-start.1
  248.0 16.5 %attend.6.gated_ref = bf16[2,504,768]{2,1,0:T(8,128)(2,1)} custom-call(s32[5]{0:T(128)} %stack.23.info_ref, bf16[1,504,5120]{2,1,0:T(8,128)(2,1)} %q_ref.7, bf16[1,504,5120]{2,1,0:T(8,128)(2,1)} %k_ref.15, bf16[1,504,5120]{2,1,0:T(8,128)(2,1)} %v_ref.15, ...), custom_call_target="tpu_custom_call", output_to_operand_aliasing={{}: (13, {})} | custom-call | flops 4607705088 | bytes 7741440 | tf_op jit(solution)/shard_map/attend/pallas_call | solution.py:225
  265.3 2.7 fusion
  268.0 2.5 collective-permute-start.8
  270.5 3.0 collective-permute-start.28
  273.5 1.3 collective-permute-done.2.dia_q
  274.8 12.0 %attend.4.gated_ref = bf16[2,504,256]{2,1,0:T(8,128)(2,1)} custom-call(s32[5]{0:T(128)} %stack.23.info_ref, bf16[1,504,5120]{2,1,0:T(8,128)(2,1)} %q_ref.7, bf16[1,504,5120]{2,1,0:T(8,128)(2,1)} %k_ref.15, bf16[1,504,5120]{2,1,0:T(8,128)(2,1)} %v_ref.15, bf16[1,504,256]{2,1,0:T(8,128)(2,1)} %collective-permute-done.seq_q, ...), custom_call_target="tpu_custom_call" | custom-call | flops 3071803392 | bytes 5160960 | tf_op jit(solution)/shard_map/attend/pallas_call | solution.py:225
  286.8 2.0 fusion.2
  288.7 2.9 collective-permute-start.27
  291.6 2.0 fusion.1
  293.6 2.9 collective-permute-start.26
  297.3 5.0 %finish.3.rest_0_ = bf16[2,504,1280]{2,1,0:T(8,128)(2,1)} custom-call(s32[5]{0:T(128)} %stack.23.info_ref, s32[10]{0:T(128)} %dynamic-slice_reduce_fusion.picks_ref, bf16[2,504,768]{2,1,0:T(8,128)(2,1)} %attend.6.gated_ref, bf16[504,5120]{1,0:T(8,128)(2,1)} %near_ref.5, bf16[504,768]{1,0:T(8,128)(2,1)} %collective-permute-done.10.far_ref, ...), custom_call_target="tpu_custom_call" | custom-call | flops 77414400 | bytes 6967296 | tf_op jit(solution)/shard_map/finish/pallas_call | solution.py:293
  302.3 3.0 finish.4.rest_0_
  305.3 3.0 finish.5
  (40 shorter events, 10.9 us)
Async XLA Ops:
  2.5 88.1 %collective-permute-start.15 = (bf16[3,504,384]{2,1,0:T(8,128)(2,1)}, bf16[3,504,384]{2,1,0:T(8,128)(2,1)}, u32[]{:S(2)}, u32[]{:S(2)}) collective-permute-start(bf16[3,504,384]{2,1,0:T(8,128)(2,1)} %get-tuple-element.33), channel_id=1, source_target_pairs={{0,1},{1,0},{64,65},{65,64},{2,3},{3,2},{66,67},{67,66},{4,5},{5,4... | collective-permute-start | bytes 3483656 | tf_op jit(solution)/shard_map/ppermute | solution.py:33
  6.5 84.9 %collective-permute-start.16 = (bf16[3,504,384]{2,1,0:T(8,128)(2,1)}, bf16[3,504,384]{2,1,0:T(8,128)(2,1)}, u32[]{:S(2)}, u32[]{:S(2)}) collective-permute-start(bf16[3,504,384]{2,1,0:T(8,128)(2,1)} %get-tuple-element.34), channel_id=1, source_target_pairs={{0,64},{1,65},{64,0},{65,1},{2,66},{3,67},{66,2},{67,3},{4,68},{5,... | collective-permute-start | bytes 3483656 | tf_op jit(solution)/shard_map/ppermute | solution.py:33
  9.4 68.3 %collective-permute-start.19 = (bf16[1,504,256]{2,1,0:T(8,128)(2,1)}, bf16[1,504,256]{2,1,0:T(8,128)(2,1)}, u32[]{:S(2)}, u32[]{:S(2)}) collective-permute-start(bf16[1,504,256]{2,1,0:T(8,128)(2,1)} %get-tuple-element.36), channel_id=1, source_target_pairs={{0,1},{1,0},{64,65},{65,64},{2,3},{3,2},{66,67},{67,66},{4,5},{5,4... | collective-permute-start | bytes 774152 | tf_op jit(solution)/shard_map/ppermute | solution.py:33
  13.0 68.6 %collective-permute-start.22 = (bf16[2,504,256]{2,1,0:T(8,128)(2,1)}, bf16[2,504,256]{2,1,0:T(8,128)(2,1)}, u32[]{:S(2)}, u32[]{:S(2)}) collective-permute-start(bf16[2,504,256]{2,1,0:T(8,128)(2,1)} %get-tuple-element.39), channel_id=1, source_target_pairs={{0,1},{1,0},{64,65},{65,64},{2,3},{3,2},{66,67},{67,66},{4,5},{5,4... | collective-permute-start | bytes 1548296 | tf_op jit(solution)/shard_map/ppermute | solution.py:33
  16.2 58.5 %collective-permute-start.7 = (f32[1,1280]{1,0:T(1,128)S(1)}, f32[1,1280]{1,0:T(1,128)}, u32[]{:S(2)}, u32[]{:S(2)}) collective-permute-start(f32[1,1280]{1,0:T(1,128)S(1)} %constant_dynamic-slice_fusion.3), channel_id=1, source_target_pairs={{0,64},{1,65},{64,0},{65,1},{2,66},{3,67},{66,2},{67,3},{4,68},{5,... | collective-permute-start | bytes 15368 | tf_op jit(solution)/shard_map/ppermute | solution.py:33
  74.7 14.9 %collective-permute-start.23 = (bf16[2,504,256]{2,1,0:T(8,128)(2,1)}, bf16[2,504,256]{2,1,0:T(8,128)(2,1)}, u32[]{:S(2)}, u32[]{:S(2)}) collective-permute-start(bf16[2,504,256]{2,1,0:T(8,128)(2,1)} %get-tuple-element.40), channel_id=1, source_target_pairs={{0,64},{1,65},{64,0},{65,1},{2,66},{3,67},{66,2},{67,3},{4,68},{5,... | collective-permute-start | bytes 1548296 | tf_op jit(solution)/shard_map/ppermute | solution.py:33
  77.8 54.9 %collective-permute-start.17 = (bf16[3,504,384]{2,1,0:T(8,128)(2,1)}, bf16[3,504,384]{2,1,0:T(8,128)(2,1)}, u32[]{:S(2)}, u32[]{:S(2)}) collective-permute-start(bf16[3,504,384]{2,1,0:T(8,128)(2,1)} %pack.11), channel_id=1, source_target_pairs={{0,65},{1,64},{64,1},{65,0},{2,67},{3,66},{66,3},{67,2},{4,69},{5,... | collective-permute-start | bytes 3483656 | tf_op jit(solution)/shard_map/ppermute | solution.py:33
  81.7 100.5 %collective-permute-start.11 = (bf16[3,504,384]{2,1,0:T(8,128)(2,1)}, bf16[3,504,384]{2,1,0:T(8,128)(2,1)}, u32[]{:S(2)}, u32[]{:S(2)}) collective-permute-start(bf16[3,504,384]{2,1,0:T(8,128)(2,1)} %get-tuple-element.30), channel_id=1, source_target_pairs={{0,1},{1,0},{64,65},{65,64},{2,3},{3,2},{66,67},{67,66},{4,5},{5,4... | collective-permute-start | bytes 3483656 | tf_op jit(solution)/shard_map/ppermute | solution.py:33
  89.6 96.2 %collective-permute-start.12 = (bf16[3,504,384]{2,1,0:T(8,128)(2,1)}, bf16[3,504,384]{2,1,0:T(8,128)(2,1)}, u32[]{:S(2)}, u32[]{:S(2)}) collective-permute-start(bf16[3,504,384]{2,1,0:T(8,128)(2,1)} %get-tuple-element.31), channel_id=1, source_target_pairs={{0,64},{1,65},{64,0},{65,1},{2,66},{3,67},{66,2},{67,3},{4,68},{5,... | collective-permute-start | bytes 3483656 | tf_op jit(solution)/shard_map/ppermute | solution.py:33
  90.6 95.2 %collective-permute-start.13 = (bf16[3,504,384]{2,1,0:T(8,128)(2,1)}, bf16[3,504,384]{2,1,0:T(8,128)(2,1)}, u32[]{:S(2)}, u32[]{:S(2)}) collective-permute-start(bf16[3,504,384]{2,1,0:T(8,128)(2,1)} %get-tuple-element.32), channel_id=1, source_target_pairs={{0,65},{1,64},{64,1},{65,0},{2,67},{3,66},{66,3},{67,2},{4,69},{5,... | collective-permute-start | bytes 3483656 | tf_op jit(solution)/shard_map/ppermute | solution.py:33
  91.3 86.1 %collective-permute-start.24 = (bf16[2,504,256]{2,1,0:T(8,128)(2,1)}, bf16[2,504,256]{2,1,0:T(8,128)(2,1)}, u32[]{:S(2)}, u32[]{:S(2)}) collective-permute-start(bf16[2,504,256]{2,1,0:T(8,128)(2,1)} %get-tuple-element.41), channel_id=1, source_target_pairs={{0,65},{1,64},{64,1},{65,0},{2,67},{3,66},{66,3},{67,2},{4,69},{5,... | collective-permute-start | bytes 1548296 | tf_op jit(solution)/shard_map/ppermute | solution.py:33
  132.7 56.8 %collective-permute-start.3 = (bf16[2,504,256]{2,1,0:T(8,128)(2,1)}, bf16[2,504,256]{2,1,0:T(8,128)(2,1)}, u32[]{:S(2)}, u32[]{:S(2)}) collective-permute-start(bf16[2,504,256]{2,1,0:T(8,128)(2,1)} %get-tuple-element.27), channel_id=1, source_target_pairs={{0,1},{1,0},{64,65},{65,64},{2,3},{3,2},{66,67},{67,66},{4,5},{5,4... | collective-permute-start | bytes 1548296 | tf_op jit(solution)/shard_map/ppermute | solution.py:33
  177.5 49.3 %collective-permute-start.18 = (bf16[4,480,384]{2,1,0:T(8,128)(2,1)}, bf16[4,480,384]{2,1,0:T(8,128)(2,1)}, u32[]{:S(2)}, u32[]{:S(2)}) collective-permute-start(bf16[4,480,384]{2,1,0:T(8,128)(2,1)} %near.6), channel_id=1, source_target_pairs={{0,2},{2,4},{4,6},{6,8},{8,10},{10,12},{12,14},{14,16},{16,18},{18... | collective-permute-start | bytes 4423688 | tf_op jit(solution)/shard_map/ppermute | solution.py:38
  182.2 31.8 %collective-permute-start.25 = (bf16[4,480,256]{2,1,0:T(8,128)(2,1)}, bf16[4,480,256]{2,1,0:T(8,128)(2,1)}, u32[]{:S(2)}, u32[]{:S(2)}) collective-permute-start(bf16[4,480,256]{2,1,0:T(8,128)(2,1)} %near.7), channel_id=1, source_target_pairs={{0,2},{2,4},{4,6},{6,8},{8,10},{10,12},{12,14},{14,16},{16,18},{18... | collective-permute-start | bytes 2949128 | tf_op jit(solution)/shard_map/ppermute | solution.py:38
  185.8 14.1 %collective-permute-start.4 = (bf16[2,504,256]{2,1,0:T(8,128)(2,1)}, bf16[2,504,256]{2,1,0:T(8,128)(2,1)}, u32[]{:S(2)}, u32[]{:S(2)}) collective-permute-start(bf16[2,504,256]{2,1,0:T(8,128)(2,1)} %get-tuple-element.28), channel_id=1, source_target_pairs={{0,64},{1,65},{64,0},{65,1},{2,66},{3,67},{66,2},{67,3},{4,68},{5,... | collective-permute-start | bytes 1548296 | tf_op jit(solution)/shard_map/ppermute | solution.py:33
  185.9 15.3 %collective-permute-start.5 = (bf16[2,504,256]{2,1,0:T(8,128)(2,1)}, bf16[2,504,256]{2,1,0:T(8,128)(2,1)}, u32[]{:S(2)}, u32[]{:S(2)}) collective-permute-start(bf16[2,504,256]{2,1,0:T(8,128)(2,1)} %get-tuple-element.29), channel_id=1, source_target_pairs={{0,65},{1,64},{64,1},{65,0},{2,67},{3,66},{66,3},{67,2},{4,69},{5,... | collective-permute-start | bytes 1548296 | tf_op jit(solution)/shard_map/ppermute | solution.py:33
  189.5 55.9 %collective-permute-start.14 = (bf16[4,480,384]{2,1,0:T(8,128)(2,1)}, bf16[4,480,384]{2,1,0:T(8,128)(2,1)}, u32[]{:S(2)}, u32[]{:S(2)}) collective-permute-start(bf16[4,480,384]{2,1,0:T(8,128)(2,1)} %near.5), channel_id=1, source_target_pairs={{0,2},{2,4},{4,6},{6,8},{8,10},{10,12},{12,14},{14,16},{16,18},{18... | collective-permute-start | bytes 4423688 | tf_op jit(solution)/shard_map/ppermute | solution.py:38
  199.8 10.8 %collective-permute-start.20 = (bf16[1,504,256]{2,1,0:T(8,128)(2,1)}, bf16[1,504,256]{2,1,0:T(8,128)(2,1)}, u32[]{:S(2)}, u32[]{:S(2)}) collective-permute-start(bf16[1,504,256]{2,1,0:T(8,128)(2,1)} %get-tuple-element.37), channel_id=1, source_target_pairs={{0,64},{1,65},{64,0},{65,1},{2,66},{3,67},{66,2},{67,3},{4,68},{5,... | collective-permute-start | bytes 774152 | tf_op jit(solution)/shard_map/ppermute | solution.py:33
  201.2 12.1 %collective-permute-start.21 = (bf16[1,504,256]{2,1,0:T(8,128)(2,1)}, bf16[1,504,256]{2,1,0:T(8,128)(2,1)}, u32[]{:S(2)}, u32[]{:S(2)}) collective-permute-start(bf16[1,504,256]{2,1,0:T(8,128)(2,1)} %get-tuple-element.38), channel_id=1, source_target_pairs={{0,65},{1,64},{64,1},{65,0},{2,67},{3,66},{66,3},{67,2},{4,69},{5,... | collective-permute-start | bytes 774152 | tf_op jit(solution)/shard_map/ppermute | solution.py:33
  210.6 53.9 %collective-permute-start.10 = (bf16[504,768]{1,0:T(8,128)(2,1)}, bf16[504,768]{1,0:T(8,128)(2,1)}, u32[]{:S(2)}, u32[]{:S(2)}) collective-permute-start(bf16[504,768]{1,0:T(8,128)(2,1)} %constant_dynamic-slice_fusion), channel_id=1, source_target_pairs={{0,65},{1,64},{64,1},{65,0},{2,67},{3,66},{66,3},{67,2},{4,69},{5,... | collective-permute-start | bytes 2322440 | tf_op jit(solution)/shard_map/ppermute | solution.py:33
  213.2 73.5 %collective-permute-start.9 = (bf16[504,256]{1,0:T(8,128)(2,1)}, bf16[504,256]{1,0:T(8,128)(2,1)}, u32[]{:S(2)}, u32[]{:S(2)}) collective-permute-start(bf16[504,256]{1,0:T(8,128)(2,1)} %get-tuple-element.43), channel_id=1, source_target_pairs={{0,65},{1,64},{64,1},{65,0},{2,67},{3,66},{66,3},{67,2},{4,69},{5,... | collective-permute-start | bytes 774152 | tf_op jit(solution)/shard_map/ppermute | solution.py:33
  213.9 54.0 %collective-permute-start = (bf16[1,504,256]{2,1,0:T(8,128)(2,1)}, bf16[1,504,256]{2,1,0:T(8,128)(2,1)}, u32[]{:S(2)}, u32[]{:S(2)}) collective-permute-start(bf16[1,504,256]{2,1,0:T(8,128)(2,1)} %get-tuple-element.24), channel_id=1, source_target_pairs={{0,1},{1,0},{64,65},{65,64},{2,3},{3,2},{66,67},{67,66},{4,5},{5,4... | collective-permute-start | bytes 774152 | tf_op jit(solution)/shard_map/ppermute | solution.py:33
  226.8 48.0 %collective-permute-start.6 = (bf16[4,480,256]{2,1,0:T(8,128)(2,1)}, bf16[4,480,256]{2,1,0:T(8,128)(2,1)}, u32[]{:S(2)}, u32[]{:S(2)}) collective-permute-start(bf16[4,480,256]{2,1,0:T(8,128)(2,1)} %near.4), channel_id=1, source_target_pairs={{0,2},{2,4},{4,6},{6,8},{8,10},{10,12},{12,14},{14,16},{16,18},{18... | collective-permute-start | bytes 2949128 | tf_op jit(solution)/shard_map/ppermute | solution.py:38
  245.4 25.1 %collective-permute-start.1 = (bf16[1,504,256]{2,1,0:T(8,128)(2,1)}, bf16[1,504,256]{2,1,0:T(8,128)(2,1)}, u32[]{:S(2)}, u32[]{:S(2)}) collective-permute-start(bf16[1,504,256]{2,1,0:T(8,128)(2,1)} %get-tuple-element.25), channel_id=1, source_target_pairs={{0,64},{1,65},{64,0},{65,1},{2,66},{3,67},{66,2},{67,3},{4,68},{5,... | collective-permute-start | bytes 774152 | tf_op jit(solution)/shard_map/ppermute | solution.py:33
  264.5 10.3 %collective-permute-start.2 = (bf16[1,504,256]{2,1,0:T(8,128)(2,1)}, bf16[1,504,256]{2,1,0:T(8,128)(2,1)}, u32[]{:S(2)}, u32[]{:S(2)}) collective-permute-start(bf16[1,504,256]{2,1,0:T(8,128)(2,1)} %get-tuple-element.26), channel_id=1, source_target_pairs={{0,65},{1,64},{64,1},{65,0},{2,67},{3,66},{66,3},{67,2},{4,69},{5,... | collective-permute-start | bytes 774152 | tf_op jit(solution)/shard_map/ppermute | solution.py:33
  268.0 23.7 %collective-permute-start.8 = (bf16[504,256]{1,0:T(8,128)(2,1)}, bf16[504,256]{1,0:T(8,128)(2,1)}, u32[]{:S(2)}, u32[]{:S(2)}) collective-permute-start(bf16[504,256]{1,0:T(8,128)(2,1)} %get-tuple-element.44), channel_id=1, source_target_pairs={{0,65},{1,64},{64,1},{65,0},{2,67},{3,66},{66,3},{67,2},{4,69},{5,... | collective-permute-start | bytes 774152 | tf_op jit(solution)/shard_map/ppermute | solution.py:33
  270.5 26.8 %collective-permute-start.28 = (bf16[480,768]{1,0:T(8,128)(2,1)}, bf16[480,768]{1,0:T(8,128)(2,1)}, u32[]{:S(2)}, u32[]{:S(2)}) collective-permute-start(bf16[480,768]{1,0:T(8,128)(2,1)} %fusion), channel_id=1, source_target_pairs={{0,2},{2,4},{4,6},{6,8},{8,10},{10,12},{12,14},{14,16},{16,18},{18... | collective-permute-start | bytes 2211848 | tf_op jit(solution)/shard_map/ppermute | solution.py:38
  286.8 9.8 %copy-start = (s32[31,10]{0,1:T(8,128)S(1)}, s32[31,10]{0,1:T(8,128)}, u32[]{:S(2)}) copy-start(s32[31,10]{0,1:T(8,128)} %param.15) | copy-start | bytes 3724
  288.7 13.6 %collective-permute-start.27 = (bf16[480,256]{1,0:T(8,128)(2,1)}, bf16[480,256]{1,0:T(8,128)(2,1)}, u32[]{:S(2)}, u32[]{:S(2)}) collective-permute-start(bf16[480,256]{1,0:T(8,128)(2,1)} %fusion.2), channel_id=1, source_target_pairs={{0,2},{2,4},{4,6},{6,8},{8,10},{10,12},{12,14},{14,16},{16,18},{18... | collective-permute-start | bytes 737288 | tf_op jit(solution)/shard_map/ppermute | solution.py:38
  293.6 11.7 %collective-permute-start.26 = (bf16[480,256]{1,0:T(8,128)(2,1)}, bf16[480,256]{1,0:T(8,128)(2,1)}, u32[]{:S(2)}, u32[]{:S(2)}) collective-permute-start(bf16[480,256]{1,0:T(8,128)(2,1)} %fusion.1), channel_id=1, source_target_pairs={{0,2},{2,4},{4,6},{6,8},{8,10},{10,12},{12,14},{14,16},{16,18},{18... | collective-permute-start | bytes 737288 | tf_op jit(solution)/shard_map/ppermute | solution.py:38

commit v2 on v1

--- a/solution.py
+++ b/solution.py
@@ -17,6 +17,7 @@
 QUARTER_HEADS = 10
 CHUNKS = (3, 3, 2, 2)
 GROUPS = ((0, 1), (2,), (3,))
+FINISHES = ((0,), (1, 2))
 SENDS = (("z", 0), ("z", 1), ("kv", 2), ("kv", 3), ("q", 2), ("q", 3))
 VMEM_LIMIT = 66000 * 1024
 PAIR_AXES = ("section", "seq")
@@ -142,7 +143,7 @@
 
 def attend_kernel(
     info_ref, q_ref, k_ref, v_ref, seq_q, sec_q, dia_q, seq_kv, sec_kv, dia_kv, near_ref,
-    own_gate, other_gate, *rest
+    own_gate, other_gate, latent_ref, *rest
 ):
     out_ref, qs, ks, vs = rest[-4:]
     rows = q_ref.shape[1]
@@ -195,28 +196,28 @@
                 jnp.bfloat16
             )
             term = gate_ref[...] * attended.astype(jnp.float32)
-            if layer == 0:
-                gated[half] = term
-            else:
-                out_ref[half] = (gated[half] + term).astype(jnp.bfloat16)
+            gated[half] = term if layer == 0 else gated[half] + term
+    out_ref[0] = (latent_ref[...].astype(jnp.float32) + gated[0]).astype(jnp.bfloat16)
+    out_ref[1] = gated[1].astype(jnp.bfloat16)
 
 
 def attend(
-    info, queries, key_states, value_states, queries_in, pairs_in, near, gate, other_gate, first,
-    heads, place, group_heads, filled,
+    info, queries, key_states, value_states, queries_in, pairs_in, near, gate, other_gate,
+    latents, first, heads, place, group_heads, filled,
 ):
     rows = queries.shape[1]
     keys = 2 * rows + TAIL
     local = pl.BlockSpec((1, rows, HEAD_DIM), lambda h, info: (0, 0, info[1] + first + h))
     last = queries_in[0].shape[0] - 1
     operands = [info, queries, key_states, value_states, *queries_in, *pairs_in, near]
-    operands += [gate, other_gate]
+    operands += [gate, other_gate, latents]
     in_specs = [local, local, local]
     in_specs += [pl.BlockSpec((1, rows, HEAD_DIM), lambda h, info: (last, 0, h))] * 3
     in_specs += [pl.BlockSpec((2, rows, HEAD_DIM), lambda h, info: (0, 0, h))] * 3
     in_specs.append(pl.BlockSpec((4, TAIL, HEAD_DIM), lambda h, info: (0, 0, h)))
     in_specs.append(pl.BlockSpec((1, HEAD_DIM), lambda h, info: (0, info[1] + first + h)))
     in_specs.append(pl.BlockSpec((1, HEAD_DIM), lambda h, info: (0, first + h)))
+    in_specs.append(pl.BlockSpec((rows, HEAD_DIM), lambda h, info: (0, info[1] + first + h)))
     aliases = {}
     if filled is not None:
         aliases = {len(operands): 0}
@@ -244,67 +245,78 @@
     )(*operands)
 
 
-def tail_rows(gated, latents, far, seq, first, width, base):
+def tail_rows(summed, far, seq):
     cut = far.shape[0] - TAIL
-    added = lax.dynamic_slice(gated, (1 - seq, cut, 0), (1, TAIL, width))[0]
-    near = lax.dynamic_slice(latents, (cut, base + first * HEAD_DIM), (TAIL, width))
-    latent = jnp.where(seq == 1, near, far[cut:])
-    return (latent.astype(jnp.float32) + added.astype(jnp.float32)).astype(jnp.bfloat16)
-
-
-def finish_kernel(info_ref, picks_ref, gated_ref, near_ref, far_ref, tail_ref, *rest):
+    mine = lax.dynamic_slice(summed, (1 - seq, cut, 0), (1, TAIL, far.shape[1]))[0]
+    whole = mine.astype(jnp.float32) + far[cut:].astype(jnp.float32)
+    return jnp.where(seq == 1, mine, whole.astype(jnp.bfloat16))
+
+
+def finish_kernel(steps, info_ref, *rest):
     out_ref = rest[-1]
-    seq = info_ref[3]
-    for half, ref in enumerate((near_ref, far_ref)):
-        whole = ref[...].astype(jnp.float32) + gated_ref[half].astype(jnp.float32)
-        out_ref[seq if half == 0 else 1 - seq] = whole.astype(jnp.bfloat16)
-    shared = info_ref[4]
-    for frame in range(BF):
-        source = jnp.clip(BF - shared + frame, 0, BF - 1)
-        weight = (picks_ref[frame].astype(jnp.float32) + 0.5) / WEIGHTS
-        begin = pl.multiple_of(source * TOK_FRAME, TOK_FRAME)
-        place = pl.ds(frame * TOK_FRAME, TOK_FRAME)
-
-        @pl.when(frame < shared)
-        def _():
-            before = tail_ref[pl.ds(begin, TOK_FRAME), :].astype(jnp.float32)
-            lead = out_ref[0, place, :].astype(jnp.float32)
-            mixed = weight * lead + (1.0 - weight) * before
-            out_ref[0, place, :] = mixed.astype(jnp.bfloat16)
-
-
-def finish(info, picks, gated, latents, far, tail, first, heads, second):
-    rows = gated.shape[1]
+    seq, shared = info_ref[3], info_ref[4]
+
+    def fill(summed_ref, far_ref, tail_ref):
+        out_ref[seq] = summed_ref[0]
+        whole = far_ref[...].astype(jnp.float32) + summed_ref[1].astype(jnp.float32)
+        out_ref[1 - seq] = whole.astype(jnp.bfloat16)
+        for frame in range(BF):
+            source = jnp.clip(BF - shared + frame, 0, BF - 1)
+            weight = (info_ref[5 + frame].astype(jnp.float32) + 0.5) / WEIGHTS
+            begin = pl.multiple_of(source * TOK_FRAME, TOK_FRAME)
+            place = pl.ds(frame * TOK_FRAME, TOK_FRAME)
+
+            @pl.when(frame < shared)
+            def _():
+                before = tail_ref[pl.ds(begin, TOK_FRAME), :].astype(jnp.float32)
+                lead = out_ref[0, place, :].astype(jnp.float32)
+                mixed = weight * lead + (1.0 - weight) * before
+                out_ref[0, place, :] = mixed.astype(jnp.bfloat16)
+
+    step = pl.program_id(0)
+    begin = 0
+    for part, count in enumerate(steps):
+        refs = rest[3 * part : 3 * part + 3]
+        if len(steps) == 1:
+            fill(*refs)
+        else:
+            pl.when((step >= begin) & (step < begin + count))(functools.partial(fill, *refs))
+        begin += count
+
+
+def finish(info, parts, first, second):
+    rows = parts[0][0].shape[1]
     width = 2 * HEAD_DIM
-    here = lambda h, info, picks: (0, info[1] // 2 + first // 2 + h)
-    part = lambda h, info, picks: (0, h)
-    operands = [info, picks, gated, latents, far, tail]
-    in_specs = [
-        pl.BlockSpec((2, rows, width), lambda h, info, picks: (0, 0, h)),
-        pl.BlockSpec((rows, width), here),
-        pl.BlockSpec((rows, width), part),
-        pl.BlockSpec((TAIL, width), part),
-    ]
+    steps = tuple(part[0].shape[2] // width for part in parts)
+    operands, in_specs = [info], []
+    begin = 0
+    for part, count in zip(parts, steps):
+        at = lambda h, begin=begin, count=count: jnp.clip(h - begin, 0, count - 1)
+        operands += part
+        in_specs += [
+            pl.BlockSpec((2, rows, width), lambda h, info, at=at: (0, 0, at(h))),
+            pl.BlockSpec((rows, width), lambda h, info, at=at: (0, at(h))),
+            pl.BlockSpec((TAIL, width), lambda h, info, at=at: (0, at(h))),
+        ]
+        begin += count
     aliases = {}
     if second is not None:
         aliases = {len(operands): 0}
         operands.append(second)
         in_specs.append(pl.BlockSpec(memory_space=pl.ANY))
     return pl.pallas_call(
-        finish_kernel,
+        functools.partial(finish_kernel, steps),
         grid_spec=pltpu.PrefetchScalarGridSpec(
-            num_scalar_prefetch=2,
-            grid=(heads // 2,),
+            num_scalar_prefetch=1,
+            grid=(begin,),
             in_specs=in_specs,
-            out_specs=pl.BlockSpec(
-                (2, rows, width), lambda h, info, picks: (0, 0, first // 2 + h)
-            ),
+            out_specs=pl.BlockSpec((2, rows, width), lambda h, info: (0, 0, first // 2 + h)),
         ),
         out_shape=jax.ShapeDtypeStruct((2, rows, QUARTER_HEADS * HEAD_DIM), jnp.bfloat16),
         input_output_aliases=aliases,
         cost_estimate=pl.CostEstimate(
-            flops=rows * heads * HEAD_DIM * 200,
-            bytes_accessed=rows * heads * HEAD_DIM * 18,
+            flops=rows * begin * width * 200,
+            bytes_accessed=rows * begin * width * 12,
             transcendentals=0,
         ),
         compiler_params=pltpu.CompilerParams(vmem_limit_bytes=VMEM_LIMIT),
@@ -324,11 +336,8 @@
     follows = span_pos > 0
     closed = jnp.where(follows, TAIL - TOK_FRAME * window[earlier], TAIL)
     shared = jnp.where(follows, intersection[earlier], 0)
-    info = jnp.stack(
-        [closed, spot(section, seq) * QUARTER_HEADS, section, seq, shared]
-    ).astype(jnp.int32)
-    picks = blend_index[earlier]
-    base = spot(section, seq) * quarter
+    info = jnp.stack([closed, spot(section, seq) * QUARTER_HEADS, section, seq, shared])
+    info = jnp.concatenate([info, blend_index[earlier]]).astype(jnp.int32)
     far_base = spot(1 - section, 1 - seq) * quarter
 
     chunks, groups = len(CHUNKS), len(GROUPS)
@@ -376,7 +385,7 @@
             near = to_next_span(near)
             filled = attend(
                 info, queries, key_states, value_states, queries_in[k], pairs_in[k], near,
-                gate_scales, other_gate, first, heads, first - group_first[g], group_heads[g], filled,
+                gate_scales, other_gate, latents, first, heads, first - group_first[g], group_heads[g], filled,
             )
         attended.append(filled)
 
@@ -385,19 +394,15 @@
         far = far_latents[g]
         if g:
             far, _ = lax.optimization_barrier((far, tails[-1]))
-        tail = tail_rows(
-            attended[g], latents, far, seq, group_first[g], group_heads[g] * HEAD_DIM, base
-        )
+        tail = tail_rows(attended[g], far, seq)
         tails.append(tail)
     arrived_tails = []
     for g in range(groups):
         arrived_tails.append(to_next_span(tails[g]))
     second = None
-    for g in range(groups):
-        second = finish(
-            info, picks, attended[g], latents, far_latents[g], arrived_tails[g],
-            group_first[g], group_heads[g], second,
-        )
+    for members in FINISHES:
+        parts = [(attended[g], far_latents[g], arrived_tails[g]) for g in members]
+        second = finish(info, parts, group_first[members[0]], second)
     return second.reshape(2 * rows, quarter)
 
 

time: 311 us -> 308 us (level)
  waiting for transfers between devices: 148 us -> 152 us
    convert_element_type x3 -> x0, other arithmetic: 6.64 us -> none  [tail_rows(): (latent.astype(jnp.float32) + added.astype(jnp.float32)).astype(jnp.bfloa...]
    select_n x0 -> x3, other arithmetic: none -> 6.09 us  [tail_rows(): return jnp.where(seq == 1, mine, whole.astype(jnp.bfloat16))]
    pallas_call x3 -> x2, Pallas kernels: 11 us -> 8.11 us  [finish(): pl.pallas_call(functools.partial(finish_kernel, steps), grid_spec=pltpu.P...]
  transfers between devices with their start and end apart: 29 -> 29, of which waited for: 7 -> 8; matrix products, arithmetic and copies ran while one was open for 5% -> 5% of each run, Pallas kernels for 29% -> 28%
where the time goes in v2:
time: 308 us; the launch traced here: 307 us
  waiting for transfers between devices  152 us (49%)
  Pallas kernels  92.7 us (30%)
  starting transfers between devices  45.9 us (15%)
  local copies, waits for them, and re-layouts  8.62 us (3%)
  other arithmetic  6.09 us (2%)
    ppermute x22, waiting for transfers between devices, to_partner(): return lax.ppermute(block, PAIR_AXES, pairs)  150 us
    pallas_call x4, Pallas kernels, attend(): pl.pallas_call(attend_kernel, grid_spec=pltpu.PrefetchScalarGridSpec(num_...  57.1 us
    ppermute x22, starting transfers between devices, to_partner(): return lax.ppermute(block, PAIR_AXES, pairs)  27.7 us
    ppermute x7, starting transfers between devices, to_next_span(): return lax.ppermute(block, 'span', [(i, i + 1) for i in range(length - 1)])  18.3 us
    pallas_call x7, Pallas kernels, pack(): pl.pallas_call(functools.partial(pack_kernel, width, start, dests, count)...  16.3 us
    pallas_call x4, Pallas kernels, near_rows(): pl.pallas_call(functools.partial(near_kernel, width, start), grid_spec=pl...  11.2 us
    pallas_call x2, Pallas kernels, finish(): pl.pallas_call(functools.partial(finish_kernel, steps), grid_spec=pltpu.P...  8.11 us
  transfers between devices with their start and end apart: 29, of which 8 were waited for; matrix products, arithmetic and copies ran while one was open for 5% of the time, Pallas kernels for 28%

profile of v2, /device:TPU:2, one launch (start us, length us, event | category | flops | bytes accessed | tf_op | source)
XLA Modules:
  0.0 306.9 jit_solution(2932657911623580228)
XLA Ops:
  0.0 2.6 pack.10
  2.6 4.0 %collective-permute-start.13 = (bf16[3,504,384]{2,1,0:T(8,128)(2,1)}, bf16[3,504,384]{2,1,0:T(8,128)(2,1)}, u32[]{:S(2)}, u32[]{:S(2)}) collective-permute-start(bf16[3,504,384]{2,1,0:T(8,128)(2,1)} %get-tuple-element.33), channel_id=1, source_target_pairs={{0,1},{1,0},{64,65},{65,64},{2,3},{3,2},{66,67},{67,66},{4,5},{5,4... | collective-permute-start | bytes 3483656 | tf_op jit(solution)/shard_map/ppermute | solution.py:34
  6.6 1.0 collective-permute-start.14
  7.6 2.0 pack.7
  9.5 1.2 collective-permute-start
  10.8 2.3 pack.8
  13.1 2.5 collective-permute-start.3
  17.3 57.5 %collective-permute-done.7.other_gate = f32[1,1280]{1,0:T(1,128)} collective-permute-done((f32[1,1280]{1,0:T(1,128)S(1)}, f32[1,1280]{1,0:T(1,128)}, u32[]{:S(2)}, u32[]{:S(2)}) %collective-permute-start.7) | collective-permute-done | bytes 5152 | tf_op jit(solution)/shard_map/ppermute | solution.py:34
  74.8 1.0 collective-permute-start.4
  75.8 2.1 pack.11
  78.6 3.1 pack.9
  82.1 7.5 %collective-permute-done.4.sec_ref.sec_kv = bf16[2,504,256]{2,1,0:T(8,128)(2,1)} collective-permute-done((bf16[2,504,256]{2,1,0:T(8,128)(2,1)}, bf16[2,504,256]{2,1,0:T(8,128)(2,1)}, u32[]{:S(2)}, u32[]{:S(2)}) %collective-permute-start.4) | collective-permute-done | bytes 516128 | tf_op jit(solution)/shard_map/ppermute | solution.py:34
  89.7 3.1 %collective-permute-start.9 = (bf16[3,504,384]{2,1,0:T(8,128)(2,1)}, bf16[3,504,384]{2,1,0:T(8,128)(2,1)}, u32[]{:S(2)}, u32[]{:S(2)}) collective-permute-start(bf16[3,504,384]{2,1,0:T(8,128)(2,1)} %get-tuple-element.30), channel_id=1, source_target_pairs={{0,1},{1,0},{64,65},{65,64},{2,3},{3,2},{66,67},{67,66},{4,5},{5,4... | collective-permute-start | bytes 3483656 | tf_op jit(solution)/shard_map/ppermute | solution.py:34
  93.5 2.4 pack.13
  95.9 12.0 %collective-permute-done.15.dia_ref.dia_q.dia_kv = bf16[3,504,384]{2,1,0:T(8,128)(2,1)} collective-permute-done((bf16[3,504,384]{2,1,0:T(8,128)(2,1)}, bf16[3,504,384]{2,1,0:T(8,128)(2,1)}, u32[]{:S(2)}, u32[]{:S(2)}) %collective-permute-start.15) | collective-permute-done | bytes 1161248 | tf_op jit(solution)/shard_map/ppermute | solution.py:34
  107.9 1.2 dynamic_slice.31
  109.1 1.2 dynamic_slice.30
  112.9 2.9 near.6
  115.8 61.7 %collective-permute-done.5.dia_ref.dia_kv = bf16[2,504,256]{2,1,0:T(8,128)(2,1)} collective-permute-done((bf16[2,504,256]{2,1,0:T(8,128)(2,1)}, bf16[2,504,256]{2,1,0:T(8,128)(2,1)}, u32[]{:S(2)}, u32[]{:S(2)}) %collective-permute-start.5) | collective-permute-done | bytes 516128 | tf_op jit(solution)/shard_map/ppermute | solution.py:34
  177.5 1.9 collective-permute-start.16
  179.4 2.8 near.4
  182.2 3.6 %collective-permute-start.6 = (bf16[4,480,256]{2,1,0:T(8,128)(2,1)}, bf16[4,480,256]{2,1,0:T(8,128)(2,1)}, u32[]{:S(2)}, u32[]{:S(2)}) collective-permute-start(bf16[4,480,256]{2,1,0:T(8,128)(2,1)} %near.4), channel_id=1, source_target_pairs={{0,2},{2,4},{4,6},{6,8},{8,10},{10,12},{12,14},{14,16},{16,18},{18... | collective-permute-start | bytes 2949128 | tf_op jit(solution)/shard_map/ppermute | solution.py:39
  186.7 2.8 near.5
  189.6 1.9 collective-permute-start.12
  191.5 8.4 %collective-permute-done.23.sec_ref.sec_kv = bf16[2,504,256]{2,1,0:T(8,128)(2,1)} collective-permute-done((bf16[2,504,256]{2,1,0:T(8,128)(2,1)}, bf16[2,504,256]{2,1,0:T(8,128)(2,1)}, u32[]{:S(2)}, u32[]{:S(2)}) %collective-permute-start.23) | collective-permute-done | bytes 516128 | tf_op jit(solution)/shard_map/ppermute | solution.py:34
  200.2 1.0 collective-permute-done.24.dia_ref.dia_kv
  201.9 2.0 pack.12
  203.9 1.9 constant_dynamic-slice_fusion
  205.8 2.1 constant_dynamic-slice_fusion.1
  207.9 2.7 near.7
  210.7 2.6 collective-permute-start.17
  214.8 12.0 %attend.4.rest_0_ = bf16[2,504,256]{2,1,0:T(8,128)(2,1)} custom-call(s32[15]{0:T(128)} %concatenate.3.info_ref, bf16[1,504,5120]{2,1,0:T(8,128)(2,1)} %q_ref.7, bf16[1,504,5120]{2,1,0:T(8,128)(2,1)} %k_ref.15, bf16[1,504,5120]{2,1,0:T(8,128)(2,1)} %v_ref.15, bf16[1,504,256]{2,1,0:T(8,128)(2,1)} %collective-permute-done.seq_q, ...), custom_call_target="tpu_custom_call" | custom-call | flops 3071803392 | bytes 5160960 | tf_op jit(solution)/shard_map/attend/pallas_call | solution.py:226
  226.9 2.1 collective-permute-start.25
  229.0 16.5 %attend.5.rest_0_ = bf16[2,504,768]{2,1,0:T(8,128)(2,1)} custom-call(s32[15]{0:T(128)} %concatenate.3.info_ref, bf16[1,504,5120]{2,1,0:T(8,128)(2,1)} %q_ref.7, bf16[1,504,5120]{2,1,0:T(8,128)(2,1)} %k_ref.15, bf16[1,504,5120]{2,1,0:T(8,128)(2,1)} %v_ref.15, bf16[3,504,384]{2,1,0:T(8,128)(2,1)} %collective-permute-done.13.seq_ref.seq_q.seq_kv, ...), custom_call_target="tpu_custom_call" | custom-call | flops 4607705088 | bytes 7741440 | tf_op jit(solution)/shard_map/attend/pallas_call | solution.py:226
  245.5 2.6 collective-permute-start.20
  248.1 16.5 %attend.6.rest_0_ = bf16[2,504,768]{2,1,0:T(8,128)(2,1)} custom-call(s32[15]{0:T(128)} %concatenate.3.info_ref, bf16[1,504,5120]{2,1,0:T(8,128)(2,1)} %q_ref.7, bf16[1,504,5120]{2,1,0:T(8,128)(2,1)} %k_ref.15, bf16[1,504,5120]{2,1,0:T(8,128)(2,1)} %v_ref.15, ...), custom_call_target="tpu_custom_call", output_to_operand_aliasing={{}: (14, {})} | custom-call | flops 4607705088 | bytes 7741440 | tf_op jit(solution)/shard_map/attend/pallas_call | solution.py:226
  265.4 2.4 fusion
  267.8 2.5 collective-permute-start.26
  270.4 3.0 collective-permute-start.28
  273.4 1.6 collective-permute-done.21.dia_q
  274.9 12.1 %attend.7.rest_3_ = bf16[2,504,256]{2,1,0:T(8,128)(2,1)} custom-call(s32[15]{0:T(128)} %concatenate.3.info_ref, bf16[1,504,5120]{2,1,0:T(8,128)(2,1)} %q_ref.7, bf16[1,504,5120]{2,1,0:T(8,128)(2,1)} %k_ref.15, bf16[1,504,5120]{2,1,0:T(8,128)(2,1)} %v_ref.15, bf16[1,504,256]{2,1,0:T(8,128)(2,1)} %collective-permute-done.19.seq_q, ...), custom_call_target="tpu_custom_call" | custom-call | flops 3071803392 | bytes 5160960 | tf_op jit(solution)/shard_map/attend/pallas_call | solution.py:226
  287.0 1.8 fusion.1
  288.8 1.8 fusion.2
  290.6 2.9 collective-permute-start.27
  293.5 2.9 collective-permute-start.18
  296.5 4.7 %finish.2.rest_6_ = bf16[2,504,1280]{2,1,0:T(8,128)(2,1)} custom-call(s32[15]{0:T(128)} %concatenate.3.info_ref, bf16[2,504,768]{2,1,0:T(8,128)(2,1)} %attend.6.rest_0_, bf16[504,768]{1,0:T(8,128)(2,1)} %collective-permute-done.17.rest_1_, bf16[480,768]{1,0:T(8,128)(2,1)} %collective-permute-done.28.rest_2_), custom_call_target="tpu_custom_call" | custom-call | flops 77414400 | bytes 4644864 | tf_op jit(solution)/shard_map/finish/pallas_call | solution.py:307
  301.2 2.3 collective-permute-done.18.rest_2_
  303.5 3.4 %finish.3 = bf16[2,504,1280]{2,1,0:T(8,128)(2,1)} custom-call(s32[15]{0:T(128)} %concatenate.3.info_ref, bf16[2,504,256]{2,1,0:T(8,128)(2,1)} %attend.4.rest_0_, bf16[504,256]{1,0:T(8,128)(2,1)} %collective-permute-done.8.rest_1_, bf16[480,256]{1,0:T(8,128)(2,1)} %collective-permute-done.18.rest_2_, ...), custom_call_target="tpu_custom_call", output_to_operand_aliasing={{}: (7, {})} | custom-call | flops 51609600 | bytes 3096576 | tf_op jit(solution)/shard_map/finish/pallas_call | solution.py:307
  (37 shorter events, 9.4 us)
Async XLA Ops:
  2.6 87.1 %collective-permute-start.13 = (bf16[3,504,384]{2,1,0:T(8,128)(2,1)}, bf16[3,504,384]{2,1,0:T(8,128)(2,1)}, u32[]{:S(2)}, u32[]{:S(2)}) collective-permute-start(bf16[3,504,384]{2,1,0:T(8,128)(2,1)} %get-tuple-element.33), channel_id=1, source_target_pairs={{0,1},{1,0},{64,65},{65,64},{2,3},{3,2},{66,67},{67,66},{4,5},{5,4... | collective-permute-start | bytes 3483656 | tf_op jit(solution)/shard_map/ppermute | solution.py:34
  6.6 86.2 %collective-permute-start.14 = (bf16[3,504,384]{2,1,0:T(8,128)(2,1)}, bf16[3,504,384]{2,1,0:T(8,128)(2,1)}, u32[]{:S(2)}, u32[]{:S(2)}) collective-permute-start(bf16[3,504,384]{2,1,0:T(8,128)(2,1)} %get-tuple-element.34), channel_id=1, source_target_pairs={{0,64},{1,65},{64,0},{65,1},{2,66},{3,67},{66,2},{67,3},{4,68},{5,... | collective-permute-start | bytes 3483656 | tf_op jit(solution)/shard_map/ppermute | solution.py:34
  9.5 68.3 %collective-permute-start = (bf16[1,504,256]{2,1,0:T(8,128)(2,1)}, bf16[1,504,256]{2,1,0:T(8,128)(2,1)}, u32[]{:S(2)}, u32[]{:S(2)}) collective-permute-start(bf16[1,504,256]{2,1,0:T(8,128)(2,1)} %get-tuple-element.24), channel_id=1, source_target_pairs={{0,1},{1,0},{64,65},{65,64},{2,3},{3,2},{66,67},{67,66},{4,5},{5,4... | collective-permute-start | bytes 774152 | tf_op jit(solution)/shard_map/ppermute | solution.py:34
  13.1 68.6 %collective-permute-start.3 = (bf16[2,504,256]{2,1,0:T(8,128)(2,1)}, bf16[2,504,256]{2,1,0:T(8,128)(2,1)}, u32[]{:S(2)}, u32[]{:S(2)}) collective-permute-start(bf16[2,504,256]{2,1,0:T(8,128)(2,1)} %get-tuple-element.27), channel_id=1, source_target_pairs={{0,1},{1,0},{64,65},{65,64},{2,3},{3,2},{66,67},{67,66},{4,5},{5,4... | collective-permute-start | bytes 1548296 | tf_op jit(solution)/shard_map/ppermute | solution.py:34
  16.3 58.5 %collective-permute-start.7 = (f32[1,1280]{1,0:T(1,128)S(1)}, f32[1,1280]{1,0:T(1,128)}, u32[]{:S(2)}, u32[]{:S(2)}) collective-permute-start(f32[1,1280]{1,0:T(1,128)S(1)} %constant_dynamic-slice_fusion.3), channel_id=1, source_target_pairs={{0,64},{1,65},{64,0},{65,1},{2,66},{3,67},{66,2},{67,3},{4,68},{5,... | collective-permute-start | bytes 15368 | tf_op jit(solution)/shard_map/ppermute | solution.py:34
  74.8 14.9 %collective-permute-start.4 = (bf16[2,504,256]{2,1,0:T(8,128)(2,1)}, bf16[2,504,256]{2,1,0:T(8,128)(2,1)}, u32[]{:S(2)}, u32[]{:S(2)}) collective-permute-start(bf16[2,504,256]{2,1,0:T(8,128)(2,1)} %get-tuple-element.28), channel_id=1, source_target_pairs={{0,64},{1,65},{64,0},{65,1},{2,66},{3,67},{66,2},{67,3},{4,68},{5,... | collective-permute-start | bytes 1548296 | tf_op jit(solution)/shard_map/ppermute | solution.py:34
  77.8 30.0 %collective-permute-start.15 = (bf16[3,504,384]{2,1,0:T(8,128)(2,1)}, bf16[3,504,384]{2,1,0:T(8,128)(2,1)}, u32[]{:S(2)}, u32[]{:S(2)}) collective-permute-start(bf16[3,504,384]{2,1,0:T(8,128)(2,1)} %pack.11), channel_id=1, source_target_pairs={{0,65},{1,64},{64,1},{65,0},{2,67},{3,66},{66,3},{67,2},{4,69},{5,... | collective-permute-start | bytes 3483656 | tf_op jit(solution)/shard_map/ppermute | solution.py:34
  81.7 100.5 %collective-permute-start.10 = (bf16[3,504,384]{2,1,0:T(8,128)(2,1)}, bf16[3,504,384]{2,1,0:T(8,128)(2,1)}, u32[]{:S(2)}, u32[]{:S(2)}) collective-permute-start(bf16[3,504,384]{2,1,0:T(8,128)(2,1)} %get-tuple-element.31), channel_id=1, source_target_pairs={{0,64},{1,65},{64,0},{65,1},{2,66},{3,67},{66,2},{67,3},{4,68},{5,... | collective-permute-start | bytes 3483656 | tf_op jit(solution)/shard_map/ppermute | solution.py:34
  89.7 96.1 %collective-permute-start.11 = (bf16[3,504,384]{2,1,0:T(8,128)(2,1)}, bf16[3,504,384]{2,1,0:T(8,128)(2,1)}, u32[]{:S(2)}, u32[]{:S(2)}) collective-permute-start(bf16[3,504,384]{2,1,0:T(8,128)(2,1)} %get-tuple-element.32), channel_id=1, source_target_pairs={{0,65},{1,64},{64,1},{65,0},{2,67},{3,66},{66,3},{67,2},{4,69},{5,... | collective-permute-start | bytes 3483656 | tf_op jit(solution)/shard_map/ppermute | solution.py:34
  89.7 96.2 %collective-permute-start.9 = (bf16[3,504,384]{2,1,0:T(8,128)(2,1)}, bf16[3,504,384]{2,1,0:T(8,128)(2,1)}, u32[]{:S(2)}, u32[]{:S(2)}) collective-permute-start(bf16[3,504,384]{2,1,0:T(8,128)(2,1)} %get-tuple-element.30), channel_id=1, source_target_pairs={{0,1},{1,0},{64,65},{65,64},{2,3},{3,2},{66,67},{67,66},{4,5},{5,4... | collective-permute-start | bytes 3483656 | tf_op jit(solution)/shard_map/ppermute | solution.py:34
  92.8 84.7 %collective-permute-start.5 = (bf16[2,504,256]{2,1,0:T(8,128)(2,1)}, bf16[2,504,256]{2,1,0:T(8,128)(2,1)}, u32[]{:S(2)}, u32[]{:S(2)}) collective-permute-start(bf16[2,504,256]{2,1,0:T(8,128)(2,1)} %get-tuple-element.29), channel_id=1, source_target_pairs={{0,65},{1,64},{64,1},{65,0},{2,67},{3,66},{66,3},{67,2},{4,69},{5,... | collective-permute-start | bytes 1548296 | tf_op jit(solution)/shard_map/ppermute | solution.py:34
  107.9 81.7 %collective-permute-start.22 = (bf16[2,504,256]{2,1,0:T(8,128)(2,1)}, bf16[2,504,256]{2,1,0:T(8,128)(2,1)}, u32[]{:S(2)}, u32[]{:S(2)}) collective-permute-start(bf16[2,504,256]{2,1,0:T(8,128)(2,1)} %get-tuple-element.39), channel_id=1, source_target_pairs={{0,1},{1,0},{64,65},{65,64},{2,3},{3,2},{66,67},{67,66},{4,5},{5,4... | collective-permute-start | bytes 1548296 | tf_op jit(solution)/shard_map/ppermute | solution.py:34
  177.5 49.3 %collective-permute-start.16 = (bf16[4,480,384]{2,1,0:T(8,128)(2,1)}, bf16[4,480,384]{2,1,0:T(8,128)(2,1)}, u32[]{:S(2)}, u32[]{:S(2)}) collective-permute-start(bf16[4,480,384]{2,1,0:T(8,128)(2,1)} %near.6), channel_id=1, source_target_pairs={{0,2},{2,4},{4,6},{6,8},{8,10},{10,12},{12,14},{14,16},{16,18},{18... | collective-permute-start | bytes 4423688 | tf_op jit(solution)/shard_map/ppermute | solution.py:39
  182.2 31.8 %collective-permute-start.6 = (bf16[4,480,256]{2,1,0:T(8,128)(2,1)}, bf16[4,480,256]{2,1,0:T(8,128)(2,1)}, u32[]{:S(2)}, u32[]{:S(2)}) collective-permute-start(bf16[4,480,256]{2,1,0:T(8,128)(2,1)} %near.4), channel_id=1, source_target_pairs={{0,2},{2,4},{4,6},{6,8},{8,10},{10,12},{12,14},{14,16},{16,18},{18... | collective-permute-start | bytes 2949128 | tf_op jit(solution)/shard_map/ppermute | solution.py:39
  185.8 14.1 %collective-permute-start.23 = (bf16[2,504,256]{2,1,0:T(8,128)(2,1)}, bf16[2,504,256]{2,1,0:T(8,128)(2,1)}, u32[]{:S(2)}, u32[]{:S(2)}) collective-permute-start(bf16[2,504,256]{2,1,0:T(8,128)(2,1)} %get-tuple-element.40), channel_id=1, source_target_pairs={{0,64},{1,65},{64,0},{65,1},{2,66},{3,67},{66,2},{67,3},{4,68},{5,... | collective-permute-start | bytes 1548296 | tf_op jit(solution)/shard_map/ppermute | solution.py:34
  185.9 15.3 %collective-permute-start.24 = (bf16[2,504,256]{2,1,0:T(8,128)(2,1)}, bf16[2,504,256]{2,1,0:T(8,128)(2,1)}, u32[]{:S(2)}, u32[]{:S(2)}) collective-permute-start(bf16[2,504,256]{2,1,0:T(8,128)(2,1)} %get-tuple-element.41), channel_id=1, source_target_pairs={{0,65},{1,64},{64,1},{65,0},{2,67},{3,66},{66,3},{67,2},{4,69},{5,... | collective-permute-start | bytes 1548296 | tf_op jit(solution)/shard_map/ppermute | solution.py:34
  189.6 55.9 %collective-permute-start.12 = (bf16[4,480,384]{2,1,0:T(8,128)(2,1)}, bf16[4,480,384]{2,1,0:T(8,128)(2,1)}, u32[]{:S(2)}, u32[]{:S(2)}) collective-permute-start(bf16[4,480,384]{2,1,0:T(8,128)(2,1)} %near.5), channel_id=1, source_target_pairs={{0,2},{2,4},{4,6},{6,8},{8,10},{10,12},{12,14},{14,16},{16,18},{18... | collective-permute-start | bytes 4423688 | tf_op jit(solution)/shard_map/ppermute | solution.py:39
  199.9 10.8 %collective-permute-start.1 = (bf16[1,504,256]{2,1,0:T(8,128)(2,1)}, bf16[1,504,256]{2,1,0:T(8,128)(2,1)}, u32[]{:S(2)}, u32[]{:S(2)}) collective-permute-start(bf16[1,504,256]{2,1,0:T(8,128)(2,1)} %get-tuple-element.25), channel_id=1, source_target_pairs={{0,64},{1,65},{64,0},{65,1},{2,66},{3,67},{66,2},{67,3},{4,68},{5,... | collective-permute-start | bytes 774152 | tf_op jit(solution)/shard_map/ppermute | solution.py:34
  201.2 12.1 %collective-permute-start.2 = (bf16[1,504,256]{2,1,0:T(8,128)(2,1)}, bf16[1,504,256]{2,1,0:T(8,128)(2,1)}, u32[]{:S(2)}, u32[]{:S(2)}) collective-permute-start(bf16[1,504,256]{2,1,0:T(8,128)(2,1)} %get-tuple-element.26), channel_id=1, source_target_pairs={{0,65},{1,64},{64,1},{65,0},{2,67},{3,66},{66,3},{67,2},{4,69},{5,... | collective-permute-start | bytes 774152 | tf_op jit(solution)/shard_map/ppermute | solution.py:34
  210.7 54.0 %collective-permute-start.17 = (bf16[504,768]{1,0:T(8,128)(2,1)}, bf16[504,768]{1,0:T(8,128)(2,1)}, u32[]{:S(2)}, u32[]{:S(2)}) collective-permute-start(bf16[504,768]{1,0:T(8,128)(2,1)} %constant_dynamic-slice_fusion.1), channel_id=1, source_target_pairs={{0,65},{1,64},{64,1},{65,0},{2,67},{3,66},{66,3},{67,2},{4,69},{5,... | collective-permute-start | bytes 2322440 | tf_op jit(solution)/shard_map/ppermute | solution.py:34
  213.3 73.7 %collective-permute-start.8 = (bf16[504,256]{1,0:T(8,128)(2,1)}, bf16[504,256]{1,0:T(8,128)(2,1)}, u32[]{:S(2)}, u32[]{:S(2)}) collective-permute-start(bf16[504,256]{1,0:T(8,128)(2,1)} %get-tuple-element.44), channel_id=1, source_target_pairs={{0,65},{1,64},{64,1},{65,0},{2,67},{3,66},{66,3},{67,2},{4,69},{5,... | collective-permute-start | bytes 774152 | tf_op jit(solution)/shard_map/ppermute | solution.py:34
  214.0 53.9 %collective-permute-start.19 = (bf16[1,504,256]{2,1,0:T(8,128)(2,1)}, bf16[1,504,256]{2,1,0:T(8,128)(2,1)}, u32[]{:S(2)}, u32[]{:S(2)}) collective-permute-start(bf16[1,504,256]{2,1,0:T(8,128)(2,1)} %get-tuple-element.36), channel_id=1, source_target_pairs={{0,1},{1,0},{64,65},{65,64},{2,3},{3,2},{66,67},{67,66},{4,5},{5,4... | collective-permute-start | bytes 774152 | tf_op jit(solution)/shard_map/ppermute | solution.py:34
  226.9 48.0 %collective-permute-start.25 = (bf16[4,480,256]{2,1,0:T(8,128)(2,1)}, bf16[4,480,256]{2,1,0:T(8,128)(2,1)}, u32[]{:S(2)}, u32[]{:S(2)}) collective-permute-start(bf16[4,480,256]{2,1,0:T(8,128)(2,1)} %near.7), channel_id=1, source_target_pairs={{0,2},{2,4},{4,6},{6,8},{8,10},{10,12},{12,14},{14,16},{16,18},{18... | collective-permute-start | bytes 2949128 | tf_op jit(solution)/shard_map/ppermute | solution.py:39
  245.5 24.9 %collective-permute-start.20 = (bf16[1,504,256]{2,1,0:T(8,128)(2,1)}, bf16[1,504,256]{2,1,0:T(8,128)(2,1)}, u32[]{:S(2)}, u32[]{:S(2)}) collective-permute-start(bf16[1,504,256]{2,1,0:T(8,128)(2,1)} %get-tuple-element.37), channel_id=1, source_target_pairs={{0,64},{1,65},{64,0},{65,1},{2,66},{3,67},{66,2},{67,3},{4,68},{5,... | collective-permute-start | bytes 774152 | tf_op jit(solution)/shard_map/ppermute | solution.py:34
  264.6 10.3 %collective-permute-start.21 = (bf16[1,504,256]{2,1,0:T(8,128)(2,1)}, bf16[1,504,256]{2,1,0:T(8,128)(2,1)}, u32[]{:S(2)}, u32[]{:S(2)}) collective-permute-start(bf16[1,504,256]{2,1,0:T(8,128)(2,1)} %get-tuple-element.38), channel_id=1, source_target_pairs={{0,65},{1,64},{64,1},{65,0},{2,67},{3,66},{66,3},{67,2},{4,69},{5,... | collective-permute-start | bytes 774152 | tf_op jit(solution)/shard_map/ppermute | solution.py:34
  267.8 21.0 %collective-permute-start.26 = (bf16[504,256]{1,0:T(8,128)(2,1)}, bf16[504,256]{1,0:T(8,128)(2,1)}, u32[]{:S(2)}, u32[]{:S(2)}) collective-permute-start(bf16[504,256]{1,0:T(8,128)(2,1)} %get-tuple-element.43), channel_id=1, source_target_pairs={{0,65},{1,64},{64,1},{65,0},{2,67},{3,66},{66,3},{67,2},{4,69},{5,... | collective-permute-start | bytes 774152 | tf_op jit(solution)/shard_map/ppermute | solution.py:34
  270.4 26.1 %collective-permute-start.28 = (bf16[480,768]{1,0:T(8,128)(2,1)}, bf16[480,768]{1,0:T(8,128)(2,1)}, u32[]{:S(2)}, u32[]{:S(2)}) collective-permute-start(bf16[480,768]{1,0:T(8,128)(2,1)} %fusion), channel_id=1, source_target_pairs={{0,2},{2,4},{4,6},{6,8},{8,10},{10,12},{12,14},{14,16},{16,18},{18... | collective-permute-start | bytes 2211848 | tf_op jit(solution)/shard_map/ppermute | solution.py:39
  290.6 10.5 %collective-permute-start.27 = (bf16[480,256]{1,0:T(8,128)(2,1)}, bf16[480,256]{1,0:T(8,128)(2,1)}, u32[]{:S(2)}, u32[]{:S(2)}) collective-permute-start(bf16[480,256]{1,0:T(8,128)(2,1)} %fusion.2), channel_id=1, source_target_pairs={{0,2},{2,4},{4,6},{6,8},{8,10},{10,12},{12,14},{14,16},{16,18},{18... | collective-permute-start | bytes 737288 | tf_op jit(solution)/shard_map/ppermute | solution.py:39
  293.5 9.9 %collective-permute-start.18 = (bf16[480,256]{1,0:T(8,128)(2,1)}, bf16[480,256]{1,0:T(8,128)(2,1)}, u32[]{:S(2)}, u32[]{:S(2)}) collective-permute-start(bf16[480,256]{1,0:T(8,128)(2,1)} %fusion.1), channel_id=1, source_target_pairs={{0,2},{2,4},{4,6},{6,8},{8,10},{10,12},{12,14},{14,16},{16,18},{18... | collective-permute-start | bytes 737288 | tf_op jit(solution)/shard_map/ppermute | solution.py:39

commit v3 on v2

--- a/solution.py
+++ b/solution.py
@@ -18,6 +18,7 @@
 CHUNKS = (3, 3, 2, 2)
 GROUPS = ((0, 1), (2,), (3,))
 FINISHES = ((0,), (1, 2))
+FINISH_HEADS = {1: 3, 2: 2}
 SENDS = (("z", 0), ("z", 1), ("kv", 2), ("kv", 3), ("q", 2), ("q", 3))
 VMEM_LIMIT = 66000 * 1024
 PAIR_AXES = ("section", "seq")
@@ -145,7 +146,7 @@
     info_ref, q_ref, k_ref, v_ref, seq_q, sec_q, dia_q, seq_kv, sec_kv, dia_kv, near_ref,
     own_gate, other_gate, latent_ref, *rest
 ):
-    out_ref, qs, ks, vs = rest[-4:]
+    out_ref, vs = rest[-2:]
     rows = q_ref.shape[1]
 
     @pl.when(pl.program_id(0) == 0)
@@ -154,12 +155,10 @@
         for slot in range(6):
             vs[slot, :, HEAD_DIM:] = (lane == 0).astype(jnp.bfloat16)
 
-    qs[0] = q_ref[0]
-    ks[0] = k_ref[0]
+    queries = (q_ref, seq_q, sec_q, dia_q)
+    keys_of = (k_ref, seq_kv, sec_kv, dia_kv)
     vs[0, :, :HEAD_DIM] = v_ref[0]
-    for slot, q_in, kv_in in ((1, seq_q, seq_kv), (2, sec_q, sec_kv), (3, dia_q, dia_kv)):
-        qs[slot] = q_in[0]
-        ks[slot] = kv_in[0]
+    for slot, kv_in in ((1, seq_kv), (2, sec_kv), (3, dia_kv)):
         vs[slot, :, :HEAD_DIM] = kv_in[1]
     vs[4, :TAIL, :HEAD_DIM] = near_ref[1]
     vs[5, :TAIL, :HEAD_DIM] = near_ref[3]
@@ -169,11 +168,11 @@
 
     gated = [None, None]
     for layer, gate_ref in enumerate((own_gate, other_gate)):
-        keys = (ks[2 * layer], ks[2 * layer + 1], near_ref[2 * layer])
+        keys = (keys_of[2 * layer][0], keys_of[2 * layer + 1][0], near_ref[2 * layer])
         values = (vs[2 * layer], vs[2 * layer + 1], vs[4 + layer, :TAIL])
         scores = []
         for half in range(2):
-            query = qs[2 * layer + half]
+            query = queries[2 * layer + half][0]
             parts = [
                 lax.dot_general(
                     query, key, (((1,), (1,)), ((), ())), preferred_element_type=jnp.float32
@@ -230,8 +229,7 @@
             grid=(heads,),
             in_specs=in_specs,
             out_specs=pl.BlockSpec((2, rows, HEAD_DIM), lambda h, info: (0, 0, place + h)),
-            scratch_shapes=[pltpu.VMEM((4, rows, HEAD_DIM), jnp.bfloat16)] * 2
-            + [pltpu.VMEM((6, rows, 2 * HEAD_DIM), jnp.bfloat16)],
+            scratch_shapes=[pltpu.VMEM((6, rows, 2 * HEAD_DIM), jnp.bfloat16)],
         ),
         out_shape=jax.ShapeDtypeStruct((2, rows, group_heads * HEAD_DIM), jnp.bfloat16),
         input_output_aliases=aliases,
@@ -240,7 +238,7 @@
             bytes_accessed=heads * HEAD_DIM * rows * 40,
             transcendentals=heads * 4 * rows * keys,
         ),
-        compiler_params=pltpu.CompilerParams(vmem_limit_bytes=VMEM_LIMIT),
+        compiler_params=pltpu.CompilerParams(vmem_limit_bytes=VMEM_LIMIT if first + heads < QUARTER_HEADS else 62 * 1024 * 1024),
         name="attend",
     )(*operands)
 
@@ -286,7 +284,7 @@
 
 def finish(info, parts, first, second):
     rows = parts[0][0].shape[1]
-    width = 2 * HEAD_DIM
+    width = FINISH_HEADS[len(parts)] * HEAD_DIM
     steps = tuple(part[0].shape[2] // width for part in parts)
     operands, in_specs = [info], []
     begin = 0
@@ -310,7 +308,9 @@
             num_scalar_prefetch=1,
             grid=(begin,),
             in_specs=in_specs,
-            out_specs=pl.BlockSpec((2, rows, width), lambda h, info: (0, 0, first // 2 + h)),
+            out_specs=pl.BlockSpec(
+                (2, rows, width), lambda h, info: (0, 0, first * HEAD_DIM // width + h)
+            ),
         ),
         out_shape=jax.ShapeDtypeStruct((2, rows, QUARTER_HEADS * HEAD_DIM), jnp.bfloat16),
         input_output_aliases=aliases,
@@ -319,7 +319,7 @@
             bytes_accessed=rows * begin * width * 12,
             transcendentals=0,
         ),
-        compiler_params=pltpu.CompilerParams(vmem_limit_bytes=VMEM_LIMIT),
+        compiler_params=pltpu.CompilerParams(vmem_limit_bytes=24 * 1024 * 1024),
         name="finish",
     )(*operands)
 

time: 308 us -> 306 us (level)
  transfers between devices with their start and end apart: 29 -> 29, of which waited for: 8 -> 9; matrix products, arithmetic and copies ran while one was open for 5% -> 4% of each run, Pallas kernels for 28% -> 28%
where the time goes in v3:
time: 306 us; the launch traced here: 305 us
  waiting for transfers between devices  153 us (50%)
  Pallas kernels  90.1 us (29%)
  starting transfers between devices  46.1 us (15%)
  local copies, waits for them, and re-layouts  9.43 us (3%)
  other arithmetic  4.59 us (2%)
    ppermute x22, waiting for transfers between devices, to_partner(): return lax.ppermute(block, PAIR_AXES, pairs)  149 us
    pallas_call x4, Pallas kernels, attend(): pl.pallas_call(attend_kernel, grid_spec=pltpu.PrefetchScalarGridSpec(num_...  56.6 us
    ppermute x22, starting transfers between devices, to_partner(): return lax.ppermute(block, PAIR_AXES, pairs)  27.7 us
    ppermute x7, starting transfers between devices, to_next_span(): return lax.ppermute(block, 'span', [(i, i + 1) for i in range(length - 1)])  18.4 us
    pallas_call x7, Pallas kernels, pack(): pl.pallas_call(functools.partial(pack_kernel, width, start, dests, count)...  16.2 us
    pallas_call x4, Pallas kernels, near_rows(): pl.pallas_call(functools.partial(near_kernel, width, start), grid_spec=pl...  11.2 us
  transfers between devices with their start and end apart: 29, of which 9 were waited for; matrix products, arithmetic and copies ran while one was open for 4% of the time, Pallas kernels for 28%

profile of v3, /device:TPU:2, one launch (start us, length us, event | category | flops | bytes accessed | tf_op | source)
XLA Modules:
  0.0 304.6 jit_solution(9270860944881989577)
XLA Ops:
  0.0 2.5 pack.10
  2.5 4.0 %collective-permute-start.13 = (bf16[3,504,384]{2,1,0:T(8,128)(2,1)}, bf16[3,504,384]{2,1,0:T(8,128)(2,1)}, u32[]{:S(2)}, u32[]{:S(2)}) collective-permute-start(bf16[3,504,384]{2,1,0:T(8,128)(2,1)} %get-tuple-element.33), channel_id=1, source_target_pairs={{0,1},{1,0},{64,65},{65,64},{2,3},{3,2},{66,67},{67,66},{4,5},{5,4... | collective-permute-start | bytes 3483656 | tf_op jit(solution)/shard_map/ppermute | solution.py:35
  7.5 2.0 pack.7
  9.4 1.2 collective-permute-start
  10.7 2.4 pack.8
  13.0 2.5 collective-permute-start.3
  16.2 1.0 collective-permute-start.7
  17.2 57.4 %collective-permute-done.7.other_gate = f32[1,1280]{1,0:T(1,128)} collective-permute-done((f32[1,1280]{1,0:T(1,128)S(1)}, f32[1,1280]{1,0:T(1,128)}, u32[]{:S(2)}, u32[]{:S(2)}) %collective-permute-start.7) | collective-permute-done | bytes 5152 | tf_op jit(solution)/shard_map/ppermute | solution.py:35
  74.7 1.0 collective-permute-start.4
  75.7 2.0 pack.11
  78.5 3.1 %pack.9 = (bf16[3,504,384]{2,1,0:T(8,128)(2,1)}, bf16[3,504,384]{2,1,0:T(8,128)(2,1)}, bf16[3,504,384]{2,1,0:T(8,128)(2,1)}) custom-call(bf16[1,504,5120]{2,1,0:T(8,128)(2,1)} %k_ref.15, bf16[1,504,5120]{2,1,0:T(8,128)(2,1)} %v_ref.15, bf16[1,504,5120]{2,1,0:T(8,128)(2,1)} %q_ref.7), custom_call_target="tpu_custom_call" | custom-call | flops 13934592 | bytes 6967296 | tf_op jit(solution)/shard_map/pack/pallas_call | solution.py:73
  82.0 7.6 %collective-permute-done.4.sec_ref.sec_kv = bf16[2,504,256]{2,1,0:T(8,128)(2,1)} collective-permute-done((bf16[2,504,256]{2,1,0:T(8,128)(2,1)}, bf16[2,504,256]{2,1,0:T(8,128)(2,1)}, u32[]{:S(2)}, u32[]{:S(2)}) %collective-permute-start.4) | collective-permute-done | bytes 516128 | tf_op jit(solution)/shard_map/ppermute | solution.py:35
  89.6 3.1 %collective-permute-start.9 = (bf16[3,504,384]{2,1,0:T(8,128)(2,1)}, bf16[3,504,384]{2,1,0:T(8,128)(2,1)}, u32[]{:S(2)}, u32[]{:S(2)}) collective-permute-start(bf16[3,504,384]{2,1,0:T(8,128)(2,1)} %get-tuple-element.30), channel_id=1, source_target_pairs={{0,1},{1,0},{64,65},{65,64},{2,3},{3,2},{66,67},{67,66},{4,5},{5,4... | collective-permute-start | bytes 3483656 | tf_op jit(solution)/shard_map/ppermute | solution.py:35
  93.4 2.4 pack.13
  95.8 12.0 %collective-permute-done.15.dia_ref.dia_q.dia_kv = bf16[3,504,384]{2,1,0:T(8,128)(2,1)} collective-permute-done((bf16[3,504,384]{2,1,0:T(8,128)(2,1)}, bf16[3,504,384]{2,1,0:T(8,128)(2,1)}, u32[]{:S(2)}, u32[]{:S(2)}) %collective-permute-start.15) | collective-permute-done | bytes 1161248 | tf_op jit(solution)/shard_map/ppermute | solution.py:35
  107.8 1.2 dynamic_slice.31
  109.0 1.2 dynamic_slice.30
  113.0 2.8 near.6
  115.9 61.6 %collective-permute-done.5.dia_ref.dia_kv = bf16[2,504,256]{2,1,0:T(8,128)(2,1)} collective-permute-done((bf16[2,504,256]{2,1,0:T(8,128)(2,1)}, bf16[2,504,256]{2,1,0:T(8,128)(2,1)}, u32[]{:S(2)}, u32[]{:S(2)}) %collective-permute-start.5) | collective-permute-done | bytes 516128 | tf_op jit(solution)/shard_map/ppermute | solution.py:35
  177.4 1.9 collective-permute-start.16
  179.3 2.8 near.4
  182.1 3.6 %collective-permute-start.6 = (bf16[4,480,256]{2,1,0:T(8,128)(2,1)}, bf16[4,480,256]{2,1,0:T(8,128)(2,1)}, u32[]{:S(2)}, u32[]{:S(2)}) collective-permute-start(bf16[4,480,256]{2,1,0:T(8,128)(2,1)} %near.4), channel_id=1, source_target_pairs={{0,2},{2,4},{4,6},{6,8},{8,10},{10,12},{12,14},{14,16},{16,18},{18... | collective-permute-start | bytes 2949128 | tf_op jit(solution)/shard_map/ppermute | solution.py:40
  186.6 2.8 near.5
  189.5 1.9 collective-permute-start.12
  191.4 8.4 %collective-permute-done.23.sec_ref.sec_kv = bf16[2,504,256]{2,1,0:T(8,128)(2,1)} collective-permute-done((bf16[2,504,256]{2,1,0:T(8,128)(2,1)}, bf16[2,504,256]{2,1,0:T(8,128)(2,1)}, u32[]{:S(2)}, u32[]{:S(2)}) %collective-permute-start.23) | collective-permute-done | bytes 516128 | tf_op jit(solution)/shard_map/ppermute | solution.py:35
  200.1 1.0 collective-permute-done.24.dia_ref.dia_kv
  201.8 2.0 pack.12
  203.8 1.9 constant_dynamic-slice_fusion
  205.7 2.1 constant_dynamic-slice_fusion.1
  207.8 2.7 near.7
  210.5 2.6 collective-permute-start.17
  214.7 11.9 %attend.4.rest_0_ = bf16[2,504,256]{2,1,0:T(8,128)(2,1)} custom-call(s32[15]{0:T(128)} %concatenate.3.info_ref, bf16[1,504,5120]{2,1,0:T(8,128)(2,1)} %q_ref.7, bf16[1,504,5120]{2,1,0:T(8,128)(2,1)} %k_ref.15, bf16[1,504,5120]{2,1,0:T(8,128)(2,1)} %v_ref.15, bf16[1,504,256]{2,1,0:T(8,128)(2,1)} %collective-permute-done.seq_q, ...), custom_call_target="tpu_custom_call" | custom-call | flops 3071803392 | bytes 5160960 | tf_op jit(solution)/shard_map/attend/pallas_call | solution.py:225
  226.6 2.1 collective-permute-start.25
  228.8 16.3 %attend.5.rest_0_ = bf16[2,504,768]{2,1,0:T(8,128)(2,1)} custom-call(s32[15]{0:T(128)} %concatenate.3.info_ref, bf16[1,504,5120]{2,1,0:T(8,128)(2,1)} %q_ref.7, bf16[1,504,5120]{2,1,0:T(8,128)(2,1)} %k_ref.15, bf16[1,504,5120]{2,1,0:T(8,128)(2,1)} %v_ref.15, bf16[3,504,384]{2,1,0:T(8,128)(2,1)} %collective-permute-done.13.seq_ref.seq_q.seq_kv, ...), custom_call_target="tpu_custom_call" | custom-call | flops 4607705088 | bytes 7741440 | tf_op jit(solution)/shard_map/attend/pallas_call | solution.py:225
  245.1 2.6 collective-permute-start.20
  247.7 16.3 %attend.6.rest_0_ = bf16[2,504,768]{2,1,0:T(8,128)(2,1)} custom-call(s32[15]{0:T(128)} %concatenate.3.info_ref, bf16[1,504,5120]{2,1,0:T(8,128)(2,1)} %q_ref.7, bf16[1,504,5120]{2,1,0:T(8,128)(2,1)} %k_ref.15, bf16[1,504,5120]{2,1,0:T(8,128)(2,1)} %v_ref.15, ...), custom_call_target="tpu_custom_call", output_to_operand_aliasing={{}: (14, {})} | custom-call | flops 4607705088 | bytes 7741440 | tf_op jit(solution)/shard_map/attend/pallas_call | solution.py:225
  264.8 2.4 fusion
  267.2 2.5 collective-permute-start.26
  269.8 3.0 collective-permute-start.28
  272.7 1.5 collective-permute-done.21.dia_q
  274.9 12.1 %attend.7.rest_3_ = bf16[2,504,256]{2,1,0:T(8,128)(2,1)} custom-call(s32[15]{0:T(128)} %concatenate.3.info_ref, bf16[1,504,5120]{2,1,0:T(8,128)(2,1)} %q_ref.7, bf16[1,504,5120]{2,1,0:T(8,128)(2,1)} %k_ref.15, bf16[1,504,5120]{2,1,0:T(8,128)(2,1)} %v_ref.15, bf16[1,504,256]{2,1,0:T(8,128)(2,1)} %collective-permute-done.19.seq_q, ...), custom_call_target="tpu_custom_call" | custom-call | flops 3071803392 | bytes 5160960 | tf_op jit(solution)/shard_map/attend/pallas_call | solution.py:225
  287.0 1.1 fusion.1
  288.1 1.0 fusion.2
  289.2 3.0 collective-permute-start.27
  292.2 2.9 collective-permute-start.18
  295.1 3.3 %finish.2.rest_6_ = bf16[2,504,1280]{2,1,0:T(8,128)(2,1)} custom-call(s32[15]{0:T(128)S(1)} %copy-done.3, bf16[2,504,768]{2,1,0:T(8,128)(2,1)S(1)} %copy-done, bf16[504,768]{1,0:T(8,128)(2,1)} %collective-permute-done.17.rest_1_, bf16[480,768]{1,0:T(8,128)(2,1)} %collective-permute-done.28.rest_2_), custom_call_target="tpu_custom_call" | custom-call | flops 77414400 | bytes 4644864 | tf_op jit(solution)/shard_map/finish/pallas_call | solution.py:305
  298.9 2.9 collective-permute-done.18.rest_2_
  301.8 2.8 finish.3
  (47 shorter events, 10.6 us)
Async XLA Ops:
  2.5 87.1 %collective-permute-start.13 = (bf16[3,504,384]{2,1,0:T(8,128)(2,1)}, bf16[3,504,384]{2,1,0:T(8,128)(2,1)}, u32[]{:S(2)}, u32[]{:S(2)}) collective-permute-start(bf16[3,504,384]{2,1,0:T(8,128)(2,1)} %get-tuple-element.33), channel_id=1, source_target_pairs={{0,1},{1,0},{64,65},{65,64},{2,3},{3,2},{66,67},{67,66},{4,5},{5,4... | collective-permute-start | bytes 3483656 | tf_op jit(solution)/shard_map/ppermute | solution.py:35
  6.5 86.2 %collective-permute-start.14 = (bf16[3,504,384]{2,1,0:T(8,128)(2,1)}, bf16[3,504,384]{2,1,0:T(8,128)(2,1)}, u32[]{:S(2)}, u32[]{:S(2)}) collective-permute-start(bf16[3,504,384]{2,1,0:T(8,128)(2,1)} %get-tuple-element.34), channel_id=1, source_target_pairs={{0,64},{1,65},{64,0},{65,1},{2,66},{3,67},{66,2},{67,3},{4,68},{5,... | collective-permute-start | bytes 3483656 | tf_op jit(solution)/shard_map/ppermute | solution.py:35
  9.4 68.3 %collective-permute-start = (bf16[1,504,256]{2,1,0:T(8,128)(2,1)}, bf16[1,504,256]{2,1,0:T(8,128)(2,1)}, u32[]{:S(2)}, u32[]{:S(2)}) collective-permute-start(bf16[1,504,256]{2,1,0:T(8,128)(2,1)} %get-tuple-element.24), channel_id=1, source_target_pairs={{0,1},{1,0},{64,65},{65,64},{2,3},{3,2},{66,67},{67,66},{4,5},{5,4... | collective-permute-start | bytes 774152 | tf_op jit(solution)/shard_map/ppermute | solution.py:35
  13.0 68.6 %collective-permute-start.3 = (bf16[2,504,256]{2,1,0:T(8,128)(2,1)}, bf16[2,504,256]{2,1,0:T(8,128)(2,1)}, u32[]{:S(2)}, u32[]{:S(2)}) collective-permute-start(bf16[2,504,256]{2,1,0:T(8,128)(2,1)} %get-tuple-element.27), channel_id=1, source_target_pairs={{0,1},{1,0},{64,65},{65,64},{2,3},{3,2},{66,67},{67,66},{4,5},{5,4... | collective-permute-start | bytes 1548296 | tf_op jit(solution)/shard_map/ppermute | solution.py:35
  16.2 58.5 %collective-permute-start.7 = (f32[1,1280]{1,0:T(1,128)S(1)}, f32[1,1280]{1,0:T(1,128)}, u32[]{:S(2)}, u32[]{:S(2)}) collective-permute-start(f32[1,1280]{1,0:T(1,128)S(1)} %constant_dynamic-slice_fusion.3), channel_id=1, source_target_pairs={{0,64},{1,65},{64,0},{65,1},{2,66},{3,67},{66,2},{67,3},{4,68},{5,... | collective-permute-start | bytes 15368 | tf_op jit(solution)/shard_map/ppermute | solution.py:35
  74.7 14.9 %collective-permute-start.4 = (bf16[2,504,256]{2,1,0:T(8,128)(2,1)}, bf16[2,504,256]{2,1,0:T(8,128)(2,1)}, u32[]{:S(2)}, u32[]{:S(2)}) collective-permute-start(bf16[2,504,256]{2,1,0:T(8,128)(2,1)} %get-tuple-element.28), channel_id=1, source_target_pairs={{0,64},{1,65},{64,0},{65,1},{2,66},{3,67},{66,2},{67,3},{4,68},{5,... | collective-permute-start | bytes 1548296 | tf_op jit(solution)/shard_map/ppermute | solution.py:35
  77.7 30.0 %collective-permute-start.15 = (bf16[3,504,384]{2,1,0:T(8,128)(2,1)}, bf16[3,504,384]{2,1,0:T(8,128)(2,1)}, u32[]{:S(2)}, u32[]{:S(2)}) collective-permute-start(bf16[3,504,384]{2,1,0:T(8,128)(2,1)} %pack.11), channel_id=1, source_target_pairs={{0,65},{1,64},{64,1},{65,0},{2,67},{3,66},{66,3},{67,2},{4,69},{5,... | collective-permute-start | bytes 3483656 | tf_op jit(solution)/shard_map/ppermute | solution.py:35
  81.6 100.5 %collective-permute-start.10 = (bf16[3,504,384]{2,1,0:T(8,128)(2,1)}, bf16[3,504,384]{2,1,0:T(8,128)(2,1)}, u32[]{:S(2)}, u32[]{:S(2)}) collective-permute-start(bf16[3,504,384]{2,1,0:T(8,128)(2,1)} %get-tuple-element.31), channel_id=1, source_target_pairs={{0,64},{1,65},{64,0},{65,1},{2,66},{3,67},{66,2},{67,3},{4,68},{5,... | collective-permute-start | bytes 3483656 | tf_op jit(solution)/shard_map/ppermute | solution.py:35
  89.6 96.1 %collective-permute-start.11 = (bf16[3,504,384]{2,1,0:T(8,128)(2,1)}, bf16[3,504,384]{2,1,0:T(8,128)(2,1)}, u32[]{:S(2)}, u32[]{:S(2)}) collective-permute-start(bf16[3,504,384]{2,1,0:T(8,128)(2,1)} %get-tuple-element.32), channel_id=1, source_target_pairs={{0,65},{1,64},{64,1},{65,0},{2,67},{3,66},{66,3},{67,2},{4,69},{5,... | collective-permute-start | bytes 3483656 | tf_op jit(solution)/shard_map/ppermute | solution.py:35
  89.6 96.2 %collective-permute-start.9 = (bf16[3,504,384]{2,1,0:T(8,128)(2,1)}, bf16[3,504,384]{2,1,0:T(8,128)(2,1)}, u32[]{:S(2)}, u32[]{:S(2)}) collective-permute-start(bf16[3,504,384]{2,1,0:T(8,128)(2,1)} %get-tuple-element.30), channel_id=1, source_target_pairs={{0,1},{1,0},{64,65},{65,64},{2,3},{3,2},{66,67},{67,66},{4,5},{5,4... | collective-permute-start | bytes 3483656 | tf_op jit(solution)/shard_map/ppermute | solution.py:35
  92.7 84.7 %collective-permute-start.5 = (bf16[2,504,256]{2,1,0:T(8,128)(2,1)}, bf16[2,504,256]{2,1,0:T(8,128)(2,1)}, u32[]{:S(2)}, u32[]{:S(2)}) collective-permute-start(bf16[2,504,256]{2,1,0:T(8,128)(2,1)} %get-tuple-element.29), channel_id=1, source_target_pairs={{0,65},{1,64},{64,1},{65,0},{2,67},{3,66},{66,3},{67,2},{4,69},{5,... | collective-permute-start | bytes 1548296 | tf_op jit(solution)/shard_map/ppermute | solution.py:35
  107.8 81.7 %collective-permute-start.22 = (bf16[2,504,256]{2,1,0:T(8,128)(2,1)}, bf16[2,504,256]{2,1,0:T(8,128)(2,1)}, u32[]{:S(2)}, u32[]{:S(2)}) collective-permute-start(bf16[2,504,256]{2,1,0:T(8,128)(2,1)} %get-tuple-element.39), channel_id=1, source_target_pairs={{0,1},{1,0},{64,65},{65,64},{2,3},{3,2},{66,67},{67,66},{4,5},{5,4... | collective-permute-start | bytes 1548296 | tf_op jit(solution)/shard_map/ppermute | solution.py:35
  177.4 49.2 %collective-permute-start.16 = (bf16[4,480,384]{2,1,0:T(8,128)(2,1)}, bf16[4,480,384]{2,1,0:T(8,128)(2,1)}, u32[]{:S(2)}, u32[]{:S(2)}) collective-permute-start(bf16[4,480,384]{2,1,0:T(8,128)(2,1)} %near.6), channel_id=1, source_target_pairs={{0,2},{2,4},{4,6},{6,8},{8,10},{10,12},{12,14},{14,16},{16,18},{18... | collective-permute-start | bytes 4423688 | tf_op jit(solution)/shard_map/ppermute | solution.py:40
  182.1 31.7 %collective-permute-start.6 = (bf16[4,480,256]{2,1,0:T(8,128)(2,1)}, bf16[4,480,256]{2,1,0:T(8,128)(2,1)}, u32[]{:S(2)}, u32[]{:S(2)}) collective-permute-start(bf16[4,480,256]{2,1,0:T(8,128)(2,1)} %near.4), channel_id=1, source_target_pairs={{0,2},{2,4},{4,6},{6,8},{8,10},{10,12},{12,14},{14,16},{16,18},{18... | collective-permute-start | bytes 2949128 | tf_op jit(solution)/shard_map/ppermute | solution.py:40
  185.7 14.1 %collective-permute-start.23 = (bf16[2,504,256]{2,1,0:T(8,128)(2,1)}, bf16[2,504,256]{2,1,0:T(8,128)(2,1)}, u32[]{:S(2)}, u32[]{:S(2)}) collective-permute-start(bf16[2,504,256]{2,1,0:T(8,128)(2,1)} %get-tuple-element.40), channel_id=1, source_target_pairs={{0,64},{1,65},{64,0},{65,1},{2,66},{3,67},{66,2},{67,3},{4,68},{5,... | collective-permute-start | bytes 1548296 | tf_op jit(solution)/shard_map/ppermute | solution.py:35
  185.8 15.3 %collective-permute-start.24 = (bf16[2,504,256]{2,1,0:T(8,128)(2,1)}, bf16[2,504,256]{2,1,0:T(8,128)(2,1)}, u32[]{:S(2)}, u32[]{:S(2)}) collective-permute-start(bf16[2,504,256]{2,1,0:T(8,128)(2,1)} %get-tuple-element.41), channel_id=1, source_target_pairs={{0,65},{1,64},{64,1},{65,0},{2,67},{3,66},{66,3},{67,2},{4,69},{5,... | collective-permute-start | bytes 1548296 | tf_op jit(solution)/shard_map/ppermute | solution.py:35
  189.5 55.6 %collective-permute-start.12 = (bf16[4,480,384]{2,1,0:T(8,128)(2,1)}, bf16[4,480,384]{2,1,0:T(8,128)(2,1)}, u32[]{:S(2)}, u32[]{:S(2)}) collective-permute-start(bf16[4,480,384]{2,1,0:T(8,128)(2,1)} %near.5), channel_id=1, source_target_pairs={{0,2},{2,4},{4,6},{6,8},{8,10},{10,12},{12,14},{14,16},{16,18},{18... | collective-permute-start | bytes 4423688 | tf_op jit(solution)/shard_map/ppermute | solution.py:40
  199.8 10.7 %collective-permute-start.1 = (bf16[1,504,256]{2,1,0:T(8,128)(2,1)}, bf16[1,504,256]{2,1,0:T(8,128)(2,1)}, u32[]{:S(2)}, u32[]{:S(2)}) collective-permute-start(bf16[1,504,256]{2,1,0:T(8,128)(2,1)} %get-tuple-element.25), channel_id=1, source_target_pairs={{0,64},{1,65},{64,0},{65,1},{2,66},{3,67},{66,2},{67,3},{4,68},{5,... | collective-permute-start | bytes 774152 | tf_op jit(solution)/shard_map/ppermute | solution.py:35
  201.1 12.0 %collective-permute-start.2 = (bf16[1,504,256]{2,1,0:T(8,128)(2,1)}, bf16[1,504,256]{2,1,0:T(8,128)(2,1)}, u32[]{:S(2)}, u32[]{:S(2)}) collective-permute-start(bf16[1,504,256]{2,1,0:T(8,128)(2,1)} %get-tuple-element.26), channel_id=1, source_target_pairs={{0,65},{1,64},{64,1},{65,0},{2,67},{3,66},{66,3},{67,2},{4,69},{5,... | collective-permute-start | bytes 774152 | tf_op jit(solution)/shard_map/ppermute | solution.py:35
  210.5 53.5 %collective-permute-start.17 = (bf16[504,768]{1,0:T(8,128)(2,1)}, bf16[504,768]{1,0:T(8,128)(2,1)}, u32[]{:S(2)}, u32[]{:S(2)}) collective-permute-start(bf16[504,768]{1,0:T(8,128)(2,1)} %constant_dynamic-slice_fusion.1), channel_id=1, source_target_pairs={{0,65},{1,64},{64,1},{65,0},{2,67},{3,66},{66,3},{67,2},{4,69},{5,... | collective-permute-start | bytes 2322440 | tf_op jit(solution)/shard_map/ppermute | solution.py:35
  213.1 73.8 %collective-permute-start.8 = (bf16[504,256]{1,0:T(8,128)(2,1)}, bf16[504,256]{1,0:T(8,128)(2,1)}, u32[]{:S(2)}, u32[]{:S(2)}) collective-permute-start(bf16[504,256]{1,0:T(8,128)(2,1)} %get-tuple-element.44), channel_id=1, source_target_pairs={{0,65},{1,64},{64,1},{65,0},{2,67},{3,66},{66,3},{67,2},{4,69},{5,... | collective-permute-start | bytes 774152 | tf_op jit(solution)/shard_map/ppermute | solution.py:35
  213.8 53.4 %collective-permute-start.19 = (bf16[1,504,256]{2,1,0:T(8,128)(2,1)}, bf16[1,504,256]{2,1,0:T(8,128)(2,1)}, u32[]{:S(2)}, u32[]{:S(2)}) collective-permute-start(bf16[1,504,256]{2,1,0:T(8,128)(2,1)} %get-tuple-element.36), channel_id=1, source_target_pairs={{0,1},{1,0},{64,65},{65,64},{2,3},{3,2},{66,67},{67,66},{4,5},{5,4... | collective-permute-start | bytes 774152 | tf_op jit(solution)/shard_map/ppermute | solution.py:35
  226.6 48.2 %collective-permute-start.25 = (bf16[4,480,256]{2,1,0:T(8,128)(2,1)}, bf16[4,480,256]{2,1,0:T(8,128)(2,1)}, u32[]{:S(2)}, u32[]{:S(2)}) collective-permute-start(bf16[4,480,256]{2,1,0:T(8,128)(2,1)} %near.7), channel_id=1, source_target_pairs={{0,2},{2,4},{4,6},{6,8},{8,10},{10,12},{12,14},{14,16},{16,18},{18... | collective-permute-start | bytes 2949128 | tf_op jit(solution)/shard_map/ppermute | solution.py:40
  245.1 24.7 %collective-permute-start.20 = (bf16[1,504,256]{2,1,0:T(8,128)(2,1)}, bf16[1,504,256]{2,1,0:T(8,128)(2,1)}, u32[]{:S(2)}, u32[]{:S(2)}) collective-permute-start(bf16[1,504,256]{2,1,0:T(8,128)(2,1)} %get-tuple-element.37), channel_id=1, source_target_pairs={{0,64},{1,65},{64,0},{65,1},{2,66},{3,67},{66,2},{67,3},{4,68},{5,... | collective-permute-start | bytes 774152 | tf_op jit(solution)/shard_map/ppermute | solution.py:35
  264.0 10.2 %collective-permute-start.21 = (bf16[1,504,256]{2,1,0:T(8,128)(2,1)}, bf16[1,504,256]{2,1,0:T(8,128)(2,1)S(1)}, u32[]{:S(2)}, u32[]{:S(2)}) collective-permute-start(bf16[1,504,256]{2,1,0:T(8,128)(2,1)} %get-tuple-element.38), channel_id=1, source_target_pairs={{0,65},{1,64},{64,1},{65,0},{2,67},{3,66},{66,3},{67,2},{4,69},{5,... | collective-permute-start | bytes 774152 | tf_op jit(solution)/shard_map/ppermute | solution.py:35
  267.2 20.9 %collective-permute-start.26 = (bf16[504,256]{1,0:T(8,128)(2,1)}, bf16[504,256]{1,0:T(8,128)(2,1)S(1)}, u32[]{:S(2)}, u32[]{:S(2)}) collective-permute-start(bf16[504,256]{1,0:T(8,128)(2,1)} %get-tuple-element.43), channel_id=1, source_target_pairs={{0,65},{1,64},{64,1},{65,0},{2,67},{3,66},{66,3},{67,2},{4,69},{5,... | collective-permute-start | bytes 774152 | tf_op jit(solution)/shard_map/ppermute | solution.py:35
  269.8 25.3 %collective-permute-start.28 = (bf16[480,768]{1,0:T(8,128)(2,1)}, bf16[480,768]{1,0:T(8,128)(2,1)}, u32[]{:S(2)}, u32[]{:S(2)}) collective-permute-start(bf16[480,768]{1,0:T(8,128)(2,1)} %fusion), channel_id=1, source_target_pairs={{0,2},{2,4},{4,6},{6,8},{8,10},{10,12},{12,14},{14,16},{16,18},{18... | collective-permute-start | bytes 2211848 | tf_op jit(solution)/shard_map/ppermute | solution.py:40
  274.2 0.7 copy-start.4
  274.9 20.2 %copy-start = (bf16[2,504,768]{2,1,0:T(8,128)(2,1)S(1)}, bf16[2,504,768]{2,1,0:T(8,128)(2,1)}, u32[]{:S(2)}) copy-start(bf16[2,504,768]{2,1,0:T(8,128)(2,1)} %attend.6.rest_0_) | copy-start | bytes 4644868
  286.9 8.2 %copy-start.3 = (s32[15]{0:T(128)S(1)}, s32[15]{0:T(128)}, u32[]{:S(2)}) copy-start(s32[15]{0:T(128)} %concatenate.3.info_ref) | copy-start | bytes 184
  289.1 12.7 %copy-start.1 = (bf16[2,504,256]{2,1,0:T(8,128)(2,1)S(1)}, bf16[2,504,256]{2,1,0:T(8,128)(2,1)}, u32[]{:S(2)}) copy-start(bf16[2,504,256]{2,1,0:T(8,128)(2,1)} %attend.4.rest_0_) | copy-start | bytes 1548292
  289.2 12.7 %copy-start.2 = (bf16[2,504,256]{2,1,0:T(8,128)(2,1)S(1)}, bf16[2,504,256]{2,1,0:T(8,128)(2,1)}, u32[]{:S(2)}) copy-start(bf16[2,504,256]{2,1,0:T(8,128)(2,1)} %attend.7.rest_3_) | copy-start | bytes 1548292
  289.2 9.8 %collective-permute-start.27 = (bf16[480,256]{1,0:T(8,128)(2,1)S(1)}, bf16[480,256]{1,0:T(8,128)(2,1)S(1)}, u32[]{:S(2)}, u32[]{:S(2)}) collective-permute-start(bf16[480,256]{1,0:T(8,128)(2,1)S(1)} %fusion.2), channel_id=1, source_target_pairs={{0,2},{2,4},{4,6},{6,8},{8,10},{10,12},{12,14},{14,16},{16,18},{18... | collective-permute-start | bytes 737288 | tf_op jit(solution)/shard_map/ppermute | solution.py:40
  292.2 9.6 %collective-permute-start.18 = (bf16[480,256]{1,0:T(8,128)(2,1)S(1)}, bf16[480,256]{1,0:T(8,128)(2,1)S(1)}, u32[]{:S(2)}, u32[]{:S(2)}) collective-permute-start(bf16[480,256]{1,0:T(8,128)(2,1)S(1)} %fusion.1), channel_id=1, source_target_pairs={{0,2},{2,4},{4,6},{6,8},{8,10},{10,12},{12,14},{14,16},{16,18},{18... | collective-permute-start | bytes 737288 | tf_op jit(solution)/shard_map/ppermute | solution.py:40

commit v4 on v3

--- a/solution.py
+++ b/solution.py
@@ -17,8 +17,8 @@
 QUARTER_HEADS = 10
 CHUNKS = (3, 3, 2, 2)
 GROUPS = ((0, 1), (2,), (3,))
-FINISHES = ((0,), (1, 2))
-FINISH_HEADS = {1: 3, 2: 2}
+FINISHES = ((0,), (1,), (2,))
+FINISH_HEADS = {6: 3, 2: 2}
 SENDS = (("z", 0), ("z", 1), ("kv", 2), ("kv", 3), ("q", 2), ("q", 3))
 VMEM_LIMIT = 66000 * 1024
 PAIR_AXES = ("section", "seq")
@@ -284,7 +284,7 @@
 
 def finish(info, parts, first, second):
     rows = parts[0][0].shape[1]
-    width = FINISH_HEADS[len(parts)] * HEAD_DIM
+    width = FINISH_HEADS[parts[0][0].shape[2] // HEAD_DIM] * HEAD_DIM
     steps = tuple(part[0].shape[2] // width for part in parts)
     operands, in_specs = [info], []
     begin = 0

time: 306 us -> 306 us (level)
    pallas_call x2 -> x3, Pallas kernels: 6.05 us -> 7.28 us  [finish(): pl.pallas_call(functools.partial(finish_kernel, steps), grid_spec=pltpu.P...]
  transfers between devices with their start and end apart: 29 -> 29, of which waited for: 9 -> 9; matrix products, arithmetic and copies ran while one was open for 4% -> 4% of each run, Pallas kernels for 28% -> 29%
where the time goes in v4:
time: 306 us; the launch traced here: 305 us
  waiting for transfers between devices  153 us (50%)
  Pallas kernels  91.3 us (30%)
  starting transfers between devices  45.5 us (15%)
  local copies, waits for them, and re-layouts  9.43 us (3%)
  other arithmetic  4.59 us (2%)
    ppermute x22, waiting for transfers between devices, to_partner(): return lax.ppermute(block, PAIR_AXES, pairs)  152 us
    pallas_call x4, Pallas kernels, attend(): pl.pallas_call(attend_kernel, grid_spec=pltpu.PrefetchScalarGridSpec(num_...  56.6 us
    ppermute x22, starting transfers between devices, to_partner(): return lax.ppermute(block, PAIR_AXES, pairs)  27 us
    ppermute x7, starting transfers between devices, to_next_span(): return lax.ppermute(block, 'span', [(i, i + 1) for i in range(length - 1)])  18.4 us
    pallas_call x7, Pallas kernels, pack(): pl.pallas_call(functools.partial(pack_kernel, width, start, dests, count)...  16.2 us
    pallas_call x4, Pallas kernels, near_rows(): pl.pallas_call(functools.partial(near_kernel, width, start), grid_spec=pl...  11.2 us
    pallas_call x3, Pallas kernels, finish(): pl.pallas_call(functools.partial(finish_kernel, steps), grid_spec=pltpu.P...  7.28 us
  transfers between devices with their start and end apart: 29, of which 9 were waited for; matrix products, arithmetic and copies ran while one was open for 4% of the time, Pallas kernels for 29%

profile of v4, /device:TPU:2, one launch (start us, length us, event | category | flops | bytes accessed | tf_op | source)
XLA Modules:
  0.0 305.0 jit_solution(8530705828037472527)
XLA Ops:
  0.0 2.5 pack.12
  2.5 4.0 %collective-permute-start.21 = (bf16[3,504,384]{2,1,0:T(8,128)(2,1)}, bf16[3,504,384]{2,1,0:T(8,128)(2,1)}, u32[]{:S(2)}, u32[]{:S(2)}) collective-permute-start(bf16[3,504,384]{2,1,0:T(8,128)(2,1)} %get-tuple-element.39), channel_id=1, source_target_pairs={{0,1},{1,0},{64,65},{65,64},{2,3},{3,2},{66,67},{67,66},{4,5},{5,4... | collective-permute-start | bytes 3483656 | tf_op jit(solution)/shard_map/ppermute | solution.py:35
  7.5 2.0 pack.9
  9.5 1.1 collective-permute-start.10
  10.6 2.4 pack.10
  13.9 1.4 collective-permute-start.7
  15.3 59.4 %collective-permute-done.7.other_gate = f32[1,1280]{1,0:T(1,128)} collective-permute-done((f32[1,1280]{1,0:T(1,128)S(1)}, f32[1,1280]{1,0:T(1,128)}, u32[]{:S(2)}, u32[]{:S(2)}) %collective-permute-start.7) | collective-permute-done | bytes 5152 | tf_op jit(solution)/shard_map/ppermute | solution.py:35
  75.7 2.0 pack.13
  78.5 3.0 pack.11
  81.6 2.5 collective-permute-start.17
  84.0 5.6 %collective-permute-done.13.sec_ref.sec_kv = bf16[2,504,256]{2,1,0:T(8,128)(2,1)} collective-permute-done((bf16[2,504,256]{2,1,0:T(8,128)(2,1)}, bf16[2,504,256]{2,1,0:T(8,128)(2,1)}, u32[]{:S(2)}, u32[]{:S(2)}) %collective-permute-start.13) | collective-permute-done | bytes 516128 | tf_op jit(solution)/shard_map/ppermute | solution.py:35
  91.3 2.5 collective-permute-start.14
  93.9 2.4 pack.8
  96.2 36.5 %collective-permute-done.23.dia_ref.dia_q.dia_kv = bf16[3,504,384]{2,1,0:T(8,128)(2,1)} collective-permute-done((bf16[3,504,384]{2,1,0:T(8,128)(2,1)}, bf16[3,504,384]{2,1,0:T(8,128)(2,1)}, u32[]{:S(2)}, u32[]{:S(2)}) %collective-permute-start.23) | collective-permute-done | bytes 1161248 | tf_op jit(solution)/shard_map/ppermute | solution.py:35
  132.7 1.2 dynamic_slice.31
  133.9 1.2 dynamic_slice.30
  137.9 2.8 near.7
  140.8 36.7 %collective-permute-done.14.dia_ref.dia_kv = bf16[2,504,256]{2,1,0:T(8,128)(2,1)} collective-permute-done((bf16[2,504,256]{2,1,0:T(8,128)(2,1)}, bf16[2,504,256]{2,1,0:T(8,128)(2,1)}, u32[]{:S(2)}, u32[]{:S(2)}) %collective-permute-start.14) | collective-permute-done | bytes 516128 | tf_op jit(solution)/shard_map/ppermute | solution.py:35
  177.4 1.9 collective-permute-start.24
  179.3 2.8 near.5
  182.1 3.6 %collective-permute-start.15 = (bf16[4,480,256]{2,1,0:T(8,128)(2,1)}, bf16[4,480,256]{2,1,0:T(8,128)(2,1)}, u32[]{:S(2)}, u32[]{:S(2)}) collective-permute-start(bf16[4,480,256]{2,1,0:T(8,128)(2,1)} %near.5), channel_id=1, source_target_pairs={{0,2},{2,4},{4,6},{6,8},{8,10},{10,12},{12,14},{14,16},{16,18},{18... | collective-permute-start | bytes 2949128 | tf_op jit(solution)/shard_map/ppermute | solution.py:40
  186.6 2.8 near.6
  189.5 1.9 collective-permute-start.20
  191.4 8.4 %collective-permute-done.4.sec_ref.sec_kv = bf16[2,504,256]{2,1,0:T(8,128)(2,1)} collective-permute-done((bf16[2,504,256]{2,1,0:T(8,128)(2,1)}, bf16[2,504,256]{2,1,0:T(8,128)(2,1)}, u32[]{:S(2)}, u32[]{:S(2)}) %collective-permute-start.4) | collective-permute-done | bytes 516128 | tf_op jit(solution)/shard_map/ppermute | solution.py:35
  201.1 1.0 collective-permute-start.9
  202.1 2.0 pack.7
  204.1 1.9 constant_dynamic-slice_fusion.1
  206.0 2.1 constant_dynamic-slice_fusion
  208.1 2.7 near.4
  210.9 3.3 %collective-permute-done.11.dia_q = bf16[1,504,256]{2,1,0:T(8,128)(2,1)} collective-permute-done((bf16[1,504,256]{2,1,0:T(8,128)(2,1)}, bf16[1,504,256]{2,1,0:T(8,128)(2,1)}, u32[]{:S(2)}, u32[]{:S(2)}) %collective-permute-start.11) | collective-permute-done | bytes 258080 | tf_op jit(solution)/shard_map/ppermute | solution.py:35
  214.8 2.5 collective-permute-start.16
  217.4 11.9 %attend.5.rest_0_ = bf16[2,504,256]{2,1,0:T(8,128)(2,1)} custom-call(s32[15]{0:T(128)} %concatenate.3.info_ref, bf16[1,504,5120]{2,1,0:T(8,128)(2,1)} %q_ref.7, bf16[1,504,5120]{2,1,0:T(8,128)(2,1)} %k_ref.15, bf16[1,504,5120]{2,1,0:T(8,128)(2,1)} %v_ref.15, bf16[1,504,256]{2,1,0:T(8,128)(2,1)} %collective-permute-done.9.seq_q, ...), custom_call_target="tpu_custom_call" | custom-call | flops 3071803392 | bytes 5160960 | tf_op jit(solution)/shard_map/attend/pallas_call | solution.py:225
  229.3 2.1 collective-permute-start.6
  231.4 16.3 %attend.6.rest_0_ = bf16[2,504,768]{2,1,0:T(8,128)(2,1)} custom-call(s32[15]{0:T(128)} %concatenate.3.info_ref, bf16[1,504,5120]{2,1,0:T(8,128)(2,1)} %q_ref.7, bf16[1,504,5120]{2,1,0:T(8,128)(2,1)} %k_ref.15, bf16[1,504,5120]{2,1,0:T(8,128)(2,1)} %v_ref.15, bf16[3,504,384]{2,1,0:T(8,128)(2,1)} %collective-permute-done.21.seq_ref.seq_q.seq_kv, ...), custom_call_target="tpu_custom_call" | custom-call | flops 4607705088 | bytes 7741440 | tf_op jit(solution)/shard_map/attend/pallas_call | solution.py:225
  247.7 1.6 collective-permute-start.1
  249.4 16.3 %attend.7.rest_0_ = bf16[2,504,768]{2,1,0:T(8,128)(2,1)} custom-call(s32[15]{0:T(128)} %concatenate.3.info_ref, bf16[1,504,5120]{2,1,0:T(8,128)(2,1)} %q_ref.7, bf16[1,504,5120]{2,1,0:T(8,128)(2,1)} %k_ref.15, bf16[1,504,5120]{2,1,0:T(8,128)(2,1)} %v_ref.15, ...), custom_call_target="tpu_custom_call", output_to_operand_aliasing={{}: (14, {})} | custom-call | flops 4607705088 | bytes 7741440 | tf_op jit(solution)/shard_map/attend/pallas_call | solution.py:225
  265.7 2.6 collective-permute-start.2
  268.3 2.4 fusion
  271.4 3.0 collective-permute-start.28
  274.4 1.5 collective-permute-done.2.dia_q
  276.6 12.1 %attend.4.rest_0_ = bf16[2,504,256]{2,1,0:T(8,128)(2,1)} custom-call(s32[15]{0:T(128)} %concatenate.3.info_ref, bf16[1,504,5120]{2,1,0:T(8,128)(2,1)} %q_ref.7, bf16[1,504,5120]{2,1,0:T(8,128)(2,1)} %k_ref.15, bf16[1,504,5120]{2,1,0:T(8,128)(2,1)} %v_ref.15, bf16[1,504,256]{2,1,0:T(8,128)(2,1)} %collective-permute-done.seq_q, ...), custom_call_target="tpu_custom_call" | custom-call | flops 3071803392 | bytes 5160960 | tf_op jit(solution)/shard_map/attend/pallas_call | solution.py:225
  288.6 1.1 fusion.1
  289.8 2.9 collective-permute-start.27
  292.7 1.0 fusion.2
  293.7 3.1 %collective-permute-start.26 = (bf16[480,256]{1,0:T(8,128)(2,1)S(1)}, bf16[480,256]{1,0:T(8,128)(2,1)S(1)}, u32[]{:S(2)}, u32[]{:S(2)}) collective-permute-start(bf16[480,256]{1,0:T(8,128)(2,1)S(1)} %fusion.2), channel_id=1, source_target_pairs={{0,2},{2,4},{4,6},{6,8},{8,10},{10,12},{12,14},{14,16},{16,18},{18... | collective-permute-start | bytes 737288 | tf_op jit(solution)/shard_map/ppermute | solution.py:40
  296.8 3.3 %finish.3.rest_3_ = bf16[2,504,1280]{2,1,0:T(8,128)(2,1)} custom-call(s32[15]{0:T(128)S(1)} %copy-done.3, bf16[2,504,768]{2,1,0:T(8,128)(2,1)S(1)} %copy-done, bf16[504,768]{1,0:T(8,128)(2,1)} %collective-permute-done.25.rest_1_, bf16[480,768]{1,0:T(8,128)(2,1)} %collective-permute-done.28.rest_2_), custom_call_target="tpu_custom_call" | custom-call | flops 77414400 | bytes 4644864 | tf_op jit(solution)/shard_map/finish/pallas_call | solution.py:305
  300.1 2.5 finish.4.rest_3_
  303.5 1.5 finish.5
  (48 shorter events, 12.3 us)
Async XLA Ops:
  2.5 88.1 %collective-permute-start.21 = (bf16[3,504,384]{2,1,0:T(8,128)(2,1)}, bf16[3,504,384]{2,1,0:T(8,128)(2,1)}, u32[]{:S(2)}, u32[]{:S(2)}) collective-permute-start(bf16[3,504,384]{2,1,0:T(8,128)(2,1)} %get-tuple-element.39), channel_id=1, source_target_pairs={{0,1},{1,0},{64,65},{65,64},{2,3},{3,2},{66,67},{67,66},{4,5},{5,4... | collective-permute-start | bytes 3483656 | tf_op jit(solution)/shard_map/ppermute | solution.py:35
  6.5 84.9 %collective-permute-start.22 = (bf16[3,504,384]{2,1,0:T(8,128)(2,1)}, bf16[3,504,384]{2,1,0:T(8,128)(2,1)}, u32[]{:S(2)}, u32[]{:S(2)}) collective-permute-start(bf16[3,504,384]{2,1,0:T(8,128)(2,1)} %get-tuple-element.40), channel_id=1, source_target_pairs={{0,64},{1,65},{64,0},{65,1},{2,66},{3,67},{66,2},{67,3},{4,68},{5,... | collective-permute-start | bytes 3483656 | tf_op jit(solution)/shard_map/ppermute | solution.py:35
  9.5 68.3 %collective-permute-start.10 = (bf16[1,504,256]{2,1,0:T(8,128)(2,1)}, bf16[1,504,256]{2,1,0:T(8,128)(2,1)}, u32[]{:S(2)}, u32[]{:S(2)}) collective-permute-start(bf16[1,504,256]{2,1,0:T(8,128)(2,1)} %get-tuple-element.31), channel_id=1, source_target_pairs={{0,64},{1,65},{64,0},{65,1},{2,66},{3,67},{66,2},{67,3},{4,68},{5,... | collective-permute-start | bytes 774152 | tf_op jit(solution)/shard_map/ppermute | solution.py:35
  12.9 68.6 %collective-permute-start.12 = (bf16[2,504,256]{2,1,0:T(8,128)(2,1)}, bf16[2,504,256]{2,1,0:T(8,128)(2,1)}, u32[]{:S(2)}, u32[]{:S(2)}) collective-permute-start(bf16[2,504,256]{2,1,0:T(8,128)(2,1)} %get-tuple-element.33), channel_id=1, source_target_pairs={{0,1},{1,0},{64,65},{65,64},{2,3},{3,2},{66,67},{67,66},{4,5},{5,4... | collective-permute-start | bytes 1548296 | tf_op jit(solution)/shard_map/ppermute | solution.py:35
  13.9 60.8 %collective-permute-start.7 = (f32[1,1280]{1,0:T(1,128)S(1)}, f32[1,1280]{1,0:T(1,128)}, u32[]{:S(2)}, u32[]{:S(2)}) collective-permute-start(f32[1,1280]{1,0:T(1,128)S(1)} %constant_dynamic-slice_fusion.3), channel_id=1, source_target_pairs={{0,64},{1,65},{64,0},{65,1},{2,66},{3,67},{66,2},{67,3},{4,68},{5,... | collective-permute-start | bytes 15368 | tf_op jit(solution)/shard_map/ppermute | solution.py:35
  74.7 14.9 %collective-permute-start.13 = (bf16[2,504,256]{2,1,0:T(8,128)(2,1)}, bf16[2,504,256]{2,1,0:T(8,128)(2,1)}, u32[]{:S(2)}, u32[]{:S(2)}) collective-permute-start(bf16[2,504,256]{2,1,0:T(8,128)(2,1)} %get-tuple-element.34), channel_id=1, source_target_pairs={{0,64},{1,65},{64,0},{65,1},{2,66},{3,67},{66,2},{67,3},{4,68},{5,... | collective-permute-start | bytes 1548296 | tf_op jit(solution)/shard_map/ppermute | solution.py:35
  77.7 54.9 %collective-permute-start.23 = (bf16[3,504,384]{2,1,0:T(8,128)(2,1)}, bf16[3,504,384]{2,1,0:T(8,128)(2,1)}, u32[]{:S(2)}, u32[]{:S(2)}) collective-permute-start(bf16[3,504,384]{2,1,0:T(8,128)(2,1)} %pack.13), channel_id=1, source_target_pairs={{0,65},{1,64},{64,1},{65,0},{2,67},{3,66},{66,3},{67,2},{4,69},{5,... | collective-permute-start | bytes 3483656 | tf_op jit(solution)/shard_map/ppermute | solution.py:35
  81.6 100.5 %collective-permute-start.17 = (bf16[3,504,384]{2,1,0:T(8,128)(2,1)}, bf16[3,504,384]{2,1,0:T(8,128)(2,1)}, u32[]{:S(2)}, u32[]{:S(2)}) collective-permute-start(bf16[3,504,384]{2,1,0:T(8,128)(2,1)} %get-tuple-element.36), channel_id=1, source_target_pairs={{0,1},{1,0},{64,65},{65,64},{2,3},{3,2},{66,67},{67,66},{4,5},{5,4... | collective-permute-start | bytes 3483656 | tf_op jit(solution)/shard_map/ppermute | solution.py:35
  89.6 96.1 %collective-permute-start.18 = (bf16[3,504,384]{2,1,0:T(8,128)(2,1)}, bf16[3,504,384]{2,1,0:T(8,128)(2,1)}, u32[]{:S(2)}, u32[]{:S(2)}) collective-permute-start(bf16[3,504,384]{2,1,0:T(8,128)(2,1)} %get-tuple-element.37), channel_id=1, source_target_pairs={{0,64},{1,65},{64,0},{65,1},{2,66},{3,67},{66,2},{67,3},{4,68},{5,... | collective-permute-start | bytes 3483656 | tf_op jit(solution)/shard_map/ppermute | solution.py:35
  90.6 95.2 %collective-permute-start.19 = (bf16[3,504,384]{2,1,0:T(8,128)(2,1)}, bf16[3,504,384]{2,1,0:T(8,128)(2,1)}, u32[]{:S(2)}, u32[]{:S(2)}) collective-permute-start(bf16[3,504,384]{2,1,0:T(8,128)(2,1)} %get-tuple-element.38), channel_id=1, source_target_pairs={{0,65},{1,64},{64,1},{65,0},{2,67},{3,66},{66,3},{67,2},{4,69},{5,... | collective-permute-start | bytes 3483656 | tf_op jit(solution)/shard_map/ppermute | solution.py:35
  91.3 86.1 %collective-permute-start.14 = (bf16[2,504,256]{2,1,0:T(8,128)(2,1)}, bf16[2,504,256]{2,1,0:T(8,128)(2,1)}, u32[]{:S(2)}, u32[]{:S(2)}) collective-permute-start(bf16[2,504,256]{2,1,0:T(8,128)(2,1)} %get-tuple-element.35), channel_id=1, source_target_pairs={{0,65},{1,64},{64,1},{65,0},{2,67},{3,66},{66,3},{67,2},{4,69},{5,... | collective-permute-start | bytes 1548296 | tf_op jit(solution)/shard_map/ppermute | solution.py:35
  132.7 56.8 %collective-permute-start.3 = (bf16[2,504,256]{2,1,0:T(8,128)(2,1)}, bf16[2,504,256]{2,1,0:T(8,128)(2,1)}, u32[]{:S(2)}, u32[]{:S(2)}) collective-permute-start(bf16[2,504,256]{2,1,0:T(8,128)(2,1)} %get-tuple-element.27), channel_id=1, source_target_pairs={{0,1},{1,0},{64,65},{65,64},{2,3},{3,2},{66,67},{67,66},{4,5},{5,4... | collective-permute-start | bytes 1548296 | tf_op jit(solution)/shard_map/ppermute | solution.py:35
  177.4 51.9 %collective-permute-start.24 = (bf16[4,480,384]{2,1,0:T(8,128)(2,1)}, bf16[4,480,384]{2,1,0:T(8,128)(2,1)}, u32[]{:S(2)}, u32[]{:S(2)}) collective-permute-start(bf16[4,480,384]{2,1,0:T(8,128)(2,1)} %near.7), channel_id=1, source_target_pairs={{0,2},{2,4},{4,6},{6,8},{8,10},{10,12},{12,14},{14,16},{16,18},{18... | collective-permute-start | bytes 4423688 | tf_op jit(solution)/shard_map/ppermute | solution.py:40
  182.1 35.2 %collective-permute-start.15 = (bf16[4,480,256]{2,1,0:T(8,128)(2,1)}, bf16[4,480,256]{2,1,0:T(8,128)(2,1)}, u32[]{:S(2)}, u32[]{:S(2)}) collective-permute-start(bf16[4,480,256]{2,1,0:T(8,128)(2,1)} %near.5), channel_id=1, source_target_pairs={{0,2},{2,4},{4,6},{6,8},{8,10},{10,12},{12,14},{14,16},{16,18},{18... | collective-permute-start | bytes 2949128 | tf_op jit(solution)/shard_map/ppermute | solution.py:40
  185.7 14.1 %collective-permute-start.4 = (bf16[2,504,256]{2,1,0:T(8,128)(2,1)}, bf16[2,504,256]{2,1,0:T(8,128)(2,1)}, u32[]{:S(2)}, u32[]{:S(2)}) collective-permute-start(bf16[2,504,256]{2,1,0:T(8,128)(2,1)} %get-tuple-element.28), channel_id=1, source_target_pairs={{0,64},{1,65},{64,0},{65,1},{2,66},{3,67},{66,2},{67,3},{4,68},{5,... | collective-permute-start | bytes 1548296 | tf_op jit(solution)/shard_map/ppermute | solution.py:35
  185.8 15.3 %collective-permute-start.5 = (bf16[2,504,256]{2,1,0:T(8,128)(2,1)}, bf16[2,504,256]{2,1,0:T(8,128)(2,1)}, u32[]{:S(2)}, u32[]{:S(2)}) collective-permute-start(bf16[2,504,256]{2,1,0:T(8,128)(2,1)} %get-tuple-element.29), channel_id=1, source_target_pairs={{0,65},{1,64},{64,1},{65,0},{2,67},{3,66},{66,3},{67,2},{4,69},{5,... | collective-permute-start | bytes 1548296 | tf_op jit(solution)/shard_map/ppermute | solution.py:35
  189.5 58.2 %collective-permute-start.20 = (bf16[4,480,384]{2,1,0:T(8,128)(2,1)}, bf16[4,480,384]{2,1,0:T(8,128)(2,1)}, u32[]{:S(2)}, u32[]{:S(2)}) collective-permute-start(bf16[4,480,384]{2,1,0:T(8,128)(2,1)} %near.6), channel_id=1, source_target_pairs={{0,2},{2,4},{4,6},{6,8},{8,10},{10,12},{12,14},{14,16},{16,18},{18... | collective-permute-start | bytes 4423688 | tf_op jit(solution)/shard_map/ppermute | solution.py:40
  199.8 14.3 %collective-permute-start.11 = (bf16[1,504,256]{2,1,0:T(8,128)(2,1)}, bf16[1,504,256]{2,1,0:T(8,128)(2,1)}, u32[]{:S(2)}, u32[]{:S(2)}) collective-permute-start(bf16[1,504,256]{2,1,0:T(8,128)(2,1)} %get-tuple-element.32), channel_id=1, source_target_pairs={{0,65},{1,64},{64,1},{65,0},{2,67},{3,66},{66,3},{67,2},{4,69},{5,... | collective-permute-start | bytes 774152 | tf_op jit(solution)/shard_map/ppermute | solution.py:35
  201.1 13.7 %collective-permute-start.9 = (bf16[1,504,256]{2,1,0:T(8,128)(2,1)}, bf16[1,504,256]{2,1,0:T(8,128)(2,1)}, u32[]{:S(2)}, u32[]{:S(2)}) collective-permute-start(bf16[1,504,256]{2,1,0:T(8,128)(2,1)} %get-tuple-element.30), channel_id=1, source_target_pairs={{0,1},{1,0},{64,65},{65,64},{2,3},{3,2},{66,67},{67,66},{4,5},{5,4... | collective-permute-start | bytes 774152 | tf_op jit(solution)/shard_map/ppermute | solution.py:35
  214.1 51.6 %collective-permute-start.25 = (bf16[504,768]{1,0:T(8,128)(2,1)}, bf16[504,768]{1,0:T(8,128)(2,1)}, u32[]{:S(2)}, u32[]{:S(2)}) collective-permute-start(bf16[504,768]{1,0:T(8,128)(2,1)} %constant_dynamic-slice_fusion), channel_id=1, source_target_pairs={{0,65},{1,64},{64,1},{65,0},{2,67},{3,66},{66,3},{67,2},{4,69},{5,... | collective-permute-start | bytes 2322440 | tf_op jit(solution)/shard_map/ppermute | solution.py:35
  214.8 73.8 %collective-permute-start.16 = (bf16[504,256]{1,0:T(8,128)(2,1)}, bf16[504,256]{1,0:T(8,128)(2,1)}, u32[]{:S(2)}, u32[]{:S(2)}) collective-permute-start(bf16[504,256]{1,0:T(8,128)(2,1)} %get-tuple-element.43), channel_id=1, source_target_pairs={{0,65},{1,64},{64,1},{65,0},{2,67},{3,66},{66,3},{67,2},{4,69},{5,... | collective-permute-start | bytes 774152 | tf_op jit(solution)/shard_map/ppermute | solution.py:35
  217.4 53.4 %collective-permute-start = (bf16[1,504,256]{2,1,0:T(8,128)(2,1)}, bf16[1,504,256]{2,1,0:T(8,128)(2,1)}, u32[]{:S(2)}, u32[]{:S(2)}) collective-permute-start(bf16[1,504,256]{2,1,0:T(8,128)(2,1)} %get-tuple-element.24), channel_id=1, source_target_pairs={{0,1},{1,0},{64,65},{65,64},{2,3},{3,2},{66,67},{67,66},{4,5},{5,4... | collective-permute-start | bytes 774152 | tf_op jit(solution)/shard_map/ppermute | solution.py:35
  229.3 47.3 %collective-permute-start.6 = (bf16[4,480,256]{2,1,0:T(8,128)(2,1)}, bf16[4,480,256]{2,1,0:T(8,128)(2,1)}, u32[]{:S(2)}, u32[]{:S(2)}) collective-permute-start(bf16[4,480,256]{2,1,0:T(8,128)(2,1)} %near.4), channel_id=1, source_target_pairs={{0,2},{2,4},{4,6},{6,8},{8,10},{10,12},{12,14},{14,16},{16,18},{18... | collective-permute-start | bytes 2949128 | tf_op jit(solution)/shard_map/ppermute | solution.py:40
  247.7 23.7 %collective-permute-start.1 = (bf16[1,504,256]{2,1,0:T(8,128)(2,1)}, bf16[1,504,256]{2,1,0:T(8,128)(2,1)}, u32[]{:S(2)}, u32[]{:S(2)}) collective-permute-start(bf16[1,504,256]{2,1,0:T(8,128)(2,1)} %get-tuple-element.25), channel_id=1, source_target_pairs={{0,64},{1,65},{64,0},{65,1},{2,66},{3,67},{66,2},{67,3},{4,68},{5,... | collective-permute-start | bytes 774152 | tf_op jit(solution)/shard_map/ppermute | solution.py:35
  265.7 10.2 %collective-permute-start.2 = (bf16[1,504,256]{2,1,0:T(8,128)(2,1)}, bf16[1,504,256]{2,1,0:T(8,128)(2,1)S(1)}, u32[]{:S(2)}, u32[]{:S(2)}) collective-permute-start(bf16[1,504,256]{2,1,0:T(8,128)(2,1)} %get-tuple-element.26), channel_id=1, source_target_pairs={{0,65},{1,64},{64,1},{65,0},{2,67},{3,66},{66,3},{67,2},{4,69},{5,... | collective-permute-start | bytes 774152 | tf_op jit(solution)/shard_map/ppermute | solution.py:35
  270.7 21.9 %collective-permute-start.8 = (bf16[504,256]{1,0:T(8,128)(2,1)}, bf16[504,256]{1,0:T(8,128)(2,1)S(1)}, u32[]{:S(2)}, u32[]{:S(2)}) collective-permute-start(bf16[504,256]{1,0:T(8,128)(2,1)} %get-tuple-element.44), channel_id=1, source_target_pairs={{0,65},{1,64},{64,1},{65,0},{2,67},{3,66},{66,3},{67,2},{4,69},{5,... | collective-permute-start | bytes 774152 | tf_op jit(solution)/shard_map/ppermute | solution.py:35
  271.4 25.4 %collective-permute-start.28 = (bf16[480,768]{1,0:T(8,128)(2,1)}, bf16[480,768]{1,0:T(8,128)(2,1)}, u32[]{:S(2)}, u32[]{:S(2)}) collective-permute-start(bf16[480,768]{1,0:T(8,128)(2,1)} %fusion), channel_id=1, source_target_pairs={{0,2},{2,4},{4,6},{6,8},{8,10},{10,12},{12,14},{14,16},{16,18},{18... | collective-permute-start | bytes 2211848 | tf_op jit(solution)/shard_map/ppermute | solution.py:40
  275.9 0.7 copy-start.4
  276.6 20.2 %copy-start = (bf16[2,504,768]{2,1,0:T(8,128)(2,1)S(1)}, bf16[2,504,768]{2,1,0:T(8,128)(2,1)}, u32[]{:S(2)}) copy-start(bf16[2,504,768]{2,1,0:T(8,128)(2,1)} %attend.7.rest_0_) | copy-start | bytes 4644868
  288.6 8.2 %copy-start.3 = (s32[15]{0:T(128)S(1)}, s32[15]{0:T(128)}, u32[]{:S(2)}) copy-start(s32[15]{0:T(128)} %concatenate.3.info_ref) | copy-start | bytes 184
  289.8 10.3 %collective-permute-start.27 = (bf16[480,256]{1,0:T(8,128)(2,1)S(1)}, bf16[480,256]{1,0:T(8,128)(2,1)S(1)}, u32[]{:S(2)}, u32[]{:S(2)}) collective-permute-start(bf16[480,256]{1,0:T(8,128)(2,1)S(1)} %fusion.1), channel_id=1, source_target_pairs={{0,2},{2,4},{4,6},{6,8},{8,10},{10,12},{12,14},{14,16},{16,18},{18... | collective-permute-start | bytes 737288 | tf_op jit(solution)/shard_map/ppermute | solution.py:40
  293.7 6.4 %copy-start.1 = (bf16[2,504,256]{2,1,0:T(8,128)(2,1)S(1)}, bf16[2,504,256]{2,1,0:T(8,128)(2,1)}, u32[]{:S(2)}) copy-start(bf16[2,504,256]{2,1,0:T(8,128)(2,1)} %attend.5.rest_0_) | copy-start | bytes 1548292
  293.7 9.8 %collective-permute-start.26 = (bf16[480,256]{1,0:T(8,128)(2,1)S(1)}, bf16[480,256]{1,0:T(8,128)(2,1)S(1)}, u32[]{:S(2)}, u32[]{:S(2)}) collective-permute-start(bf16[480,256]{1,0:T(8,128)(2,1)S(1)} %fusion.2), channel_id=1, source_target_pairs={{0,2},{2,4},{4,6},{6,8},{8,10},{10,12},{12,14},{14,16},{16,18},{18... | collective-permute-start | bytes 737288 | tf_op jit(solution)/shard_map/ppermute | solution.py:40
  300.1 3.4 %copy-start.2 = (bf16[2,504,256]{2,1,0:T(8,128)(2,1)S(1)}, bf16[2,504,256]{2,1,0:T(8,128)(2,1)}, u32[]{:S(2)}) copy-start(bf16[2,504,256]{2,1,0:T(8,128)(2,1)} %attend.4.rest_0_) | copy-start | bytes 1548292
